TPU v7x, 32 devices: a whole 2x2x4 slice. The times are simulated.
32 devices in a mesh: ctx: 2 (over y), dp: 16 (over z, x, core).
Axes of the slice: x: 2, y: 2, z: 4, core: 2. Of those that a mesh axis runs over, the one named last changes fastest.
Arguments:
- queries: bfloat16 [16, 256, 1024], P('dp', 'ctx'), may hold values from -20 to 20
- keys: bfloat16 [16, 256, 1024], P('dp', 'ctx'), may hold values from -4 to 4
- values: bfloat16 [16, 256, 1024], P('dp', 'ctx'), may hold values from -6 to 6
- d_mixed: bfloat16 [16, 256, 1024], P('dp', 'ctx'), may hold values from -6 to 6
- series_ids: int32 [16, 256], P('dp', 'ctx'), may hold values from 0 to 3, never falling along the last dimension, each value on 1 to 192 neighbouring positions
- variate_ids: int32 [16, 256], P('dp', 'ctx'), may hold values from 0 to 3
- variate_bias: float32 [2, 16], replicated, may hold values from -4 to 4
- w_out: bfloat16 [1024, 1024], P('dp'), may hold values from -0.1875 to 0.1875
Outputs:
- mixed: bfloat16 [16, 256, 1024], P('dp', 'ctx')
- q_grad: bfloat16 [16, 256, 1024], P('dp', 'ctx')
- k_grad: bfloat16 [16, 256, 1024], P('dp', 'ctx')
- v_grad: bfloat16 [16, 256, 1024], P('dp', 'ctx')
- w_grad: float32 [1024, 1024], P('dp')
- bias_grad: float32 [2, 16], replicated
Inputs may be any that keep to these rules, and one draw needn't show every extreme that they name: `series_ids`: within a packed row series numbers never fall; each series spans 1 to 192 consecutive tokens and some series spans exactly 192.
All inputs are finite; a program needn't handle non-finite values.
Results may differ from a plain program's by a relative error of at most 0.015.
Values may be sent and summed in bfloat16 or wider, within the bound.
No kernel may reach another device: no remote copies, remote signals or barrier semaphores. Data moves between devices by JAX's collectives and lax.ppermute only.
A program may use at most 128 MiB of HBM per device.

v0:
```python
import jax
import jax.numpy as jnp
from jax import lax
from jax.sharding import PartitionSpec as P

HEADS = 16
HEAD_DIM = 64


NEG = -1e30
group_width = 4


def shifted_2(shard, axis, by):
    count = lax.axis_size(axis)
    pairs = [(i, i + by) for i in range(count) if 0 <= i + by < count]
    return lax.ppermute(shard, axis, pairs)


def split_heads(block):
    rows = block.shape[0]
    return block.reshape(rows, HEADS // group_width, group_width, HEAD_DIM).transpose(1, 0, 2, 3)


def merge_heads(block):
    rows = block.shape[1]
    return block.transpose(1, 0, 2, 3).reshape(rows, HEADS * HEAD_DIM)


def stats_groups(rows_heads):
    count = rows_heads.shape[0]
    return rows_heads.reshape(count, HEADS // group_width, group_width).transpose(1, 2, 0)


def scored(q_group, k_group, bias_group, q_tag, k_tag, q_var, k_var):
    raw = jnp.einsum(
        "qhd,khd->hqk", q_group, k_group, preferred_element_type=jnp.float32
    ) * HEAD_DIM ** (-0.5)
    same = (q_var[:, None] == k_var[None, :])[None]
    allowed = (q_tag[:, None] == k_tag[None, :])[None]
    shifted = raw + jnp.where(same, bias_group[0][:, None, None], bias_group[1][:, None, None])
    return (jnp.where(allowed, shifted, NEG), allowed, same)


def joined(pieces):
    return [jnp.concatenate(items, axis=0) for items in zip(*pieces)]


def on_device(queries, keys, values, d_mixed, series_ids, variate_ids, variate_bias, w_out):
    query = queries[0]
    key_rows = keys[0]
    value_rows = values[0]
    upstream = d_mixed[0]
    tags = series_ids[0] + 1
    variety = variate_ids[0]
    tok = query.shape[0]
    n_ctx = lax.axis_size("ctx")
    most = tok * n_ctx // 2 + tok // 2
    reach = min((most - 2) // tok + 1, n_ctx - 1)
    scale = HEAD_DIM ** (-0.5)
    w_full = lax.all_gather(w_out, "dp", axis=0, tiled=True)
    d_context = lax.dot_general(
        upstream, w_full, (((1,), (1,)), ((), ())), preferred_element_type=jnp.float32
    ).astype(jnp.bfloat16)
    bias_groups = variate_bias.reshape(2, HEADS // group_width, group_width).transpose(1, 0, 2)
    pieces = [(key_rows, value_rows, tags, variety)]
    for dist in range(1, reach + 1):
        pieces.append(shifted_2((key_rows, value_rows, tags, variety), "ctx", dist))
        pieces.append(shifted_2((key_rows, value_rows, tags, variety), "ctx", -dist))
    key_set, value_set, key_tags, key_vars = joined(pieces)
    q_groups = split_heads(query)
    k_groups = split_heads(key_set)
    v_groups = split_heads(value_set)

    def forward_group(items):
        q_group, k_group, v_group, bias_group = items
        scores, allowed, same = scored(
            q_group, k_group, bias_group, tags, key_tags, variety, key_vars
        )
        top = jnp.max(scores, axis=2, keepdims=True)
        total = jnp.sum(jnp.where(allowed, jnp.exp(scores - top), 0.0), axis=2, keepdims=True)
        lse = top + jnp.log(total)
        probs = jnp.where(allowed, jnp.exp(scores - lse), 0.0)
        context = jnp.einsum(
            "hqk,khd->qhd", probs.astype(jnp.bfloat16), v_group, preferred_element_type=jnp.float32
        )
        return (context, lse[:, :, 0], probs)

    context_groups, lse_groups, prob_groups = lax.map(
        forward_group, (q_groups, k_groups, v_groups, bias_groups)
    )
    context = merge_heads(context_groups)
    context_bf = context.astype(jnp.bfloat16)
    delta_rows = jnp.sum(
        (d_context.astype(jnp.float32) * context).reshape(tok, HEADS, HEAD_DIM), axis=2
    )
    lse_rows = lse_groups.transpose(2, 0, 1).reshape(tok, HEADS)
    d_groups = split_heads(d_context)
    delta_groups = stats_groups(delta_rows)

    def query_group(items):
        k_group, v_group, d_group, probs, delta_group, bias_group = items
        same = (variety[:, None] == key_vars[None, :])[None]
        dprob = jnp.einsum("qhd,khd->hqk", d_group, v_group, preferred_element_type=jnp.float32)
        dscore = probs * (dprob - delta_group[:, :, None])
        grads = (
            jnp.einsum(
                "hqk,khd->qhd",
                dscore.astype(jnp.bfloat16),
                k_group,
                preferred_element_type=jnp.float32,
            )
            * scale
        )
        sums = jnp.stack(
            [
                jnp.sum(jnp.where(same, dscore, 0.0), axis=(1, 2)),
                jnp.sum(jnp.where(same, 0.0, dscore), axis=(1, 2)),
            ]
        )
        return (grads, sums)

    q_grads, sum_groups = lax.map(
        query_group, (k_groups, v_groups, d_groups, prob_groups, delta_groups, bias_groups)
    )
    bias_terms = sum_groups.transpose(1, 0, 2).reshape(2, HEADS)
    front = [(query, d_context, tags, variety)]
    numbers = [(lse_rows, delta_rows)]
    for dist in range(1, reach + 1):
        front.append(shifted_2((query, d_context, tags, variety), "ctx", dist))
        numbers.append(shifted_2((lse_rows, delta_rows), "ctx", dist))
        front.append(shifted_2((query, d_context, tags, variety), "ctx", -dist))
        numbers.append(shifted_2((lse_rows, delta_rows), "ctx", -dist))
    remote_q, remote_d, remote_tags, remote_vars = joined(front)
    remote_lse, remote_delta = joined(numbers)

    def key_group(items):
        q_group, d_group, lse_group, delta_group, k_group, v_group, bias_group = items
        scores, allowed, same = scored(
            q_group, k_group, bias_group, remote_tags, tags, remote_vars, variety
        )
        probs = jnp.where(allowed, jnp.exp(scores - lse_group[:, :, None]), 0.0)
        dprob = jnp.einsum("qhd,khd->hqk", d_group, v_group, preferred_element_type=jnp.float32)
        dscore = probs * (dprob - delta_group[:, :, None])
        k_grad = (
            jnp.einsum(
                "hqk,qhd->khd",
                dscore.astype(jnp.bfloat16),
                q_group,
                preferred_element_type=jnp.float32,
            )
            * scale
        )
        v_grad = jnp.einsum(
            "hqk,qhd->khd", probs.astype(jnp.bfloat16), d_group, preferred_element_type=jnp.float32
        )
        return (k_grad, v_grad)

    k_grads, v_grads = lax.map(
        key_group,
        (
            split_heads(remote_q),
            split_heads(remote_d),
            stats_groups(remote_lse),
            stats_groups(remote_delta),
            split_heads(key_rows),
            split_heads(value_rows),
            bias_groups,
        ),
    )
    q_out = merge_heads(q_grads).astype(jnp.bfloat16)
    k_out = merge_heads(k_grads).astype(jnp.bfloat16)
    v_out = merge_heads(v_grads).astype(jnp.bfloat16)
    mixed = jnp.dot(context_bf, w_full, preferred_element_type=jnp.float32).astype(jnp.bfloat16)
    partial_rows = lax.psum_scatter(
        lax.dot_general(
            context_bf, upstream, (((0,), (0,)), ((), ())), preferred_element_type=jnp.float32
        ),
        "dp",
        scatter_dimension=0,
        tiled=True,
    )
    w_grad = lax.psum(partial_rows, "ctx")
    bias_grad = lax.psum(bias_terms, ("ctx", "dp"))
    return (mixed[None], q_out[None], k_out[None], v_out[None], w_grad, bias_grad)


def solution(mesh):
    return jax.shard_map(
        on_device,
        mesh=mesh,
        in_specs=(
            P("dp", "ctx", None),
            P("dp", "ctx", None),
            P("dp", "ctx", None),
            P("dp", "ctx", None),
            P("dp", "ctx"),
            P("dp", "ctx"),
            P(),
            P("dp", None),
        ),
        out_specs=(
            P("dp", "ctx", None),
            P("dp", "ctx", None),
            P("dp", "ctx", None),
            P("dp", "ctx", None),
            P("dp", None),
            P(),
        ),
        check_vma=False,
    )
```

profile of v0, /device:TPU:0, one launch (start us, length us, event | category | flops | bytes accessed | tf_op | source)
XLA Modules:
  0.0 179.6 jit_solution(639569366921417282)
XLA Ops:
  7.3 1.2 copy.31
  8.4 4.9 %collective-permute-start = (bf16[128,1024]{0,1:T(8,128)(2,1)S(1)}, bf16[128,1024]{0,1:T(8,128)(2,1)S(1)}, u32[]{:S(2)}, u32[]{:S(2)}) collective-permute-start(bf16[128,1024]{0,1:T(8,128)(2,1)S(1)} %bitcast.263), channel_id=1, source_target_pairs={{0,16},{1,17},{2,18},{3,19},{4,20},{5,21},{6,22},{7,23},{8,24},{9,... | collective-permute-start | bytes 786440 | tf_op jit(solution)/shard_map/ppermute | solution.py:17
  13.4 1.3 collective-permute-start.1
  14.7 4.6 %collective-permute-start.4 = (bf16[128,1024]{1,0:T(8,128)(2,1)}, bf16[128,1024]{1,0:T(8,128)(2,1)S(1)}, u32[]{:S(2)}, u32[]{:S(2)}) collective-permute-start(bf16[128,1024]{1,0:T(8,128)(2,1)} %bitcast.278), channel_id=1, source_target_pairs={{0,16},{1,17},{2,18},{3,19},{4,20},{5,21},{6,22},{7,23},{8,24},{9,... | collective-permute-start | bytes 786440 | tf_op jit(solution)/shard_map/ppermute | solution.py:17
  19.9 1.3 collective-permute-start.2
  21.2 1.3 collective-permute-start.3
  22.6 1.1 copy.34
  24.6 4.4 %collective-permute-start.6 = (s32[128]{0:T(128)}, s32[128]{0:T(128)S(1)}, u32[]{:S(2)}, u32[]{:S(2)}) collective-permute-start(s32[128]{0:T(128)} %bitcast.285), channel_id=1, source_target_pairs={{0,16},{1,17},{2,18},{3,19},{4,20},{5,21},{6,22},{7,23},{8,24},{9,... | collective-permute-start | bytes 1544 | tf_op jit(solution)/shard_map/ppermute | solution.py:17
  29.0 1.1 copy.33
  30.2 1.3 collective-permute-start.7
  31.5 1.3 collective-permute-start.5
  32.8 2.8 %collective-permute-done.7 = s32[128]{0:T(128)S(1)} collective-permute-done((s32[128]{0:T(128)S(1)}, s32[128]{0:T(128)S(1)}, u32[]{:S(2)}, u32[]{:S(2)}) %collective-permute-start.7) | collective-permute-done | bytes 544 | tf_op jit(solution)/shard_map/ppermute | solution.py:17
  36.7 1.1 maximum_bitcast_fusion.1
  37.8 2.0 %collective-permute-done.5 = bf16[128,1024]{1,0:T(8,128)(2,1)S(1)} collective-permute-done((bf16[128,1024]{1,0:T(8,128)(2,1)S(1)}, bf16[128,1024]{1,0:T(8,128)(2,1)S(1)}, u32[]{:S(2)}, u32[]{:S(2)}) %collective-permute-start.5) | collective-permute-done | bytes 262176 | tf_op jit(solution)/shard_map/ppermute | solution.py:17
  41.7 9.7 %while.41 = (s32[]{:T(128)}, f32[4,128,4,64]{1,3,2,0:T(8,128)S(1)}, f32[4,4,128]{2,1,0:T(4,128)S(1)}, f32[4,4,128,384]{3,2,1,0:T(8,128)}, bf16[4,384,4,64]{1,3,2...) while((s32[]{:T(128)}, f32[4,128,4,64]{1,3,2,0:T(8,128)S(1)}, ...), condition=%wide.region_3.4_spmd.clone, body=%wide.region_0.3_spmd.sunk.clone | while | flops 52985344 | bytes 4892413 | solution.py:89
  45.1 1.1 bitcast_dynamic-update-slice_fusion.7
  51.5 2.6 %fusion.62 = f32[1024,1024]{1,0:T(8,128)} fusion(bf16[128,1024]{0,1:T(8,128)(2,1)S(1)} %bitcast.267, bf16[1,128,1024]{2,1,0:T(8,128)(2,1)S(1)} %copy-done), kind=kOutput, calls=%fused_computation.97 | convolution fusion | flops 268435456 | bytes 4718592 | tf_op jit(solution)/shard_map/dot_general | solution.py:176
  55.1 1.5 collective-permute-start.8
  56.5 1.3 collective-permute-start.9
  59.3 4.5 %collective-permute-start.10 = (f32[128,16]{0,1:T(8,128)S(1)}, f32[128,16]{0,1:T(8,128)S(1)}, u32[]{:S(2)}, u32[]{:S(2)}) collective-permute-start(f32[128,16]{0,1:T(8,128)S(1)} %bitcast.295), channel_id=1, source_target_pairs={{0,16},{1,17},{2,18},{3,19},{4,20},{5,21},{6,22},{7,23},{8,24},{9,... | collective-permute-start | bytes 24584 | tf_op jit(solution)/shard_map/ppermute | solution.py:17
  63.8 1.3 collective-permute-start.11
  66.7 2.7 %collective-permute-done.11 = f32[128,16]{0,1:T(8,128)S(1)} collective-permute-done((f32[128,16]{0,1:T(8,128)S(1)}, f32[128,16]{0,1:T(8,128)S(1)}, u32[]{:S(2)}, u32[]{:S(2)}) %collective-permute-start.11) | collective-permute-done | bytes 8224 | tf_op jit(solution)/shard_map/ppermute | solution.py:17
  69.4 3.1 %convert_multiply_fusion = (f32[128,1024]{1,0:T(8,128)S(1)}, bf16[128,1024]{1,0:T(8,128)(2,1)}) fusion(f32[128,1024]{1,0:T(8,128)S(1)} %copy.39, bf16[1024,1024]{1,0:T(8,128)(2,1)} %all-gather.2.cloned.1.call-done, bf16[1,128,1024]{2,1,0:T(8,128)(2,1)S(1)} %copy-done), kind=kOutput, calls=%fused_computation.96 | convolution fusion | flops 268828672 | bytes 3670016 | tf_op jit(solution)/shard_map/dot_general | solution.py:62
  73.4 1.9 %collective-permute-start.14 = (f32[128,16]{0,1:T(8,128)}, f32[128,16]{0,1:T(8,128)S(1)}, u32[]{:S(2)}, u32[]{:S(2)}) collective-permute-start(f32[128,16]{0,1:T(8,128)} %bitcast_reduce_fusion), channel_id=1, source_target_pairs={{0,16},{1,17},{2,18},{3,19},{4,20},{5,21},{6,22},{7,23},{8,24},{9,... | collective-permute-start | bytes 24584 | tf_op jit(solution)/shard_map/ppermute | solution.py:17
  75.3 1.3 collective-permute-start.15
  76.6 5.3 %collective-permute-start.12 = (bf16[128,1024]{1,0:T(8,128)(2,1)}, bf16[128,1024]{1,0:T(8,128)(2,1)}, u32[]{:S(2)}, u32[]{:S(2)}) collective-permute-start(bf16[128,1024]{1,0:T(8,128)(2,1)} %get-tuple-element.364), channel_id=1, source_target_pairs={{0,16},{1,17},{2,18},{3,19},{4,20},{5,21},{6,22},{7,23},{8,24},{9,... | collective-permute-start | bytes 786440 | tf_op jit(solution)/shard_map/ppermute | solution.py:17
  81.8 1.3 collective-permute-start.13
  83.1 1.8 %copy.38 = bf16[128,1024]{0,1:T(8,128)(2,1)} copy(bf16[128,1024]{1,0:T(8,128)(2,1)} %get-tuple-element.364) | data formatting | bytes 524288 | tf_op jit(solution)/shard_map/convert_element_type | solution.py:64
  84.9 15.8 %while.42 = (s32[]{:T(128)}, bf16[4,128,4,64]{1,3,2,0:T(8,128)(2,1)S(1)}, f32[4,2,4]{2,1,0:T(2,128)S(1)}, bf16[4,384,4,64]{1,3,2,0:T(8,128)(2,1)}, f32[4,4,128,3...) while((s32[]{:T(128)}, ...), condition=%wide.region_8.9_spmd.clone, body=%wide.region_5.8_spmd.sunk.clone | while | flops 51789824 | bytes 2273933 | solution.py:123
  85.9 1.8 %select_reduce_fusion.8 = (f32[4]{0:T(128)S(1)}, f32[4]{0:T(128)S(1)}, bf16[4,128,384]{2,1,0:T(8,128)(2,1)S(1)}) fusion(pred[128,384]{1,0:T(8,128)(4,1)S(1)} %broadcast_compare_fusion.12, f32[4,128]{1,0:T(4,128)S(1)} %dynamic-slice_bitcast_fusion.7, bf16[4,384,4,64]{1,3,2,0:T(8,128)(2,1)} %get-tuple-element.778, s32[]{:T(128)} %get-tuple-element.762, ...), kind=kOutput, calls=%fused_computation.34.clone.1.clone | convolution fusion | flops 26542072 | bytes 1494560 | tf_op jit(solution)/shard_map/while/body/eval_jaxpr/qhd,khd->hqk/dot_general | solution.py:104
  87.7 1.2 fusion.112
  89.8 1.8 %select_reduce_fusion.8 = (f32[4]{0:T(128)S(1)}, f32[4]{0:T(128)S(1)}, bf16[4,128,384]{2,1,0:T(8,128)(2,1)S(1)}) fusion(pred[128,384]{1,0:T(8,128)(4,1)S(1)} %broadcast_compare_fusion.12, f32[4,128]{1,0:T(4,128)S(1)} %dynamic-slice_bitcast_fusion.7, bf16[4,384,4,64]{1,3,2,0:T(8,128)(2,1)} %get-tuple-element.778, s32[]{:T(128)} %get-tuple-element.762, ...), kind=kOutput, calls=%fused_computation.34.clone.1.clone | convolution fusion | flops 26542072 | bytes 1494560 | tf_op jit(solution)/shard_map/while/body/eval_jaxpr/qhd,khd->hqk/dot_general | solution.py:104
  91.6 1.2 fusion.112
  93.6 1.8 select_reduce_fusion.8
  95.4 1.2 fusion.112
  97.4 2.0 %select_reduce_fusion.8 = (f32[4]{0:T(128)S(1)}, f32[4]{0:T(128)S(1)}, bf16[4,128,384]{2,1,0:T(8,128)(2,1)S(1)}) fusion(pred[128,384]{1,0:T(8,128)(4,1)S(1)} %broadcast_compare_fusion.12, f32[4,128]{1,0:T(4,128)S(1)} %dynamic-slice_bitcast_fusion.7, bf16[4,384,4,64]{1,3,2,0:T(8,128)(2,1)} %get-tuple-element.778, s32[]{:T(128)} %get-tuple-element.762, ...), kind=kOutput, calls=%fused_computation.34.clone.1.clone | convolution fusion | flops 26542072 | bytes 1494560 | tf_op jit(solution)/shard_map/while/body/eval_jaxpr/qhd,khd->hqk/dot_general | solution.py:104
  99.5 1.2 fusion.112
  100.8 1.2 fusion.61
  102.0 42.5 %psum.15 = f32[2,16]{1,0:T(2,128)} all-reduce(f32[2,16]{1,0:T(2,128)S(1)} %reshape.290), channel_id=1, replica_groups=mesh['ctx'=2,'dp'=16] {'ctx','dp'}, use_global_device_ids=true, to_apply=%region_13.14 | all-reduce | flops 32 | bytes 256 | tf_op jit(solution)/shard_map/psum | solution.py:184
  146.1 1.2 pad_maximum_fusion
  147.7 12.6 %while.43 = (s32[]{:T(128)}, bf16[4,128,4,64]{1,3,2,0:T(8,128)(2,1)S(1)}, bf16[4,128,4,64]{1,3,2,0:T(8,128)(2,1)}, bf16[4,384,4,64]{1,3,2,0:T(8,128)(2,1)S(1)}, ...) while((s32[]{:T(128)}, ...), condition=%wide.region_10.11_spmd.clone, body=%wide.region_9.10_spmd.sunk.clone | while | flops 102760448 | bytes 4109073 | solution.py:159
  148.0 1.4 fusion.120
  151.1 1.4 fusion.120
  154.2 1.4 fusion.120
  157.4 1.4 fusion.120
  161.2 1.8 copy.49
  163.0 8.4 %all-reduce.2.cloned.1.call-done = f32[64,1024]{1,0:T(8,128)} async-done(((f32[64,1024]{1,0:T(8,128)}), f32[64,1024]{1,0:T(8,128)}) %all-reduce.2.cloned.1.call-update) | async-done | bytes 262160 | tf_op jit(solution)/shard_map/psum | solution.py:183
  171.4 1.7 copy.100
  (152 shorter events, 31.0 us)
Async XLA Ops:
  7.2 44.3 %copy-start = (bf16[1,128,1024]{2,1,0:T(8,128)(2,1)S(1)}, bf16[1,128,1024]{2,1,0:T(8,128)(2,1)}, u32[]{:S(2)}) copy-start(bf16[1,128,1024]{2,1,0:T(8,128)(2,1)} %param.17) | copy-start | bytes 786436
  7.2 24.3 %copy-start.7 = (bf16[1,128,1024]{2,1,0:T(8,128)(2,1)S(1)}, bf16[1,128,1024]{2,1,0:T(8,128)(2,1)}, u32[]{:S(2)}) copy-start(bf16[1,128,1024]{2,1,0:T(8,128)(2,1)} %param.15) | copy-start | bytes 786436
  7.2 23.0 %copy-start.11 = (s32[1,128]{1,0:T(1,128)S(1)}, s32[1,128]{1,0:T(1,128)}, u32[]{:S(2)}) copy-start(s32[1,128]{1,0:T(1,128)} %param.19) | copy-start | bytes 1540
  7.2 22.9 %copy-start.12 = (f32[2,16]{1,0:T(2,128)S(1)}, f32[2,16]{1,0:T(2,128)}, u32[]{:S(2)}) copy-start(f32[2,16]{1,0:T(2,128)} %param.20) | copy-start | bytes 388
  7.2 62.2 %all-gather.2.cloned.1.call-start = ((), (), s32[]{:S(2)}) async-start(), calls=%async_computation.1 | async-start | bytes 2228224 | tf_op jit(solution)/shard_map/all_gather | solution.py:61
  8.4 27.4 %collective-permute-start = (bf16[128,1024]{0,1:T(8,128)(2,1)S(1)}, bf16[128,1024]{0,1:T(8,128)(2,1)S(1)}, u32[]{:S(2)}, u32[]{:S(2)}) collective-permute-start(bf16[128,1024]{0,1:T(8,128)(2,1)S(1)} %bitcast.263), channel_id=1, source_target_pairs={{0,16},{1,17},{2,18},{3,19},{4,20},{5,21},{6,22},{7,23},{8,24},{9,... | collective-permute-start | bytes 786440 | tf_op jit(solution)/shard_map/ppermute | solution.py:17
  13.4 22.5 %collective-permute-start.1 = (bf16[128,1024]{0,1:T(8,128)(2,1)S(1)}, bf16[128,1024]{0,1:T(8,128)(2,1)S(1)}, u32[]{:S(2)}, u32[]{:S(2)}) collective-permute-start(bf16[128,1024]{0,1:T(8,128)(2,1)S(1)} %bitcast.264), channel_id=1, source_target_pairs={{16,0},{17,1},{18,2},{19,3},{20,4},{21,5},{22,6},{23,7},{24,8},{25... | collective-permute-start | bytes 786440 | tf_op jit(solution)/shard_map/ppermute | solution.py:17
  14.7 21.0 %collective-permute-start.4 = (bf16[128,1024]{1,0:T(8,128)(2,1)}, bf16[128,1024]{1,0:T(8,128)(2,1)S(1)}, u32[]{:S(2)}, u32[]{:S(2)}) collective-permute-start(bf16[128,1024]{1,0:T(8,128)(2,1)} %bitcast.278), channel_id=1, source_target_pairs={{0,16},{1,17},{2,18},{3,19},{4,20},{5,21},{6,22},{7,23},{8,24},{9,... | collective-permute-start | bytes 786440 | tf_op jit(solution)/shard_map/ppermute | solution.py:17
  19.9 4.7 %collective-permute-start.2 = (s32[128]{0:T(128)S(1)}, s32[128]{0:T(128)S(1)}, u32[]{:S(2)}, u32[]{:S(2)}) collective-permute-start(s32[128]{0:T(128)S(1)} %add_bitcast_fusion), channel_id=1, source_target_pairs={{0,16},{1,17},{2,18},{3,19},{4,20},{5,21},{6,22},{7,23},{8,24},{9,... | collective-permute-start | bytes 1544 | tf_op jit(solution)/shard_map/ppermute | solution.py:17
  21.2 9.0 %collective-permute-start.3 = (s32[128]{0:T(128)S(1)}, s32[128]{0:T(128)S(1)}, u32[]{:S(2)}, u32[]{:S(2)}) collective-permute-start(s32[128]{0:T(128)S(1)} %add_bitcast_fusion), channel_id=1, source_target_pairs={{16,0},{17,1},{18,2},{19,3},{20,4},{21,5},{22,6},{23,7},{24,8},{25... | collective-permute-start | bytes 1544 | tf_op jit(solution)/shard_map/ppermute | solution.py:17
  22.5 125.2 %reduce-scatter.2.cloned.1.call-start = ((), (), s32[]{:S(2)}) async-start(), calls=%async_computation.2 | async-start | bytes 4456448 | tf_op jit(solution)/shard_map/reduce_scatter | solution.py:175
  23.7 17.0 %copy-start.6 = (bf16[1,128,1024]{1,2,0:T(8,128)(2,1)}, bf16[1,128,1024]{1,2,0:T(8,128)(2,1)S(1)}, u32[]{:S(2)}) copy-start(bf16[1,128,1024]{1,2,0:T(8,128)(2,1)S(1)} %copy.34) | copy-start | bytes 786436
  24.6 6.9 %collective-permute-start.6 = (s32[128]{0:T(128)}, s32[128]{0:T(128)S(1)}, u32[]{:S(2)}, u32[]{:S(2)}) collective-permute-start(s32[128]{0:T(128)} %bitcast.285), channel_id=1, source_target_pairs={{0,16},{1,17},{2,18},{3,19},{4,20},{5,21},{6,22},{7,23},{8,24},{9,... | collective-permute-start | bytes 1544 | tf_op jit(solution)/shard_map/ppermute | solution.py:17
  30.2 5.5 %collective-permute-start.7 = (s32[128]{0:T(128)S(1)}, s32[128]{0:T(128)S(1)}, u32[]{:S(2)}, u32[]{:S(2)}) collective-permute-start(s32[128]{0:T(128)S(1)} %bitcast.286), channel_id=1, source_target_pairs={{16,0},{17,1},{18,2},{19,3},{20,4},{21,5},{22,6},{23,7},{24,8},{25... | collective-permute-start | bytes 1544 | tf_op jit(solution)/shard_map/ppermute | solution.py:17
  31.5 8.3 %collective-permute-start.5 = (bf16[128,1024]{1,0:T(8,128)(2,1)S(1)}, bf16[128,1024]{1,0:T(8,128)(2,1)S(1)}, u32[]{:S(2)}, u32[]{:S(2)}) collective-permute-start(bf16[128,1024]{1,0:T(8,128)(2,1)S(1)} %bitcast.279), channel_id=1, source_target_pairs={{16,0},{17,1},{18,2},{19,3},{20,4},{21,5},{22,6},{23,7},{24,8},{25... | collective-permute-start | bytes 786440 | tf_op jit(solution)/shard_map/ppermute | solution.py:17
  35.9 0.7 copy-start.9
  35.9 0.8 copy-start.10
  51.4 2.7 %copy-start.3 = (bf16[4,384,4,64]{1,3,2,0:T(8,128)(2,1)}, bf16[4,384,4,64]{1,3,2,0:T(8,128)(2,1)S(1)}, u32[]{:S(2)}) copy-start(bf16[4,384,4,64]{1,3,2,0:T(8,128)(2,1)S(1)} %get-tuple-element.836) | copy-start | bytes 2359300
  51.4 2.7 %copy-start.4 = (bf16[4,384,4,64]{1,3,2,0:T(8,128)(2,1)}, bf16[4,384,4,64]{1,3,2,0:T(8,128)(2,1)S(1)}, u32[]{:S(2)}) copy-start(bf16[4,384,4,64]{1,3,2,0:T(8,128)(2,1)S(1)} %get-tuple-element.837) | copy-start | bytes 2359300
  54.1 1.0 copy-start.8
  54.1 117.2 %all-reduce.2.cloned.1.call-start = ((), (), s32[]{:S(2)}) async-start(), calls=%async_computation.3 | async-start | bytes 524288 | tf_op jit(solution)/shard_map/psum | solution.py:183
  55.1 10.1 %collective-permute-start.8 = (bf16[128,1024]{1,0:T(8,128)(2,1)S(1)}, bf16[128,1024]{1,0:T(8,128)(2,1)S(1)}, u32[]{:S(2)}, u32[]{:S(2)}) collective-permute-start(bf16[128,1024]{1,0:T(8,128)(2,1)S(1)} %bitcast.280), channel_id=1, source_target_pairs={{0,16},{1,17},{2,18},{3,19},{4,20},{5,21},{6,22},{7,23},{8,24},{9,... | collective-permute-start | bytes 786440 | tf_op jit(solution)/shard_map/ppermute | solution.py:17
  56.5 8.8 %collective-permute-start.9 = (bf16[128,1024]{1,0:T(8,128)(2,1)S(1)}, bf16[128,1024]{1,0:T(8,128)(2,1)S(1)}, u32[]{:S(2)}, u32[]{:S(2)}) collective-permute-start(bf16[128,1024]{1,0:T(8,128)(2,1)S(1)} %bitcast.281), channel_id=1, source_target_pairs={{16,0},{17,1},{18,2},{19,3},{20,4},{21,5},{22,6},{23,7},{24,8},{25... | collective-permute-start | bytes 786440 | tf_op jit(solution)/shard_map/ppermute | solution.py:17
  59.3 7.4 %collective-permute-start.10 = (f32[128,16]{0,1:T(8,128)S(1)}, f32[128,16]{0,1:T(8,128)S(1)}, u32[]{:S(2)}, u32[]{:S(2)}) collective-permute-start(f32[128,16]{0,1:T(8,128)S(1)} %bitcast.295), channel_id=1, source_target_pairs={{0,16},{1,17},{2,18},{3,19},{4,20},{5,21},{6,22},{7,23},{8,24},{9,... | collective-permute-start | bytes 24584 | tf_op jit(solution)/shard_map/ppermute | solution.py:17
  63.8 5.5 %collective-permute-start.11 = (f32[128,16]{0,1:T(8,128)S(1)}, f32[128,16]{0,1:T(8,128)S(1)}, u32[]{:S(2)}, u32[]{:S(2)}) collective-permute-start(f32[128,16]{0,1:T(8,128)S(1)} %bitcast.296), channel_id=1, source_target_pairs={{16,0},{17,1},{18,2},{19,3},{20,4},{21,5},{22,6},{23,7},{24,8},{25... | collective-permute-start | bytes 24584 | tf_op jit(solution)/shard_map/ppermute | solution.py:17
  73.4 71.9 %collective-permute-start.14 = (f32[128,16]{0,1:T(8,128)}, f32[128,16]{0,1:T(8,128)S(1)}, u32[]{:S(2)}, u32[]{:S(2)}) collective-permute-start(f32[128,16]{0,1:T(8,128)} %bitcast_reduce_fusion), channel_id=1, source_target_pairs={{0,16},{1,17},{2,18},{3,19},{4,20},{5,21},{6,22},{7,23},{8,24},{9,... | collective-permute-start | bytes 24584 | tf_op jit(solution)/shard_map/ppermute | solution.py:17
  75.3 70.0 %collective-permute-start.15 = (f32[128,16]{0,1:T(8,128)}, f32[128,16]{0,1:T(8,128)S(1)}, u32[]{:S(2)}, u32[]{:S(2)}) collective-permute-start(f32[128,16]{0,1:T(8,128)} %bitcast_reduce_fusion), channel_id=1, source_target_pairs={{16,0},{17,1},{18,2},{19,3},{20,4},{21,5},{22,6},{23,7},{24,8},{25... | collective-permute-start | bytes 24584 | tf_op jit(solution)/shard_map/ppermute | solution.py:17
  76.6 69.5 %collective-permute-start.12 = (bf16[128,1024]{1,0:T(8,128)(2,1)}, bf16[128,1024]{1,0:T(8,128)(2,1)}, u32[]{:S(2)}, u32[]{:S(2)}) collective-permute-start(bf16[128,1024]{1,0:T(8,128)(2,1)} %get-tuple-element.364), channel_id=1, source_target_pairs={{0,16},{1,17},{2,18},{3,19},{4,20},{5,21},{6,22},{7,23},{8,24},{9,... | collective-permute-start | bytes 786440 | tf_op jit(solution)/shard_map/ppermute | solution.py:17
  81.8 64.2 %collective-permute-start.13 = (bf16[128,1024]{1,0:T(8,128)(2,1)}, bf16[128,1024]{1,0:T(8,128)(2,1)}, u32[]{:S(2)}, u32[]{:S(2)}) collective-permute-start(bf16[128,1024]{1,0:T(8,128)(2,1)} %get-tuple-element.364), channel_id=1, source_target_pairs={{16,0},{17,1},{18,2},{19,3},{20,4},{21,5},{22,6},{23,7},{24,8},{25... | collective-permute-start | bytes 786440 | tf_op jit(solution)/shard_map/ppermute | solution.py:17
  84.9 15.9 %copy-start.1 = (bf16[1024,1024]{1,0:T(8,128)(2,1)S(1)}, bf16[1024,1024]{1,0:T(8,128)(2,1)}, u32[]{:S(2)}) copy-start(bf16[1024,1024]{1,0:T(8,128)(2,1)} %all-gather.2.cloned.1.call-done) | copy-start | bytes 6291460
  146.0 1.7 copy-start.2
  146.0 1.7 copy-start.5
Sparse Core Ops, SparseCore 0:
  22.6 43.8 all-gather.1
  70.4 72.1 reduce-scatter.1
  147.8 23.4 all-reduce.1
where the time goes:
time: 181 us; the launch traced here: 180 us
  blocking collectives  42.5 us (23%)
  starting transfers between devices  38.7 us (21%)
  matrix products  33.7 us (19%)
  local copies, waits for them, and re-layouts  19.3 us (11%)
  waiting for transfers between devices  16.9 us (9%)
  between operations  14.2 us (8%)
  other arithmetic  13.7 us (8%)
    psum x1, blocking collectives, on_device(): bias_grad = lax.psum(bias_terms, ('ctx', 'dp'))  42.5 us
    ppermute x16, starting transfers between devices, shifted_2(): return lax.ppermute(shard, axis, pairs)  38.6 us
    unnamed x35, local copies, waits for them, and re-layouts  11.7 us
    psum x1, waiting for transfers between devices, on_device(): w_grad = lax.psum(partial_rows, 'ctx')  8.41 us
    ppermute x16, waiting for transfers between devices, shifted_2(): return lax.ppermute(shard, axis, pairs)  8.41 us
    dot_general x4, matrix products, query_group(): jnp.einsum('qhd,khd->hqk', d_group, v_group, preferred_element_type=jnp.f...  7.44 us
    dot_general x8, matrix products, scored(): jnp.einsum('qhd,khd->hqk', q_group, k_group, preferred_element_type=jnp.f...  7.35 us
    dot_general x4, matrix products, query_group(): jnp.einsum('hqk,khd->qhd', dscore.astype(jnp.bfloat16), k_group, preferre...  4.94 us
  transfers between devices with their start and end apart: 19, of which 5 were waited for; matrix products, arithmetic and copies ran while one was open for 35% of the time, Pallas kernels for 0%

commit v1 on v0

v1 whole, which is shorter than its diff:
```python
import functools

import jax
import jax.numpy as jnp
from jax import lax
from jax.experimental import pallas as pl
from jax.experimental.pallas import tpu as pltpu
from jax.sharding import PartitionSpec as P


HEADS = 16
HEAD_DIM = 64
GROUP = 4
PAIR = GROUP * HEAD_DIM
SCALE = HEAD_DIM ** -0.5
NEG = -1e30
BF = jnp.bfloat16
F32 = jnp.float32


def dot_nt(a, b):
    return lax.dot_general(a, b, (((1,), (1,)), ((), ())), preferred_element_type=F32)


def dot_tn(a, b):
    return lax.dot_general(a, b, (((0,), (0,)), ((), ())), preferred_element_type=F32)


def dot_nn(a, b):
    return lax.dot_general(a, b, (((1,), (0,)), ((), ())), preferred_element_type=F32)


def both(own_ref, oth_ref):
    return jnp.concatenate([own_ref[...], oth_ref[...]], axis=0)


def id_masks(own_ref, oth_ref):
    row = jnp.concatenate([own_ref[...], oth_ref[...]], axis=1)
    col = jnp.transpose(jnp.broadcast_to(row, (128, row.shape[1])))[:, :1]
    return row, col


def forward_kernel(bias_ref, ido_ref, idx_ref, qo_ref, qx_ref, ko_ref, kx_ref, vo_ref, vx_ref,
                   ctx_ref, wo_ref, wx_ref, neg_ref, same_ref):
    pair = pl.program_id(0)
    tok = qo_ref.shape[0]
    n = neg_ref.shape[0] // tok

    @pl.when(pair == 0)
    def _():
        row, col = id_masks(ido_ref, idx_ref)
        neg_ref[...] = jnp.where((row >> 8) == (col >> 8), 0.0, NEG)
        same_ref[...] = jnp.where((row & 255) == (col & 255), 1.0, 0.0)

    q = both(qo_ref, qx_ref)
    k = both(ko_ref, kx_ref)
    v = both(vo_ref, vx_ref)
    for half in range(GROUP):
        head = GROUP * pair + half
        gap = bias_ref[0, head] - bias_ref[1, head]
        lanes = slice(half * HEAD_DIM, (half + 1) * HEAD_DIM)
        qh = q[:, lanes] * jnp.asarray(SCALE, BF)
        kh, vh = k[:, lanes], v[:, lanes]
        for chunk in range(n):
            rows = slice(chunk * tok, (chunk + 1) * tok)
            s = dot_nt(qh[rows], kh) + (same_ref[rows, :] * gap + neg_ref[rows, :])
            e = jnp.exp(s - jnp.max(s, axis=1, keepdims=True))
            w = (e * (1.0 / jnp.sum(e, axis=1, keepdims=True))).astype(BF)
            ctx_ref[rows, lanes] = dot_nn(w, vh)
            if chunk == 0:
                wo_ref[half] = w
            else:
                wx_ref[half, (chunk - 1) * tok:chunk * tok, :] = w[:, :tok]


def weight_kernel(where_ref, ctx_ref, do_ref, dx_ref, keep_ref, send_ref):
    grads = dot_tn(ctx_ref[...].astype(BF), both(do_ref, dx_ref))
    nb, block, cols = keep_ref.shape
    grads = grads.reshape(nb, 2, block, cols)
    low = where_ref[1] == 0
    keep_ref[...] = jnp.where(low, grads[:, 0], grads[:, 1])
    send_ref[...] = jnp.where(low, grads[:, 1], grads[:, 0]).astype(BF)


def backward_kernel(pieces, where_ref, ido_ref, idx_ref, do_ref, dx_ref, qo_ref, qx_ref, ko_ref,
                    kx_ref, vo_ref, vx_ref, ctx_ref, wo_ref, wx_ref, *rest):
    piece_refs = rest[:len(pieces)]
    mixed_ref, qg_ref, kg_ref, vg_ref, bg_ref, wbuf_ref, same_ref, acc_ref, dall_ref = rest[len(pieces):]
    pair = pl.program_id(0)
    tok = qo_ref.shape[0]
    block = wbuf_ref.shape[2]
    nb = PAIR // (2 * block)

    @pl.when(pair == 0)
    def _():
        row, col = id_masks(ido_ref, idx_ref)
        same_ref[...] = jnp.where((row & 255) == (col[:tok] & 255), 1.0, 0.0)
        acc_ref[...] = jnp.zeros_like(acc_ref)
        dall_ref[...] = both(do_ref, dx_ref)
        for piece, ref in zip(pieces, piece_refs):
            index = jnp.bitwise_xor(where_ref[2], piece)
            wbuf_ref[index // 2, index % 2] = ref[...]

    w = wbuf_ref[pl.ds(pair * nb, nb)].reshape(PAIR, wbuf_ref.shape[3])
    d_pair = dot_nt(dall_ref[...], w).astype(BF)
    ctx = ctx_ref[...]
    acc_ref[...] += dot_nn(ctx[:tok].astype(BF), w)
    prod = d_pair.astype(F32) * ctx
    q = both(qo_ref, qx_ref) * jnp.asarray(SCALE, BF)
    k = both(ko_ref, kx_ref)
    v = both(vo_ref, vx_ref)
    same = same_ref[...]
    for half in range(GROUP):
        lanes = slice(half * HEAD_DIM, (half + 1) * HEAD_DIM)
        dh, qh, kh, vh = d_pair[:, lanes], q[:, lanes], k[:, lanes], v[:, lanes]
        delta = jnp.sum(prod[:, lanes], axis=1, keepdims=True)
        wo, wx = wo_ref[half], wx_ref[half]
        ds = wo.astype(F32) * (dot_nt(dh[:tok], vh) - delta[:tok])
        bg_ref[0, 2 * half:2 * half + 1, :] = jnp.sum(ds * same, axis=0, keepdims=True)
        bg_ref[0, 2 * half + 1:2 * half + 2, :] = jnp.sum(ds, axis=0, keepdims=True)
        ds = ds.astype(BF)
        qg_ref[:, lanes] = (dot_nn(ds, kh) * SCALE).astype(BF)
        dx = (wx.astype(F32) * (dot_nt(dh[tok:], vh[:tok]) - delta[tok:])).astype(BF)
        kg_ref[:, lanes] = (dot_tn(ds[:, :tok], qh[:tok]) + dot_tn(dx, qh[tok:])).astype(BF)
        vg_ref[:, lanes] = (dot_tn(wo[:, :tok], dh[:tok]) + dot_tn(wx, dh[tok:])).astype(BF)

    @pl.when(pair == pl.num_programs(0) - 1)
    def _():
        mixed_ref[...] = acc_ref[...].astype(BF)


def on_device(queries, keys, values, d_mixed, series_ids, variate_ids, variate_bias, w_out):
    query, key_rows, value_rows, upstream = queries[0], keys[0], values[0], d_mixed[0]
    tok, width = query.shape
    n_ctx, n_dp = lax.axis_size("ctx"), lax.axis_size("dp")
    total, pairs, cols, block = tok * n_ctx, width // PAIR, width // n_ctx, width // n_dp
    me_ctx, me_dp = lax.axis_index("ctx"), lax.axis_index("dp")
    bits = [1 << i for i in range(n_dp.bit_length() - 1)]
    assert 1 << len(bits) == n_dp and n_dp > 1 and n_ctx > 1

    def swap(array, bit):
        return lax.ppermute(array, "dp", [(i, i ^ bit) for i in range(n_dp)])

    def turn(array, by):
        return lax.ppermute(array, "ctx", [(i, (i + by) % n_ctx) for i in range(n_ctx)])

    def others(array, axis):
        parts = [turn(array, by) for by in range(1, n_ctx)]
        return parts[0] if len(parts) == 1 else jnp.concatenate(parts, axis=axis)

    kx = others(key_rows, 0)
    vx = others(value_rows, 0)
    qx = others(query, 0)
    code = series_ids * 256 + variate_ids
    code_x = others(code, 1)
    dx = others(upstream, 0)

    pieces = {0: w_out}
    for bit in reversed(bits):
        for piece in list(pieces):
            pieces[piece ^ bit] = swap(pieces[piece], bit)
    order = list(pieces)
    where = jnp.stack([me_ctx, me_dp % 2, me_dp]).astype(jnp.int32)

    smem = pl.BlockSpec(memory_space=pltpu.SMEM)

    def whole(array):
        return pl.BlockSpec(array.shape, lambda i, *_: (0,) * array.ndim)

    def lane(rows):
        return pl.BlockSpec((rows, PAIR), lambda i, *_: (0, i))

    own, oth, row = lane(tok), lane(total - tok), lane(total)
    w_specs = [pl.BlockSpec((GROUP, tok, total), lambda i, *_: (i, 0, 0)),
               pl.BlockSpec((GROUP, total - tok, tok), lambda i, *_: (i, 0, 0))]
    params = pltpu.CompilerParams(dimension_semantics=("arbitrary",), vmem_limit_bytes=24 << 20)
    ctx, w_own, w_oth = pl.pallas_call(
        forward_kernel,
        grid=(pairs,),
        in_specs=[smem, whole(code), whole(code_x), own, oth, own, oth, own, oth],
        out_specs=[row, *w_specs],
        out_shape=[jax.ShapeDtypeStruct((total, width), F32),
                   jax.ShapeDtypeStruct((HEADS, tok, total), BF),
                   jax.ShapeDtypeStruct((HEADS, total - tok, tok), BF)],
        scratch_shapes=[pltpu.VMEM((total, total), F32), pltpu.VMEM((total, total), F32)],
        compiler_params=params,
        cost_estimate=pl.CostEstimate(flops=4 * HEADS * total * total * HEAD_DIM * 4,
                                      bytes_accessed=8 << 20, transcendentals=HEADS * total * total),
        name="forward",
    )(variate_bias, code, code_x, query, qx, key_rows, kx, value_rows, vx)

    half_spec = lambda rows: pl.BlockSpec((rows, cols), lambda i, where: (0, where[0]))
    keep, send = pl.pallas_call(
        weight_kernel,
        grid_spec=pltpu.PrefetchScalarGridSpec(
            num_scalar_prefetch=1,
            grid=(2,),
            in_specs=[pl.BlockSpec((total, width // 2), lambda i, *_: (0, i)), half_spec(tok),
                      half_spec(total - tok)],
            out_specs=[pl.BlockSpec((n_dp // 4, block, cols), lambda i, *_: (i, 0, 0))] * 2),
        out_shape=[jax.ShapeDtypeStruct((n_dp // 2, block, cols), F32),
                   jax.ShapeDtypeStruct((n_dp // 2, block, cols), BF)],
        compiler_params=params,
        cost_estimate=pl.CostEstimate(flops=2 * total * width * cols, bytes_accessed=4 << 20,
                                      transcendentals=0),
        name="weights",
    )(where, ctx, upstream, dx)

    for bit in bits:
        summed = keep + swap(send, bit).astype(F32)
        if bit != bits[-1]:
            low = (me_dp // (2 * bit)) % 2 == 0
            summed = summed.reshape(-1, 2, block, cols)
            keep = jnp.where(low, summed[:, 0], summed[:, 1])
            send = jnp.where(low, summed[:, 1], summed[:, 0]).astype(BF)
    summed = summed[0]
    sent = summed.astype(BF)
    if n_ctx == 2:
        got = turn(sent, 1).astype(F32)
        first = me_ctx == 0
        w_grad = jnp.concatenate([jnp.where(first, summed, got), jnp.where(first, got, summed)], axis=1)
    else:
        parts = [summed] + [turn(sent, by).astype(F32) for by in range(1, n_ctx)]
        w_grad = jnp.concatenate(
            [sum(jnp.where((me_ctx - by) % n_ctx == c, part, 0.0) for by, part in enumerate(parts))
             for c in range(n_ctx)], axis=1)

    mixed, q_grad, k_grad, v_grad, bias_rows = pl.pallas_call(
        functools.partial(backward_kernel, order),
        grid=(pairs,),
        in_specs=[smem, whole(code), whole(code_x), whole(upstream), whole(dx), own, oth, own, oth,
                  own, oth, row, *w_specs, *[whole(w_out)] * n_dp],
        out_specs=[whole(query), own, own, own, pl.BlockSpec((1, 2 * GROUP, total), lambda i, *_: (i, 0, 0))],
        out_shape=[jax.ShapeDtypeStruct((tok, width), BF)] * 4
        + [jax.ShapeDtypeStruct((pairs, 2 * GROUP, total), F32)],
        scratch_shapes=[pltpu.VMEM((n_dp // 2, 2, block, width), BF), pltpu.VMEM((tok, total), F32),
                        pltpu.VMEM((tok, width), F32), pltpu.VMEM((total, width), BF)],
        compiler_params=params,
        cost_estimate=pl.CostEstimate(flops=10 * HEADS * total * total * HEAD_DIM * 4,
                                      bytes_accessed=10 << 20, transcendentals=0),
        name="backward",
    )(where, code, code_x, upstream, dx, query, qx, key_rows, kx, value_rows, vx, ctx, w_own, w_oth,
      *[pieces[p] for p in order])

    sums = jnp.sum(bias_rows, axis=2)
    for bit in bits:
        sums = sums + swap(sums, bit)
    sums = sum((turn(sums, by) for by in range(1, n_ctx)), sums)
    sums = sums.reshape(pairs, GROUP, 2)
    bias_grad = jnp.stack([sums[:, :, 0].reshape(HEADS), (sums[:, :, 1] - sums[:, :, 0]).reshape(HEADS)])
    return mixed[None], q_grad[None], k_grad[None], v_grad[None], w_grad, bias_grad


def solution(mesh):
    data = P("dp", "ctx", None)

    return jax.shard_map(
        on_device,
        mesh=mesh,
        in_specs=(data, data, data, data, P("dp", "ctx"), P("dp", "ctx"), P(), P("dp", None)),
        out_specs=(data, data, data, data, P("dp", None), P()),
        check_vma=False,
    )
```

time: 181 us -> 106 us (0.59)
  blocking collectives: 42.5 us -> 0 us
  matrix products: 33.7 us -> 0 us
  waiting for transfers between devices: 16.9 us -> 46 us
  Pallas kernels: 0 us -> 18.2 us
  local copies, waits for them, and re-layouts: 19.3 us -> 5.64 us
  between operations: 14.2 us -> 0.93 us
  other arithmetic: 13.7 us -> 4.32 us
  starting transfers between devices: 38.7 us -> 30.1 us
    psum x1 -> x0, blocking collectives: 42.5 us -> none  [on_device(): bias_grad = lax.psum(bias_terms, ('ctx', 'dp'))]
    ppermute x16 -> x30, waiting for transfers between devices: 8.41 us -> 46 us  [the longest x7 23.5 us: turn(): lax.ppermute(array, 'ctx', [(i, (i + by) % n_ctx) for i in range(n_ctx)])]
    dot_general x31 -> x0, matrix products: 33.7 us -> none  [the longest x4 7.44 us: query_group(): jnp.einsum('qhd,khd->hqk', d_group, v_group, preferred_element_type=jnp.f...]
    pallas_call x0 -> x3, Pallas kernels: none -> 18.2 us  [the longest x1 10.7 us: on_device(): pl.pallas_call(functools.partial(backward_kernel, order), grid=(pairs,),...]
    ppermute x16 -> x30, starting transfers between devices: 38.6 us -> 30.1 us  [the longest x23 19.9 us: swap(): return lax.ppermute(array, 'dp', [(i, i ^ bit) for i in range(n_dp)])]
    psum x1 -> x0, waiting for transfers between devices: 8.41 us -> none  [on_device(): w_grad = lax.psum(partial_rows, 'ctx')]
    unnamed x35 -> x40, local copies, waits for them, and re-layouts: 11.7 us -> 5.2 us
    dynamic_update_slice x12 -> x0, other arithmetic: 4.45 us -> none  [the longest x8 4.38 us: on_device(): lax.map(forward_group, (q_groups, k_groups, v_groups, bias_groups))]
  transfers between devices with their start and end apart: 19 -> 30, of which waited for: 5 -> 14; matrix products, arithmetic and copies ran while one was open for 35% -> 4% of each run, Pallas kernels for 0% -> 16%
where the time goes in v1:
time: 106 us; the launch traced here: 105 us
  waiting for transfers between devices  46 us (43%)
  starting transfers between devices  30.1 us (28%)
  Pallas kernels  18.2 us (17%)
  local copies, waits for them, and re-layouts  5.64 us (5%)
  other arithmetic  4.32 us (4%)
    ppermute x7, waiting for transfers between devices, turn(): lax.ppermute(array, 'ctx', [(i, (i + by) % n_ctx) for i in range(n_ctx)])  23.5 us
    ppermute x23, waiting for transfers between devices, swap(): return lax.ppermute(array, 'dp', [(i, i ^ bit) for i in range(n_dp)])  22.5 us
    ppermute x23, starting transfers between devices, swap(): return lax.ppermute(array, 'dp', [(i, i ^ bit) for i in range(n_dp)])  19.9 us
    pallas_call x1, Pallas kernels, on_device(): pl.pallas_call(functools.partial(backward_kernel, order), grid=(pairs,),...  10.7 us
    ppermute x7, starting transfers between devices, turn(): lax.ppermute(array, 'ctx', [(i, (i + by) % n_ctx) for i in range(n_ctx)])  10.3 us
    pallas_call x1, Pallas kernels, on_device(): pl.pallas_call(forward_kernel, grid=(pairs,), in_specs=[smem, whole(code)...  6.1 us
    unnamed x40, local copies, waits for them, and re-layouts  5.2 us
    add x2, other arithmetic, on_device(): summed = keep + swap(send, bit).astype(F32)  2.66 us
  transfers between devices with their start and end apart: 30, of which 14 were waited for; matrix products, arithmetic and copies ran while one was open for 4% of the time, Pallas kernels for 16%

profile of v1, /device:TPU:0, one launch (start us, length us, event | category | flops | bytes accessed | tf_op | source)
XLA Modules:
  0.0 105.3 jit_solution(16910646142290556816)
XLA Ops:
  0.6 3.1 %collective-permute-start.2 = (bf16[128,1024]{1,0:T(8,128)(2,1)}, bf16[128,1024]{1,0:T(8,128)(2,1)S(1)}, u32[]{:S(2)}, u32[]{:S(2)}) collective-permute-start(bf16[128,1024]{1,0:T(8,128)(2,1)} %bitcast.76), channel_id=1, source_target_pairs={{0,16},{16,0},{1,17},{17,1},{2,18},{18,2},{3,19},{19,3},{4,20},{20... | collective-permute-start | bytes 786440 | tf_op jit(solution)/shard_map/ppermute | solution.py:145
  3.8 1.9 %collective-permute-start.4 = (bf16[128,1024]{1,0:T(8,128)(2,1)}, bf16[128,1024]{1,0:T(8,128)(2,1)S(1)}, u32[]{:S(2)}, u32[]{:S(2)}) collective-permute-start(bf16[128,1024]{1,0:T(8,128)(2,1)} %bitcast.82), channel_id=1, source_target_pairs={{0,16},{16,0},{1,17},{17,1},{2,18},{18,2},{3,19},{19,3},{4,20},{20... | collective-permute-start | bytes 786440 | tf_op jit(solution)/shard_map/ppermute | solution.py:145
  5.8 2.0 %collective-permute-start = (s32[1,128]{1,0:T(1,128)S(1)}, s32[1,128]{1,0:T(1,128)S(1)}, u32[]{:S(2)}, u32[]{:S(2)}) collective-permute-start(s32[1,128]{1,0:T(1,128)S(1)} %multiply_add_fusion.ido_ref), channel_id=1, source_target_pairs={{0,16},{16,0},{1,17},{17,1},{2,18},{18,2},{3,19},{19,3},{4,20},{20... | collective-permute-start | bytes 1544 | tf_op jit(solution)/shard_map/ppermute | solution.py:145
  7.9 19.3 %collective-permute-done.idx_ref = s32[1,128]{1,0:T(1,128)S(1)} collective-permute-done((s32[1,128]{1,0:T(1,128)S(1)}, s32[1,128]{1,0:T(1,128)S(1)}, u32[]{:S(2)}, u32[]{:S(2)}) %collective-permute-start) | collective-permute-done | bytes 544 | tf_op jit(solution)/shard_map/ppermute | solution.py:145
  27.2 1.0 copy-done.1
  28.2 0.9 copy-done.3
  29.2 0.9 copy-done.5
  30.1 6.1 %forward.1 = (f32[256,1024]{1,0:T(8,128)S(1)}, bf16[16,128,256]{2,1,0:T(8,128)(2,1)S(1)}, bf16[16,128,128]{2,1,0:T(8,128)(2,1)S(1)}) custom-call(f32[2,16]{1,0:T(2,128)S(1)} %copy-done.12, s32[1,128]{1,0:T(1,128)S(1)} %multiply_add_fusion.ido_ref, s32[1,128]{1,0:T(1,128)S(1)} %collective-permute-done.idx_ref, bf16[128,1024]{1,0:T(8,128)(2,1)S(1)} %bitcast.77, ...), custom_call_target="tpu_custom_call" | custom-call | flops 1073741824 | bytes 8388608 | tf_op jit(solution)/shard_map/forward/pallas_call | solution.py:177
  36.3 1.0 copy-done.13
  37.3 1.4 %weights.1 = (f32[8,64,512]{2,1,0:T(8,128)S(1)}, bf16[8,64,512]{2,1,0:T(8,128)(2,1)S(1)}) custom-call(s32[3]{0:T(128)S(1)} %pad_add_fusion.where_ref, f32[256,1024]{1,0:T(8,128)S(1)} %get-tuple-element.16.ctx_ref, bf16[128,1024]{1,0:T(8,128)(2,1)S(1)} %bitcast.74, bf16[128,1024]{1,0:T(8,128)(2,1)S(1)} %collective-permute-done.1.dx_ref), custom_call_target="tpu_custom_call" | custom-call | flops 268435456 | bytes 4194304 | tf_op jit(solution)/shard_map/weights/pallas_call | solution.py:193
  38.8 2.9 %collective-permute-start.5 = (bf16[64,1024]{1,0:T(8,128)(2,1)S(1)}, bf16[64,1024]{1,0:T(8,128)(2,1)}, u32[]{:S(2)}, u32[]{:S(2)}) collective-permute-start(bf16[64,1024]{1,0:T(8,128)(2,1)S(1)} %copy-done.11), channel_id=1, source_target_pairs={{0,8},{1,9},{2,10},{3,11},{4,12},{5,13},{6,14},{7,15},{8,0},{9,1},... | collective-permute-start | bytes 393224 | tf_op jit(solution)/shard_map/ppermute | solution.py:142
  41.6 1.2 %convert_add_fusion = f32[8,64,512]{2,1,0:T(8,128)S(1)} fusion(f32[8,64,512]{2,1,0:T(8,128)S(1)} %get-tuple-element.23, bf16[8,64,512]{2,1,0:T(8,128)(2,1)} %collective-permute-done.20), kind=kLoop, calls=%fused_computation | loop fusion | flops 524288 | bytes 2621440 | tf_op jit(solution)/shard_map/add | solution.py:210
  43.0 1.6 %collective-permute-start.21 = (bf16[4,64,512]{2,1,0:T(8,128)(2,1)S(1)}, bf16[4,64,512]{2,1,0:T(8,128)(2,1)S(1)}, u32[]{:S(2)}, u32[]{:S(2)}) collective-permute-start(bf16[4,64,512]{2,1,0:T(8,128)(2,1)S(1)} %fusion), channel_id=1, source_target_pairs={{0,2},{1,3},{2,0},{3,1},{4,6},{5,7},{6,4},{7,5},{8,10},{9,11},{10,... | collective-permute-start | bytes 786440 | tf_op jit(solution)/shard_map/ppermute | solution.py:142
  44.5 1.6 %collective-permute-start.6 = (bf16[64,1024]{1,0:T(8,128)(2,1)S(1)}, bf16[64,1024]{1,0:T(8,128)(2,1)S(1)}, u32[]{:S(2)}, u32[]{:S(2)}) collective-permute-start(bf16[64,1024]{1,0:T(8,128)(2,1)S(1)} %copy-done.11), channel_id=1, source_target_pairs={{0,4},{1,5},{2,6},{3,7},{4,0},{5,1},{6,2},{7,3},{8,12},{9,13},{10,... | collective-permute-start | bytes 393224 | tf_op jit(solution)/shard_map/ppermute | solution.py:142
  46.1 0.5 collective-permute-start.8
  46.6 2.1 %collective-permute-done.5.rest_1_ = bf16[64,1024]{1,0:T(8,128)(2,1)} collective-permute-done((bf16[64,1024]{1,0:T(8,128)(2,1)S(1)}, bf16[64,1024]{1,0:T(8,128)(2,1)}, u32[]{:S(2)}, u32[]{:S(2)}) %collective-permute-start.5) | collective-permute-done | bytes 131104 | tf_op jit(solution)/shard_map/ppermute | solution.py:142
  48.7 0.6 collective-permute-start.7
  49.3 2.1 %collective-permute-done.6.rest_2_ = bf16[64,1024]{1,0:T(8,128)(2,1)S(1)} collective-permute-done((bf16[64,1024]{1,0:T(8,128)(2,1)S(1)}, bf16[64,1024]{1,0:T(8,128)(2,1)S(1)}, u32[]{:S(2)}, u32[]{:S(2)}) %collective-permute-start.6) | collective-permute-done | bytes 131104 | tf_op jit(solution)/shard_map/ppermute | solution.py:142
  51.4 2.7 %collective-permute-done.8.rest_4_ = bf16[64,1024]{1,0:T(8,128)(2,1)S(1)} collective-permute-done((bf16[64,1024]{1,0:T(8,128)(2,1)S(1)}, bf16[64,1024]{1,0:T(8,128)(2,1)S(1)}, u32[]{:S(2)}, u32[]{:S(2)}) %collective-permute-start.8) | collective-permute-done | bytes 131104 | tf_op jit(solution)/shard_map/ppermute | solution.py:142
  54.2 1.5 %collective-permute-start.10 = (bf16[64,1024]{1,0:T(8,128)(2,1)S(1)}, bf16[64,1024]{1,0:T(8,128)(2,1)S(1)}, u32[]{:S(2)}, u32[]{:S(2)}) collective-permute-start(bf16[64,1024]{1,0:T(8,128)(2,1)S(1)} %collective-permute-done.6.rest_2_), channel_id=1, source_target_pairs={{0,2},{1,3},{2,0},{3,1},{4,6},{5,7},{6,4},{7,5},{8,10},{9,11},{10,... | collective-permute-start | bytes 393224 | tf_op jit(solution)/shard_map/ppermute | solution.py:142
  55.7 0.5 collective-permute-start.9
  56.2 1.6 %collective-permute-start.11 = (bf16[64,1024]{1,0:T(8,128)(2,1)S(1)}, bf16[64,1024]{1,0:T(8,128)(2,1)S(1)}, u32[]{:S(2)}, u32[]{:S(2)}) collective-permute-start(bf16[64,1024]{1,0:T(8,128)(2,1)S(1)} %collective-permute-done.7.rest_3_), channel_id=1, source_target_pairs={{0,2},{1,3},{2,0},{3,1},{4,6},{5,7},{6,4},{7,5},{8,10},{9,11},{10,... | collective-permute-start | bytes 393224 | tf_op jit(solution)/shard_map/ppermute | solution.py:142
  57.8 1.4 %bitcast_add_fusion = f32[4,64,512]{2,1,0:T(8,128)S(1)} fusion(bf16[4,64,512]{2,1,0:T(8,128)(2,1)S(1)} %collective-permute-done.21, f32[4,2,64,512]{3,2,1,0:T(8,128)} %bitcast.86, pred[]{:T(512)S(6)} %eq.20), kind=kLoop, calls=%fused_computation.3 | loop fusion | flops 393216 | bytes 1835009 | tf_op jit(solution)/shard_map/add | solution.py:210
  59.2 0.2 collective-permute-start.13
  59.5 0.3 collective-permute-start.15
  59.8 0.7 collective-permute-done.10.rest_6_
  60.6 2.5 %collective-permute-done.9.rest_5_ = bf16[64,1024]{1,0:T(8,128)(2,1)S(1)} collective-permute-done((bf16[64,1024]{1,0:T(8,128)(2,1)}, bf16[64,1024]{1,0:T(8,128)(2,1)S(1)}, u32[]{:S(2)}, u32[]{:S(2)}) %collective-permute-start.9) | collective-permute-done | bytes 131104 | tf_op jit(solution)/shard_map/ppermute | solution.py:142
  63.1 1.4 %collective-permute-done.11.rest_7_ = bf16[64,1024]{1,0:T(8,128)(2,1)S(1)} collective-permute-done((bf16[64,1024]{1,0:T(8,128)(2,1)S(1)}, bf16[64,1024]{1,0:T(8,128)(2,1)S(1)}, u32[]{:S(2)}, u32[]{:S(2)}) %collective-permute-start.11) | collective-permute-done | bytes 131104 | tf_op jit(solution)/shard_map/ppermute | solution.py:142
  64.6 1.6 %collective-permute-start.22 = (bf16[2,64,512]{2,1,0:T(8,128)(2,1)S(1)}, bf16[2,64,512]{2,1,0:T(8,128)(2,1)S(1)}, u32[]{:S(2)}, u32[]{:S(2)}) collective-permute-start(bf16[2,64,512]{2,1,0:T(8,128)(2,1)S(1)} %fusion.4), channel_id=1, source_target_pairs={{0,4},{1,5},{2,6},{3,7},{4,0},{5,1},{6,2},{7,3},{8,12},{9,13},{10,... | collective-permute-start | bytes 393224 | tf_op jit(solution)/shard_map/ppermute | solution.py:142
  66.3 1.2 %copy-done.14 = bf16[16,128,256]{2,1,0:T(8,128)(2,1)S(1)} copy-done((bf16[16,128,256]{2,1,0:T(8,128)(2,1)S(1)}, bf16[16,128,256]{2,1,0:T(8,128)(2,1)}, u32[]{:S(2)}) %copy-start.14) | copy-done | bytes 1048600
  67.5 10.7 %backward.1 = (bf16[128,1024]{1,0:T(8,128)(2,1)}, bf16[128,1024]{1,0:T(8,128)(2,1)}, bf16[128,1024]{1,0:T(8,128)(2,1)}, bf16[128,1024]{1,0:T(8,128)(2,1)}, f32[4,8,256]{2,1,0:T(8,128)S(1)}) custom-call(s32[3]{0:T(128)S(1)} %pad_add_fusion.where_ref, s32[1,128]{1,0:T(1,128)S(1)} %multiply_add_fusion.ido_ref, s32[1,128]{1,0:T(1,128)S(1)} %collective-permute-done.idx_ref, ...), custom_call_target="tpu_custom_call" | custom-call | flops 2684354560 | bytes 10485760 | tf_op jit(solution)/shard_map/backward/pallas_call | solution.py:228
  78.3 0.2 collective-permute-start.25
  78.5 0.9 collective-permute-done.25
  79.5 1.5 %collective-permute-start.26 = (f32[4,8]{1,0:T(4,128)S(1)}, f32[4,8]{1,0:T(4,128)S(1)}, u32[]{:S(2)}, u32[]{:S(2)}) collective-permute-start(f32[4,8]{1,0:T(4,128)S(1)} %add.55), channel_id=1, source_target_pairs={{0,2},{1,3},{2,0},{3,1},{4,6},{5,7},{6,4},{7,5},{8,10},{9,11},{10,... | collective-permute-start | bytes 392 | tf_op jit(solution)/shard_map/ppermute | solution.py:142
  81.0 2.1 %collective-permute-done.26 = f32[4,8]{1,0:T(4,128)S(1)} collective-permute-done((f32[4,8]{1,0:T(4,128)S(1)}, f32[4,8]{1,0:T(4,128)S(1)}, u32[]{:S(2)}, u32[]{:S(2)}) %collective-permute-start.26) | collective-permute-done | bytes 160 | tf_op jit(solution)/shard_map/ppermute | solution.py:142
  83.1 1.2 %collective-permute-start.27 = (f32[4,8]{1,0:T(4,128)S(1)}, f32[4,8]{1,0:T(4,128)S(1)}, u32[]{:S(2)}, u32[]{:S(2)}) collective-permute-start(f32[4,8]{1,0:T(4,128)S(1)} %add.56), channel_id=1, source_target_pairs={{0,4},{1,5},{2,6},{3,7},{4,0},{5,1},{6,2},{7,3},{8,12},{9,13},{10,... | collective-permute-start | bytes 392 | tf_op jit(solution)/shard_map/ppermute | solution.py:142
  84.3 2.4 %collective-permute-done.27 = f32[4,8]{1,0:T(4,128)S(1)} collective-permute-done((f32[4,8]{1,0:T(4,128)S(1)}, f32[4,8]{1,0:T(4,128)S(1)}, u32[]{:S(2)}, u32[]{:S(2)}) %collective-permute-start.27) | collective-permute-done | bytes 160 | tf_op jit(solution)/shard_map/ppermute | solution.py:142
  86.7 1.9 %collective-permute-start.28 = (f32[4,8]{1,0:T(4,128)S(1)}, f32[4,8]{1,0:T(4,128)S(1)}, u32[]{:S(2)}, u32[]{:S(2)}) collective-permute-start(f32[4,8]{1,0:T(4,128)S(1)} %add.57), channel_id=1, source_target_pairs={{0,8},{1,9},{2,10},{3,11},{4,12},{5,13},{6,14},{7,15},{8,0},{9,1},... | collective-permute-start | bytes 392 | tf_op jit(solution)/shard_map/ppermute | solution.py:142
  88.6 2.5 %collective-permute-done.28 = f32[4,8]{1,0:T(4,128)S(1)} collective-permute-done((f32[4,8]{1,0:T(4,128)S(1)}, f32[4,8]{1,0:T(4,128)S(1)}, u32[]{:S(2)}, u32[]{:S(2)}) %collective-permute-start.28) | collective-permute-done | bytes 160 | tf_op jit(solution)/shard_map/ppermute | solution.py:142
  91.1 1.5 %collective-permute-start.29 = (f32[4,8]{1,0:T(4,128)S(1)}, f32[4,8]{1,0:T(4,128)S(1)}, u32[]{:S(2)}, u32[]{:S(2)}) collective-permute-start(f32[4,8]{1,0:T(4,128)S(1)} %add.58), channel_id=1, source_target_pairs={{0,16},{16,0},{1,17},{17,1},{2,18},{18,2},{3,19},{19,3},{4,20},{20... | collective-permute-start | bytes 392 | tf_op jit(solution)/shard_map/ppermute | solution.py:145
  92.7 2.1 %collective-permute-done.29 = f32[4,8]{1,0:T(4,128)S(1)} collective-permute-done((f32[4,8]{1,0:T(4,128)S(1)}, f32[4,8]{1,0:T(4,128)S(1)}, u32[]{:S(2)}, u32[]{:S(2)}) %collective-permute-start.29) | collective-permute-done | bytes 160 | tf_op jit(solution)/shard_map/ppermute | solution.py:145
  94.9 2.0 %collective-permute-start.23 = (bf16[1,64,512]{2,1,0:T(8,128)(2,1)S(1)}, bf16[1,64,512]{2,1,0:T(8,128)(2,1)S(1)}, u32[]{:S(2)}, u32[]{:S(2)}) collective-permute-start(bf16[1,64,512]{2,1,0:T(8,128)(2,1)S(1)} %fusion.5), channel_id=1, source_target_pairs={{0,8},{1,9},{2,10},{3,11},{4,12},{5,13},{6,14},{7,15},{8,0},{9,1},... | collective-permute-start | bytes 196616 | tf_op jit(solution)/shard_map/ppermute | solution.py:142
  96.9 0.1 copy.35
  97.3 2.9 %collective-permute-done.23 = bf16[1,64,512]{2,1,0:T(8,128)(2,1)S(1)} collective-permute-done((bf16[1,64,512]{2,1,0:T(8,128)(2,1)S(1)}, bf16[1,64,512]{2,1,0:T(8,128)(2,1)S(1)}, u32[]{:S(2)}, u32[]{:S(2)}) %collective-permute-start.23) | collective-permute-done | bytes 65568 | tf_op jit(solution)/shard_map/ppermute | solution.py:142
  100.2 1.6 %collective-permute-start.24 = (bf16[64,512]{1,0:T(8,128)(2,1)S(1)}, bf16[64,512]{1,0:T(8,128)(2,1)S(1)}, u32[]{:S(2)}, u32[]{:S(2)}) collective-permute-start(bf16[64,512]{1,0:T(8,128)(2,1)S(1)} %get-tuple-element.26), channel_id=1, source_target_pairs={{0,16},{16,0},{1,17},{17,1},{2,18},{18,2},{3,19},{19,3},{4,20},{20... | collective-permute-start | bytes 196616 | tf_op jit(solution)/shard_map/ppermute | solution.py:145
  101.8 0.6 pad_maximum_fusion.1
  102.3 2.2 %collective-permute-done.24 = bf16[64,512]{1,0:T(8,128)(2,1)S(1)} collective-permute-done((bf16[64,512]{1,0:T(8,128)(2,1)S(1)}, bf16[64,512]{1,0:T(8,128)(2,1)S(1)}, u32[]{:S(2)}, u32[]{:S(2)}) %collective-permute-start.24) | collective-permute-done | bytes 65568 | tf_op jit(solution)/shard_map/ppermute | solution.py:145
  104.5 0.7 pad_maximum_fusion
  (80 shorter events, 1.1 us)
Async XLA Ops:
  0.6 26.5 %collective-permute-start.2 = (bf16[128,1024]{1,0:T(8,128)(2,1)}, bf16[128,1024]{1,0:T(8,128)(2,1)S(1)}, u32[]{:S(2)}, u32[]{:S(2)}) collective-permute-start(bf16[128,1024]{1,0:T(8,128)(2,1)} %bitcast.76), channel_id=1, source_target_pairs={{0,16},{16,0},{1,17},{17,1},{2,18},{18,2},{3,19},{19,3},{4,20},{20... | collective-permute-start | bytes 786440 | tf_op jit(solution)/shard_map/ppermute | solution.py:145
  3.7 23.5 %collective-permute-start.3 = (bf16[128,1024]{1,0:T(8,128)(2,1)}, bf16[128,1024]{1,0:T(8,128)(2,1)S(1)}, u32[]{:S(2)}, u32[]{:S(2)}) collective-permute-start(bf16[128,1024]{1,0:T(8,128)(2,1)} %bitcast.79), channel_id=1, source_target_pairs={{0,16},{16,0},{1,17},{17,1},{2,18},{18,2},{3,19},{19,3},{4,20},{20... | collective-permute-start | bytes 786440 | tf_op jit(solution)/shard_map/ppermute | solution.py:145
  3.8 2.0 %copy-start.18 = (s32[1,128]{1,0:T(1,128)S(1)}, s32[1,128]{1,0:T(1,128)}, u32[]{:S(2)}) copy-start(s32[1,128]{1,0:T(1,128)} %param.13) | copy-start | bytes 1540
  3.8 2.0 %copy-start.19 = (s32[1,128]{1,0:T(1,128)S(1)}, s32[1,128]{1,0:T(1,128)}, u32[]{:S(2)}) copy-start(s32[1,128]{1,0:T(1,128)} %param.12) | copy-start | bytes 1540
  3.8 23.4 %collective-permute-start.4 = (bf16[128,1024]{1,0:T(8,128)(2,1)}, bf16[128,1024]{1,0:T(8,128)(2,1)S(1)}, u32[]{:S(2)}, u32[]{:S(2)}) collective-permute-start(bf16[128,1024]{1,0:T(8,128)(2,1)} %bitcast.82), channel_id=1, source_target_pairs={{0,16},{16,0},{1,17},{17,1},{2,18},{18,2},{3,19},{19,3},{4,20},{20... | collective-permute-start | bytes 786440 | tf_op jit(solution)/shard_map/ppermute | solution.py:145
  5.7 31.5 %collective-permute-start.1 = (bf16[128,1024]{1,0:T(8,128)(2,1)}, bf16[128,1024]{1,0:T(8,128)(2,1)S(1)}, u32[]{:S(2)}, u32[]{:S(2)}) collective-permute-start(bf16[128,1024]{1,0:T(8,128)(2,1)} %bitcast.73), channel_id=1, source_target_pairs={{0,16},{16,0},{1,17},{17,1},{2,18},{18,2},{3,19},{19,3},{4,20},{20... | collective-permute-start | bytes 786440 | tf_op jit(solution)/shard_map/ppermute | solution.py:145
  5.8 21.3 %collective-permute-start = (s32[1,128]{1,0:T(1,128)S(1)}, s32[1,128]{1,0:T(1,128)S(1)}, u32[]{:S(2)}, u32[]{:S(2)}) collective-permute-start(s32[1,128]{1,0:T(1,128)S(1)} %multiply_add_fusion.ido_ref), channel_id=1, source_target_pairs={{0,16},{16,0},{1,17},{17,1},{2,18},{18,2},{3,19},{19,3},{4,20},{20... | collective-permute-start | bytes 1544 | tf_op jit(solution)/shard_map/ppermute | solution.py:145
  7.8 19.4 %copy-start.12 = (f32[2,16]{1,0:T(2,128)S(1)}, f32[2,16]{1,0:T(2,128)}, u32[]{:S(2)}) copy-start(f32[2,16]{1,0:T(2,128)} %bias_ref.1) | copy-start | bytes 388
  7.9 29.4 %copy-start = (bf16[1,128,1024]{2,1,0:T(8,128)(2,1)S(1)}, bf16[1,128,1024]{2,1,0:T(8,128)(2,1)}, u32[]{:S(2)}) copy-start(bf16[1,128,1024]{2,1,0:T(8,128)(2,1)} %param.11) | copy-start | bytes 786436
  27.2 9.1 %copy-start.7 = (bf16[128,1024]{1,0:T(8,128)(2,1)}, bf16[128,1024]{1,0:T(8,128)(2,1)S(1)}, u32[]{:S(2)}) copy-start(bf16[128,1024]{1,0:T(8,128)(2,1)S(1)} %collective-permute-done.3.kx_ref) | copy-start | bytes 786436
  27.2 1.0 copy-start.1
  30.1 6.1 %copy-start.9 = (bf16[128,1024]{1,0:T(8,128)(2,1)}, bf16[128,1024]{1,0:T(8,128)(2,1)S(1)}, u32[]{:S(2)}) copy-start(bf16[128,1024]{1,0:T(8,128)(2,1)S(1)} %collective-permute-done.4.vx_ref) | copy-start | bytes 786436
  36.3 1.0 copy-start.13
  37.3 1.4 %copy-start.15 = (bf16[16,128,128]{2,1,0:T(8,128)(2,1)}, bf16[16,128,128]{2,1,0:T(8,128)(2,1)S(1)}, u32[]{:S(2)}) copy-start(bf16[16,128,128]{2,1,0:T(8,128)(2,1)S(1)} %get-tuple-element.18.wx_ref) | copy-start | bytes 1572868
  37.3 1.5 %copy-start.11 = (bf16[64,1024]{1,0:T(8,128)(2,1)S(1)}, bf16[64,1024]{1,0:T(8,128)(2,1)}, u32[]{:S(2)}) copy-start(bf16[64,1024]{1,0:T(8,128)(2,1)} %rest_0_.1) | copy-start | bytes 393220
  38.7 3.0 %collective-permute-start.20 = (bf16[8,64,512]{2,1,0:T(8,128)(2,1)S(1)}, bf16[8,64,512]{2,1,0:T(8,128)(2,1)}, u32[]{:S(2)}, u32[]{:S(2)}) collective-permute-start(bf16[8,64,512]{2,1,0:T(8,128)(2,1)S(1)} %get-tuple-element.24), channel_id=1, source_target_pairs={{0,1},{1,0},{2,3},{3,2},{4,5},{5,4},{6,7},{7,6},{8,9},{9,8},{10,11... | collective-permute-start | bytes 1572872 | tf_op jit(solution)/shard_map/ppermute | solution.py:142
  38.8 10.0 %collective-permute-start.5 = (bf16[64,1024]{1,0:T(8,128)(2,1)S(1)}, bf16[64,1024]{1,0:T(8,128)(2,1)}, u32[]{:S(2)}, u32[]{:S(2)}) collective-permute-start(bf16[64,1024]{1,0:T(8,128)(2,1)S(1)} %copy-done.11), channel_id=1, source_target_pairs={{0,8},{1,9},{2,10},{3,11},{4,12},{5,13},{6,14},{7,15},{8,0},{9,1},... | collective-permute-start | bytes 393224 | tf_op jit(solution)/shard_map/ppermute | solution.py:142
  42.9 5.9 %copy-start.17 = (f32[8,64,512]{2,1,0:T(8,128)}, f32[8,64,512]{2,1,0:T(8,128)S(1)}, u32[]{:S(2)}) copy-start(f32[8,64,512]{2,1,0:T(8,128)S(1)} %convert_add_fusion) | copy-start | bytes 3145732
  43.0 13.3 %collective-permute-start.21 = (bf16[4,64,512]{2,1,0:T(8,128)(2,1)S(1)}, bf16[4,64,512]{2,1,0:T(8,128)(2,1)S(1)}, u32[]{:S(2)}, u32[]{:S(2)}) collective-permute-start(bf16[4,64,512]{2,1,0:T(8,128)(2,1)S(1)} %fusion), channel_id=1, source_target_pairs={{0,2},{1,3},{2,0},{3,1},{4,6},{5,7},{6,4},{7,5},{8,10},{9,11},{10,... | collective-permute-start | bytes 786440 | tf_op jit(solution)/shard_map/ppermute | solution.py:142
  44.5 6.9 %collective-permute-start.6 = (bf16[64,1024]{1,0:T(8,128)(2,1)S(1)}, bf16[64,1024]{1,0:T(8,128)(2,1)S(1)}, u32[]{:S(2)}, u32[]{:S(2)}) collective-permute-start(bf16[64,1024]{1,0:T(8,128)(2,1)S(1)} %copy-done.11), channel_id=1, source_target_pairs={{0,4},{1,5},{2,6},{3,7},{4,0},{5,1},{6,2},{7,3},{8,12},{9,13},{10,... | collective-permute-start | bytes 393224 | tf_op jit(solution)/shard_map/ppermute | solution.py:142
  46.1 8.1 %collective-permute-start.8 = (bf16[64,1024]{1,0:T(8,128)(2,1)S(1)}, bf16[64,1024]{1,0:T(8,128)(2,1)S(1)}, u32[]{:S(2)}, u32[]{:S(2)}) collective-permute-start(bf16[64,1024]{1,0:T(8,128)(2,1)S(1)} %copy-done.11), channel_id=1, source_target_pairs={{0,2},{1,3},{2,0},{3,1},{4,6},{5,7},{6,4},{7,5},{8,10},{9,11},{10,... | collective-permute-start | bytes 393224 | tf_op jit(solution)/shard_map/ppermute | solution.py:142
  46.6 9.1 %collective-permute-start.12 = (bf16[64,1024]{1,0:T(8,128)(2,1)S(1)}, bf16[64,1024]{1,0:T(8,128)(2,1)S(1)}, u32[]{:S(2)}, u32[]{:S(2)}) collective-permute-start(bf16[64,1024]{1,0:T(8,128)(2,1)S(1)} %copy-done.11), channel_id=1, source_target_pairs={{0,1},{1,0},{2,3},{3,2},{4,5},{5,4},{6,7},{7,6},{8,9},{9,8},{10,11... | collective-permute-start | bytes 393224 | tf_op jit(solution)/shard_map/ppermute | solution.py:142
  48.7 7.5 %collective-permute-start.7 = (bf16[64,1024]{1,0:T(8,128)(2,1)}, bf16[64,1024]{1,0:T(8,128)(2,1)S(1)}, u32[]{:S(2)}, u32[]{:S(2)}) collective-permute-start(bf16[64,1024]{1,0:T(8,128)(2,1)} %collective-permute-done.5.rest_1_), channel_id=1, source_target_pairs={{0,4},{1,5},{2,6},{3,7},{4,0},{5,1},{6,2},{7,3},{8,12},{9,13},{10,... | collective-permute-start | bytes 393224 | tf_op jit(solution)/shard_map/ppermute | solution.py:142
  49.3 16.9 %copy-start.16 = (bf16[16,128,128]{2,1,0:T(8,128)(2,1)S(1)}, bf16[16,128,128]{2,1,0:T(8,128)(2,1)}, u32[]{:S(2)}) copy-start(bf16[16,128,128]{2,1,0:T(8,128)(2,1)} %copy-done.15) | copy-start | bytes 1572868
  51.4 8.0 %collective-permute-start.14 = (bf16[64,1024]{1,0:T(8,128)(2,1)S(1)}, bf16[64,1024]{1,0:T(8,128)(2,1)S(1)}, u32[]{:S(2)}, u32[]{:S(2)}) collective-permute-start(bf16[64,1024]{1,0:T(8,128)(2,1)S(1)} %collective-permute-done.6.rest_2_), channel_id=1, source_target_pairs={{0,1},{1,0},{2,3},{3,2},{4,5},{5,4},{6,7},{7,6},{8,9},{9,8},{10,11... | collective-permute-start | bytes 393224 | tf_op jit(solution)/shard_map/ppermute | solution.py:142
  54.2 6.4 %collective-permute-start.10 = (bf16[64,1024]{1,0:T(8,128)(2,1)S(1)}, bf16[64,1024]{1,0:T(8,128)(2,1)S(1)}, u32[]{:S(2)}, u32[]{:S(2)}) collective-permute-start(bf16[64,1024]{1,0:T(8,128)(2,1)S(1)} %collective-permute-done.6.rest_2_), channel_id=1, source_target_pairs={{0,2},{1,3},{2,0},{3,1},{4,6},{5,7},{6,4},{7,5},{8,10},{9,11},{10,... | collective-permute-start | bytes 393224 | tf_op jit(solution)/shard_map/ppermute | solution.py:142
  55.7 7.4 %collective-permute-start.9 = (bf16[64,1024]{1,0:T(8,128)(2,1)}, bf16[64,1024]{1,0:T(8,128)(2,1)S(1)}, u32[]{:S(2)}, u32[]{:S(2)}) collective-permute-start(bf16[64,1024]{1,0:T(8,128)(2,1)} %collective-permute-done.5.rest_1_), channel_id=1, source_target_pairs={{0,2},{1,3},{2,0},{3,1},{4,6},{5,7},{6,4},{7,5},{8,10},{9,11},{10,... | collective-permute-start | bytes 393224 | tf_op jit(solution)/shard_map/ppermute | solution.py:142
  56.2 3.0 %collective-permute-start.16 = (bf16[64,1024]{1,0:T(8,128)(2,1)S(1)}, bf16[64,1024]{1,0:T(8,128)(2,1)S(1)}, u32[]{:S(2)}, u32[]{:S(2)}) collective-permute-start(bf16[64,1024]{1,0:T(8,128)(2,1)S(1)} %collective-permute-done.8.rest_4_), channel_id=1, source_target_pairs={{0,1},{1,0},{2,3},{3,2},{4,5},{5,4},{6,7},{7,6},{8,9},{9,8},{10,11... | collective-permute-start | bytes 393224 | tf_op jit(solution)/shard_map/ppermute | solution.py:142
  56.2 8.3 %collective-permute-start.11 = (bf16[64,1024]{1,0:T(8,128)(2,1)S(1)}, bf16[64,1024]{1,0:T(8,128)(2,1)S(1)}, u32[]{:S(2)}, u32[]{:S(2)}) collective-permute-start(bf16[64,1024]{1,0:T(8,128)(2,1)S(1)} %collective-permute-done.7.rest_3_), channel_id=1, source_target_pairs={{0,2},{1,3},{2,0},{3,1},{4,6},{5,7},{6,4},{7,5},{8,10},{9,11},{10,... | collective-permute-start | bytes 393224 | tf_op jit(solution)/shard_map/ppermute | solution.py:142
  57.8 8.5 %copy-start.4 = (bf16[1,128,1024]{2,1,0:T(8,128)(2,1)S(1)}, bf16[1,128,1024]{2,1,0:T(8,128)(2,1)}, u32[]{:S(2)}) copy-start(bf16[1,128,1024]{2,1,0:T(8,128)(2,1)} %param.9) | copy-start | bytes 786436
  57.8 8.5 %copy-start.6 = (bf16[1,128,1024]{2,1,0:T(8,128)(2,1)S(1)}, bf16[1,128,1024]{2,1,0:T(8,128)(2,1)}, u32[]{:S(2)}) copy-start(bf16[1,128,1024]{2,1,0:T(8,128)(2,1)} %param.10) | copy-start | bytes 786436
  57.8 8.5 %copy-start.8 = (bf16[128,1024]{1,0:T(8,128)(2,1)S(1)}, bf16[128,1024]{1,0:T(8,128)(2,1)}, u32[]{:S(2)}) copy-start(bf16[128,1024]{1,0:T(8,128)(2,1)} %copy-done.7) | copy-start | bytes 786436
  57.8 8.5 %copy-start.10 = (bf16[128,1024]{1,0:T(8,128)(2,1)S(1)}, bf16[128,1024]{1,0:T(8,128)(2,1)}, u32[]{:S(2)}) copy-start(bf16[128,1024]{1,0:T(8,128)(2,1)} %copy-done.9) | copy-start | bytes 786436
  59.2 7.0 %copy-start.2 = (bf16[1,128,1024]{2,1,0:T(8,128)(2,1)S(1)}, bf16[1,128,1024]{2,1,0:T(8,128)(2,1)}, u32[]{:S(2)}) copy-start(bf16[1,128,1024]{2,1,0:T(8,128)(2,1)} %param.8) | copy-start | bytes 786436
  59.2 5.3 %collective-permute-start.13 = (bf16[64,1024]{1,0:T(8,128)(2,1)}, bf16[64,1024]{1,0:T(8,128)(2,1)S(1)}, u32[]{:S(2)}, u32[]{:S(2)}) collective-permute-start(bf16[64,1024]{1,0:T(8,128)(2,1)} %collective-permute-done.5.rest_1_), channel_id=1, source_target_pairs={{0,1},{1,0},{2,3},{3,2},{4,5},{5,4},{6,7},{7,6},{8,9},{9,8},{10,11... | collective-permute-start | bytes 393224 | tf_op jit(solution)/shard_map/ppermute | solution.py:142
  59.5 6.7 %collective-permute-start.15 = (bf16[64,1024]{1,0:T(8,128)(2,1)S(1)}, bf16[64,1024]{1,0:T(8,128)(2,1)S(1)}, u32[]{:S(2)}, u32[]{:S(2)}) collective-permute-start(bf16[64,1024]{1,0:T(8,128)(2,1)S(1)} %collective-permute-done.7.rest_3_), channel_id=1, source_target_pairs={{0,1},{1,0},{2,3},{3,2},{4,5},{5,4},{6,7},{7,6},{8,9},{9,8},{10,11... | collective-permute-start | bytes 393224 | tf_op jit(solution)/shard_map/ppermute | solution.py:142
  60.6 5.6 %collective-permute-start.18 = (bf16[64,1024]{1,0:T(8,128)(2,1)S(1)}, bf16[64,1024]{1,0:T(8,128)(2,1)S(1)}, u32[]{:S(2)}, u32[]{:S(2)}) collective-permute-start(bf16[64,1024]{1,0:T(8,128)(2,1)S(1)} %collective-permute-done.10.rest_6_), channel_id=1, source_target_pairs={{0,1},{1,0},{2,3},{3,2},{4,5},{5,4},{6,7},{7,6},{8,9},{9,8},{10,11... | collective-permute-start | bytes 393224 | tf_op jit(solution)/shard_map/ppermute | solution.py:142
  63.1 3.1 %collective-permute-start.17 = (bf16[64,1024]{1,0:T(8,128)(2,1)S(1)}, bf16[64,1024]{1,0:T(8,128)(2,1)S(1)}, u32[]{:S(2)}, u32[]{:S(2)}) collective-permute-start(bf16[64,1024]{1,0:T(8,128)(2,1)S(1)} %collective-permute-done.9.rest_5_), channel_id=1, source_target_pairs={{0,1},{1,0},{2,3},{3,2},{4,5},{5,4},{6,7},{7,6},{8,9},{9,8},{10,11... | collective-permute-start | bytes 393224 | tf_op jit(solution)/shard_map/ppermute | solution.py:142
  64.5 1.7 %collective-permute-start.19 = (bf16[64,1024]{1,0:T(8,128)(2,1)S(1)}, bf16[64,1024]{1,0:T(8,128)(2,1)S(1)}, u32[]{:S(2)}, u32[]{:S(2)}) collective-permute-start(bf16[64,1024]{1,0:T(8,128)(2,1)S(1)} %collective-permute-done.11.rest_7_), channel_id=1, source_target_pairs={{0,1},{1,0},{2,3},{3,2},{4,5},{5,4},{6,7},{7,6},{8,9},{9,8},{10,11... | collective-permute-start | bytes 393224 | tf_op jit(solution)/shard_map/ppermute | solution.py:142
  64.6 30.3 %collective-permute-start.22 = (bf16[2,64,512]{2,1,0:T(8,128)(2,1)S(1)}, bf16[2,64,512]{2,1,0:T(8,128)(2,1)S(1)}, u32[]{:S(2)}, u32[]{:S(2)}) collective-permute-start(bf16[2,64,512]{2,1,0:T(8,128)(2,1)S(1)} %fusion.4), channel_id=1, source_target_pairs={{0,4},{1,5},{2,6},{3,7},{4,0},{5,1},{6,2},{7,3},{8,12},{9,13},{10,... | collective-permute-start | bytes 393224 | tf_op jit(solution)/shard_map/ppermute | solution.py:142
  66.3 1.2 %copy-start.14 = (bf16[16,128,256]{2,1,0:T(8,128)(2,1)S(1)}, bf16[16,128,256]{2,1,0:T(8,128)(2,1)}, u32[]{:S(2)}) copy-start(bf16[16,128,256]{2,1,0:T(8,128)(2,1)} %copy-done.13) | copy-start | bytes 3145732
  78.3 1.2 %collective-permute-start.25 = (f32[4,8]{1,0:T(4,128)S(1)}, f32[4,8]{1,0:T(4,128)S(1)}, u32[]{:S(2)}, u32[]{:S(2)}) collective-permute-start(f32[4,8]{1,0:T(4,128)S(1)} %reduce_sum.9), channel_id=1, source_target_pairs={{0,1},{1,0},{2,3},{3,2},{4,5},{5,4},{6,7},{7,6},{8,9},{9,8},{10,11... | collective-permute-start | bytes 392 | tf_op jit(solution)/shard_map/ppermute | solution.py:142
  79.5 3.6 %collective-permute-start.26 = (f32[4,8]{1,0:T(4,128)S(1)}, f32[4,8]{1,0:T(4,128)S(1)}, u32[]{:S(2)}, u32[]{:S(2)}) collective-permute-start(f32[4,8]{1,0:T(4,128)S(1)} %add.55), channel_id=1, source_target_pairs={{0,2},{1,3},{2,0},{3,1},{4,6},{5,7},{6,4},{7,5},{8,10},{9,11},{10,... | collective-permute-start | bytes 392 | tf_op jit(solution)/shard_map/ppermute | solution.py:142
  83.1 3.6 %collective-permute-start.27 = (f32[4,8]{1,0:T(4,128)S(1)}, f32[4,8]{1,0:T(4,128)S(1)}, u32[]{:S(2)}, u32[]{:S(2)}) collective-permute-start(f32[4,8]{1,0:T(4,128)S(1)} %add.56), channel_id=1, source_target_pairs={{0,4},{1,5},{2,6},{3,7},{4,0},{5,1},{6,2},{7,3},{8,12},{9,13},{10,... | collective-permute-start | bytes 392 | tf_op jit(solution)/shard_map/ppermute | solution.py:142
  86.7 4.5 %collective-permute-start.28 = (f32[4,8]{1,0:T(4,128)S(1)}, f32[4,8]{1,0:T(4,128)S(1)}, u32[]{:S(2)}, u32[]{:S(2)}) collective-permute-start(f32[4,8]{1,0:T(4,128)S(1)} %add.57), channel_id=1, source_target_pairs={{0,8},{1,9},{2,10},{3,11},{4,12},{5,13},{6,14},{7,15},{8,0},{9,1},... | collective-permute-start | bytes 392 | tf_op jit(solution)/shard_map/ppermute | solution.py:142
  91.1 3.6 %collective-permute-start.29 = (f32[4,8]{1,0:T(4,128)S(1)}, f32[4,8]{1,0:T(4,128)S(1)}, u32[]{:S(2)}, u32[]{:S(2)}) collective-permute-start(f32[4,8]{1,0:T(4,128)S(1)} %add.58), channel_id=1, source_target_pairs={{0,16},{16,0},{1,17},{17,1},{2,18},{18,2},{3,19},{19,3},{4,20},{20... | collective-permute-start | bytes 392 | tf_op jit(solution)/shard_map/ppermute | solution.py:145
  94.9 5.2 %collective-permute-start.23 = (bf16[1,64,512]{2,1,0:T(8,128)(2,1)S(1)}, bf16[1,64,512]{2,1,0:T(8,128)(2,1)S(1)}, u32[]{:S(2)}, u32[]{:S(2)}) collective-permute-start(bf16[1,64,512]{2,1,0:T(8,128)(2,1)S(1)} %fusion.5), channel_id=1, source_target_pairs={{0,8},{1,9},{2,10},{3,11},{4,12},{5,13},{6,14},{7,15},{8,0},{9,1},... | collective-permute-start | bytes 196616 | tf_op jit(solution)/shard_map/ppermute | solution.py:142
  100.2 4.3 %collective-permute-start.24 = (bf16[64,512]{1,0:T(8,128)(2,1)S(1)}, bf16[64,512]{1,0:T(8,128)(2,1)S(1)}, u32[]{:S(2)}, u32[]{:S(2)}) collective-permute-start(bf16[64,512]{1,0:T(8,128)(2,1)S(1)} %get-tuple-element.26), channel_id=1, source_target_pairs={{0,16},{16,0},{1,17},{17,1},{2,18},{18,2},{3,19},{19,3},{4,20},{20... | collective-permute-start | bytes 196616 | tf_op jit(solution)/shard_map/ppermute | solution.py:145
  (2 other events, 1.9 us)

commit v2 on v1

v2 whole, which is shorter than its diff:
```python
import functools

import jax
import jax.numpy as jnp
from jax import lax
from jax.experimental import pallas as pl
from jax.experimental.pallas import tpu as pltpu
from jax.sharding import PartitionSpec as P


HEADS = 16
HEAD_DIM = 64
GROUP = 4
LANES = GROUP * HEAD_DIM
SCALE = HEAD_DIM ** -0.5
NEG = -1e30
TAIL = 16
BF = jnp.bfloat16
F32 = jnp.float32


def dot_nt(a, b):
    return lax.dot_general(a, b, (((1,), (1,)), ((), ())), preferred_element_type=F32)


def dot_tn(a, b):
    return lax.dot_general(a, b, (((0,), (0,)), ((), ())), preferred_element_type=F32)


def dot_nn(a, b):
    return lax.dot_general(a, b, (((1,), (0,)), ((), ())), preferred_element_type=F32)


def both(own_ref, oth_ref):
    return jnp.concatenate([own_ref[...], oth_ref[...]], axis=0)


def columns(row):
    return jnp.transpose(jnp.broadcast_to(row, (128, row.shape[1])))[:, :1]


def low_bit(bit):
    return (lax.axis_index("dp") // bit) % 2 == 0


def prepare_kernel(series_ref, variate_ref, *refs):
    count = (len(refs) - 2) // 2
    sources, code_ref, targets, sem = refs[:count], refs[count], refs[count + 1:-1], refs[-1]
    copies = [pltpu.make_async_copy(source, target, sem.at[i])
              for i, (source, target) in enumerate(zip(sources, targets))]
    for copy in copies:
        copy.start()
    code_ref[...] = series_ref[...] * 256 + variate_ref[...]
    for copy in copies:
        copy.wait()


def each_group(width, body):
    def step(group, carry):
        body(group, pl.ds(pl.multiple_of(group * LANES, LANES), LANES))
        return carry

    lax.fori_loop(0, width // LANES, step, 0)


def forward_kernel(own, bias_ref, ido_ref, idx_ref, q_ref, ko_ref, kx_ref, vo_ref, vx_ref,
                   ctx_ref, w_ref, neg_ref, same_ref):
    count, tok = q_ref.shape[0], ko_ref.shape[0]
    row = jnp.concatenate([ido_ref[...], idx_ref[...]], axis=1)
    col = columns(ido_ref[...] if own else idx_ref[...])
    neg_ref[...] = jnp.where((row >> 8) == (col >> 8), 0.0, NEG)
    same_ref[...] = jnp.where((row & 255) == (col & 255), 1.0, 0.0)

    def body(group, at):
        k = jnp.concatenate([ko_ref[:, at], kx_ref[:, at]], axis=0)
        v = jnp.concatenate([vo_ref[:, at], vx_ref[:, at]], axis=0)
        q = q_ref[:, at] * jnp.asarray(SCALE, BF)
        for start in range(0, count, tok):
            rows = slice(start, start + tok)
            found = []
            for part in range(GROUP):
                head = GROUP * group + part
                gap = bias_ref[0, head] - bias_ref[1, head]
                lanes = slice(part * HEAD_DIM, (part + 1) * HEAD_DIM)
                s = dot_nt(q[rows, lanes], k[:, lanes]) + (same_ref[rows, :] * gap + neg_ref[rows, :])
                e = jnp.exp(s - jnp.max(s, axis=1, keepdims=True))
                w = (e * (1.0 / jnp.sum(e, axis=1, keepdims=True))).astype(BF)
                found.append(dot_nn(w, v[:, lanes]))
                w_ref[head, rows, :] = w if own else w[:, :tok]
            ctx_ref[rows, at] = jnp.concatenate(found, axis=1)

    each_group(ko_ref.shape[1], body)


def split(summed, bit, keep_ref, send_ref):
    n, block, cols = keep_ref.shape
    low = low_bit(bit)
    summed = summed.reshape(n, 2, block, cols)
    keep_ref[...] = jnp.where(low, summed[:, 0], summed[:, 1])
    send = jnp.where(low, summed[:, 1], summed[:, 0]).astype(BF)
    send_ref[:n * block, :] = send.reshape(n * block, cols)


def weight_kernel(co_ref, cx_ref, do_ref, dx_ref, keep_ref, send_ref):
    n, _, cols = keep_ref.shape
    cut = pl.ds(pl.multiple_of(lax.axis_index("ctx") * cols, 128), cols)
    d = jnp.concatenate([do_ref[:, cut], dx_ref[:, cut]], axis=0)
    half = co_ref.shape[1] // 2
    for part in range(2):
        at = slice(part * half, (part + 1) * half)
        c = jnp.concatenate([co_ref[:, at], cx_ref[:, at]], axis=0).astype(BF)
        split(dot_tn(c, d), 1, keep_ref.at[part * n // 2:(part + 1) * n // 2],
              send_ref.at[part * half // 2:(part + 1) * half // 2])


def pack_tail(sums, send_ref):
    rows, cols = send_ref.shape
    high = sums.astype(BF)
    low = (sums - high.astype(F32)).astype(BF)
    place = lax.broadcasted_iota(jnp.int32, (TAIL, 128), 0)
    tail = jnp.where(place == 0, high.astype(F32), jnp.where(place == 1, low.astype(F32), 0.0)).astype(BF)
    send_ref[rows - TAIL:, :128] = tail
    if cols > 128:
        send_ref[rows - TAIL:, 128:] = jnp.zeros((TAIL, cols - 128), BF)


def unpack_tail(got_ref):
    tail = got_ref[got_ref.shape[0] - TAIL:, :128].astype(F32)
    return tail[0:1] + tail[1:2]


def halve_kernel(bit, last, packed, keep_ref, got_ref, *refs):
    n, block, cols = keep_ref.shape
    summed = keep_ref[...] + got_ref[:n * block, :].astype(F32).reshape(n, block, cols)
    refs = list(refs)
    sums = None
    if packed is not None:
        sums = refs.pop(0)[...] + (refs.pop(0)[...] if packed == "apart" else unpack_tail(got_ref))
    out_ref, send_ref = refs[0], refs[1]
    if last:
        out_ref[...] = summed[0]
        send_ref[:block, :] = summed[0].astype(BF)
    else:
        split(summed, bit, out_ref, send_ref)
    if sums is not None:
        pack_tail(sums, send_ref)
        refs[2][...] = sums


def add_kernel(a_ref, b_ref, out_ref):
    out_ref[...] = a_ref[...] + b_ref[...]


def final_kernel(keep_ref, sums_ref, *refs):
    got, (w_ref, bias_ref) = refs[:-2], refs[-2:]
    block, cols = keep_ref.shape
    n, me = lax.axis_size("ctx"), lax.axis_index("ctx")
    sums = sums_ref[...]
    w_ref[:, pl.ds(pl.multiple_of(me * cols, 128), cols)] = keep_ref[...]
    for by, ref in enumerate(got, 1):
        sums = sums + unpack_tail(ref)
        at = pl.multiple_of(((me + n - by) % n) * cols, 128)
        w_ref[:, pl.ds(at, cols)] = ref[:block, :].astype(F32)
    same, total = sums[:, :HEADS], sums[:, HEADS:2 * HEADS]
    bias_ref[0:1, :] = same
    bias_ref[1:2, :] = total - same


def score_grad_kernel(pieces, ido_ref, idx_ref, do_ref, dx_ref, vo_ref, vx_ref, co_ref, cx_ref,
                      wo_ref, wx_ref, *rest):
    piece_refs = rest[:len(pieces)]
    wfull_ref, dc_ref, so_ref, sx_ref, sums_ref, same_ref, rows_ref = rest[len(pieces):]
    tok = vo_ref.shape[0]
    nb = LANES // (2 * wfull_ref.shape[2])
    row = jnp.concatenate([ido_ref[...], idx_ref[...]], axis=1)
    same_ref[...] = jnp.where((row & 255) == (columns(ido_ref[...]) & 255), 1.0, 0.0)
    for piece, ref in zip(pieces, piece_refs):
        index = jnp.bitwise_xor(lax.axis_index("dp"), piece)
        wfull_ref[index // 2, index % 2] = ref[...]

    def body(group, at):
        w = wfull_ref[pl.ds(group * nb, nb)].reshape(LANES, wfull_ref.shape[3])
        d = dot_nt(both(do_ref, dx_ref), w).astype(BF)
        dc_ref[:, at] = d
        prod = d.astype(F32) * jnp.concatenate([co_ref[:, at], cx_ref[:, at]], axis=0)
        v = jnp.concatenate([vo_ref[:, at], vx_ref[:, at]], axis=0)
        same = same_ref[...]
        for part in range(GROUP):
            lanes = slice(part * HEAD_DIM, (part + 1) * HEAD_DIM)
            dh, vh = d[:, lanes], v[:, lanes]
            delta = jnp.sum(prod[:, lanes], axis=1, keepdims=True)
            head = GROUP * group + part
            ds = wo_ref[head].astype(F32) * (dot_nt(dh[:tok], vh) - delta[:tok])
            rows_ref[pl.ds(head, 1), :] = jnp.sum(ds * same, axis=0, keepdims=True)
            rows_ref[pl.ds(HEADS + head, 1), :] = jnp.sum(ds, axis=0, keepdims=True)
            so_ref[head] = ds.astype(BF)
            sx_ref[head] = (wx_ref[head].astype(F32) * (dot_nt(dh[tok:], vh[:tok]) - delta[tok:])).astype(BF)

    each_group(vo_ref.shape[1], body)
    col = jnp.sum(rows_ref[...], axis=1, keepdims=True)
    col = jnp.concatenate([col, jnp.zeros((128 - 2 * HEADS, 1), F32)], axis=0)
    sums_ref[...] = jnp.transpose(jnp.broadcast_to(col, (128, 128)))[:1]


def input_grad_kernel(qo_ref, qx_ref, ko_ref, kx_ref, co_ref, dc_ref, wo_ref, wx_ref, so_ref, sx_ref,
                      wfull_ref, mixed_ref, qg_ref, kg_ref, vg_ref, acc_ref):
    tok = qo_ref.shape[0]
    nb = LANES // (2 * wfull_ref.shape[2])
    acc_ref[...] = jnp.zeros_like(acc_ref)

    def body(group, at):
        w = wfull_ref[pl.ds(group * nb, nb)].reshape(LANES, wfull_ref.shape[3])
        acc_ref[...] += dot_nn(co_ref[:, at].astype(BF), w)
        q = jnp.concatenate([qo_ref[:, at], qx_ref[:, at]], axis=0) * jnp.asarray(SCALE, BF)
        k = jnp.concatenate([ko_ref[:, at], kx_ref[:, at]], axis=0)
        d = dc_ref[:, at]
        found = []
        for part in range(GROUP):
            lanes = slice(part * HEAD_DIM, (part + 1) * HEAD_DIM)
            dh, qh, kh = d[:, lanes], q[:, lanes], k[:, lanes]
            head = GROUP * group + part
            so, sx, wo, wx = so_ref[head], sx_ref[head], wo_ref[head], wx_ref[head]
            found.append((dot_nn(so, kh) * SCALE,
                          dot_tn(so[:, :tok], qh[:tok]) + dot_tn(sx, qh[tok:]),
                          dot_tn(wo[:, :tok], dh[:tok]) + dot_tn(wx, dh[tok:])))
        for ref, parts in zip((qg_ref, kg_ref, vg_ref), zip(*found)):
            ref[:, at] = jnp.concatenate(parts, axis=1).astype(BF)

    each_group(qo_ref.shape[1], body)
    mixed_ref[...] = acc_ref[...].astype(BF)


def shape(dims, dtype):
    return jax.ShapeDtypeStruct(dims, dtype)


def cost(flops):
    return pl.CostEstimate(flops=flops, bytes_accessed=4 << 20, transcendentals=0)


def plain(kernel, args, outs, flops=1 << 22, scratch=(), in_specs=None, limit=8 << 20):
    spec = pl.BlockSpec(memory_space=pltpu.VMEM)
    return pl.pallas_call(
        kernel, in_specs=in_specs or [spec] * len(args), out_specs=[spec] * len(outs), out_shape=outs,
        scratch_shapes=scratch, compiler_params=pltpu.CompilerParams(vmem_limit_bytes=limit),
        cost_estimate=cost(flops))(*args)


def on_device(queries, keys, values, d_mixed, series_ids, variate_ids, variate_bias, w_out):
    query, key_rows, value_rows, upstream = queries[0], keys[0], values[0], d_mixed[0]
    tok, width = query.shape
    n_ctx, n_dp = lax.axis_size("ctx"), lax.axis_size("dp")
    total, cols, block = tok * n_ctx, width // n_ctx, width // n_dp
    rest = total - tok
    bits = [1 << i for i in range(n_dp.bit_length() - 1)]
    assert 1 << len(bits) == n_dp and len(bits) > 3 and n_ctx > 1

    def swap(array, bit):
        return lax.ppermute(array, "dp", [(i, i ^ bit) for i in range(n_dp)])

    def turns(array):
        return [lax.ppermute(array, "ctx", [(i, (i + by) % n_ctx) for i in range(n_ctx)])
                for by in range(1, n_ctx)]

    def others(array, axis):
        parts = turns(array)
        return parts[0] if len(parts) == 1 else jnp.concatenate(parts, axis=axis)

    kx = others(key_rows, 0)
    vx = others(value_rows, 0)
    qx = others(query, 0)
    vmem, smem, hbm = [pl.BlockSpec(memory_space=space) for space in (pltpu.VMEM, pltpu.SMEM, pltpu.HBM)]
    limit = (12 << 20) + 40 * total * width
    local = [query, key_rows, value_rows, upstream]
    code, query, key_rows, value_rows, upstream = plain(
        prepare_kernel, [series_ids, variate_ids, *local],
        [shape(series_ids.shape, jnp.int32)] + [shape(a.shape, BF) for a in local],
        scratch=[pltpu.SemaphoreType.DMA((len(local),))], in_specs=[vmem] * 2 + [hbm] * len(local))
    code_x = others(code, 1)
    dx = others(local[3], 0)

    pieces = {0: w_out}
    for bit in reversed(bits):
        for piece in list(pieces):
            pieces[piece ^ bit] = swap(pieces[piece], bit)
    order = list(pieces)

    o_shape, x_shape = shape((HEADS, tok, total), BF), shape((HEADS, rest, tok), BF)

    def forward(is_own, rows):
        args = [variate_bias, code, code_x, query if is_own else qx, key_rows, kx, value_rows, vx]
        return plain(functools.partial(forward_kernel, is_own), args,
                     [shape((rows, width), F32), o_shape if is_own else x_shape],
                     16 * HEADS * rows * total * HEAD_DIM, [pltpu.VMEM((rows, total), F32)] * 2,
                     [smem] + [vmem] * (len(args) - 1), limit)

    ctx_o, w_o = forward(True, tok)
    ctx_x, w_x = forward(False, rest)
    keep, send = plain(weight_kernel, [ctx_o, ctx_x, upstream, dx],
                       [shape((n_dp // 2, block, cols), F32), shape((width // 2, cols), BF)],
                       2 * total * width * cols, limit=limit)
    w_full, d_ctx, s_o, s_x, sums = plain(
        functools.partial(score_grad_kernel, order),
        [code, code_x, upstream, dx, value_rows, vx, ctx_o, ctx_x, w_o, w_x, *[pieces[p] for p in order]],
        [shape((n_dp // 2, 2, block, width), BF), shape((total, width), BF), o_shape, x_shape,
         shape((1, 128), F32)], 16 * HEADS * total * total * HEAD_DIM,
        [pltpu.VMEM((tok, total), F32), pltpu.VMEM((2 * HEADS, total), F32)], limit=limit)

    early = bits[:2]
    for bit in early:
        got = swap(sums, bit)
        if bit != early[-1]:
            sums, = plain(add_kernel, [sums, got], [shape((1, 128), F32)])
    for bit, after in zip(bits, bits[1:] + [None]):
        got_rows = swap(send, bit)
        n = keep.shape[0]
        packed = None if bit < early[-1] else ("apart" if bit == early[-1] else "joined")
        extra = {None: [], "apart": [sums, got], "joined": [sums]}[packed]
        rows = block if after is None else n // 2 * block
        outs = [shape((block, cols) if after is None else (n // 2, block, cols), F32),
                shape((rows + (TAIL if packed else 0), cols), BF)]
        if packed:
            outs.append(shape((1, 128), F32))
        done = plain(functools.partial(halve_kernel, after, after is None, packed),
                     [keep, got_rows, *extra], outs)
        keep, send = done[:2]
        if packed:
            sums = done[2]
    parts = turns(send)
    w_grad, bias_grad = plain(final_kernel, [keep, sums, *parts],
                              [shape((block, width), F32), shape((2, HEADS), F32)])
    mixed, q_grad, k_grad, v_grad = plain(
        input_grad_kernel, [query, qx, key_rows, kx, ctx_o, d_ctx, w_o, w_x, s_o, s_x, w_full],
        [shape((tok, width), BF)] * 4, 16 * HEADS * total * total * HEAD_DIM,
        [pltpu.VMEM((tok, width), F32)], limit=limit)
    return mixed[None], q_grad[None], k_grad[None], v_grad[None], w_grad, bias_grad


def solution(mesh):
    data = P("dp", "ctx", None)

    return jax.shard_map(
        on_device,
        mesh=mesh,
        in_specs=(data, data, data, data, P("dp", "ctx"), P("dp", "ctx"), P(), P("dp", None)),
        out_specs=(data, data, data, data, P("dp", None), P()),
        check_vma=False,
    )
```

time: 106 us -> 90 us (0.85)
  waiting for transfers between devices: 46 us -> 36.2 us
  other arithmetic: 4.32 us -> 0 us
  starting transfers between devices: 30.1 us -> 27.9 us
    ppermute x7 -> x6, waiting for transfers between devices: 23.5 us -> 14.1 us  [turns(): lax.ppermute(array, 'ctx', [(i, (i + by) % n_ctx) for i in range(n_ctx)])]
    add x8 -> x0, other arithmetic: 2.68 us -> none  [the longest x2 2.66 us: on_device(): summed = keep + swap(send, bit).astype(F32)]
    ppermute x7 -> x6, starting transfers between devices: 10.3 us -> 8.64 us  [turns(): lax.ppermute(array, 'ctx', [(i, (i + by) % n_ctx) for i in range(n_ctx)])]
    pallas_call x3 -> x12, Pallas kernels: 18.2 us -> 19.1 us  [plain(): pl.pallas_call(kernel, in_specs=in_specs or [spec] * len(args), out_specs...]
    ppermute x23 -> x21, starting transfers between devices: 19.9 us -> 19.2 us  [swap(): return lax.ppermute(array, 'dp', [(i, i ^ bit) for i in range(n_dp)])]
    unnamed x40 -> x16, local copies, waits for them, and re-layouts: 5.2 us -> 5.79 us
    ppermute x23 -> x21, waiting for transfers between devices: 22.5 us -> 22.1 us  [swap(): return lax.ppermute(array, 'dp', [(i, i ^ bit) for i in range(n_dp)])]
  transfers between devices with their start and end apart: 30 -> 27, of which waited for: 14 -> 10; matrix products, arithmetic and copies ran while one was open for 4% -> 0% of each run, Pallas kernels for 16% -> 20%
where the time goes in v2:
time: 90 us; the launch traced here: 89.8 us
  waiting for transfers between devices  36.2 us (40%)
  starting transfers between devices  27.9 us (31%)
  Pallas kernels  19.1 us (21%)
  local copies, waits for them, and re-layouts  5.79 us (6%)
    ppermute x21, waiting for transfers between devices, swap(): return lax.ppermute(array, 'dp', [(i, i ^ bit) for i in range(n_dp)])  22.1 us
    ppermute x21, starting transfers between devices, swap(): return lax.ppermute(array, 'dp', [(i, i ^ bit) for i in range(n_dp)])  19.2 us
    pallas_call x12, Pallas kernels, plain(): pl.pallas_call(kernel, in_specs=in_specs or [spec] * len(args), out_specs...  19.1 us
    ppermute x6, waiting for transfers between devices, turns(): lax.ppermute(array, 'ctx', [(i, (i + by) % n_ctx) for i in range(n_ctx)])  14.1 us
    ppermute x6, starting transfers between devices, turns(): lax.ppermute(array, 'ctx', [(i, (i + by) % n_ctx) for i in range(n_ctx)])  8.64 us
    unnamed x16, local copies, waits for them, and re-layouts  5.79 us
  transfers between devices with their start and end apart: 27, of which 10 were waited for; matrix products, arithmetic and copies ran while one was open for 0% of the time, Pallas kernels for 20%

profile of v2, /device:TPU:0, one launch (start us, length us, event | category | flops | bytes accessed | tf_op | source)
XLA Modules:
  0.0 89.8 jit_solution(16003129912365058911)
XLA Ops:
  0.6 3.1 %collective-permute-start.1 = (bf16[128,1024]{1,0:T(8,128)(2,1)}, bf16[128,1024]{1,0:T(8,128)(2,1)S(1)}, u32[]{:S(2)}, u32[]{:S(2)}) collective-permute-start(bf16[128,1024]{1,0:T(8,128)(2,1)} %bitcast.8), channel_id=1, source_target_pairs={{0,16},{16,0},{1,17},{17,1},{2,18},{18,2},{3,19},{19,3},{4,20},{20... | collective-permute-start | bytes 786440 | tf_op jit(solution)/shard_map/ppermute | solution.py:262
  3.7 0.1 collective-permute-start.3
  3.8 1.9 %collective-permute-start = (bf16[128,1024]{1,0:T(8,128)(2,1)}, bf16[128,1024]{1,0:T(8,128)(2,1)S(1)}, u32[]{:S(2)}, u32[]{:S(2)}) collective-permute-start(bf16[128,1024]{1,0:T(8,128)(2,1)} %bitcast.12), channel_id=1, source_target_pairs={{0,16},{16,0},{1,17},{17,1},{2,18},{18,2},{3,19},{19,3},{4,20},{20... | collective-permute-start | bytes 786440 | tf_op jit(solution)/shard_map/ppermute | solution.py:262
  5.7 0.1 collective-permute-start.4
  5.8 0.9 %copy-done = bf16[1,128,1024]{2,1,0:T(8,128)(2,1)S(1)} copy-done((bf16[1,128,1024]{2,1,0:T(8,128)(2,1)S(1)}, bf16[1,128,1024]{2,1,0:T(8,128)(2,1)}, u32[]{:S(2)}) %copy-start) | copy-done | bytes 262168
  6.8 0.9 %copy-done.1 = bf16[1,128,1024]{2,1,0:T(8,128)(2,1)S(1)} copy-done((bf16[1,128,1024]{2,1,0:T(8,128)(2,1)S(1)}, bf16[1,128,1024]{2,1,0:T(8,128)(2,1)}, u32[]{:S(2)}) %copy-start.1) | copy-done | bytes 262168
  7.7 0.9 %copy-done.2 = bf16[1,128,1024]{2,1,0:T(8,128)(2,1)S(1)} copy-done((bf16[1,128,1024]{2,1,0:T(8,128)(2,1)S(1)}, bf16[1,128,1024]{2,1,0:T(8,128)(2,1)}, u32[]{:S(2)}) %copy-start.2) | copy-done | bytes 262168
  8.7 0.9 %copy-done.3 = bf16[1,128,1024]{2,1,0:T(8,128)(2,1)S(1)} copy-done((bf16[1,128,1024]{2,1,0:T(8,128)(2,1)S(1)}, bf16[1,128,1024]{2,1,0:T(8,128)(2,1)}, u32[]{:S(2)}) %copy-start.3) | copy-done | bytes 262168
  9.6 0.7 copy-done.5
  10.3 0.7 copy-done.6
  10.9 0.1 shard_map.127
  11.0 2.0 %collective-permute-start.2 = (s32[1,128]{1,0:T(1,128)S(1)}, s32[1,128]{1,0:T(1,128)S(1)}, u32[]{:S(2)}, u32[]{:S(2)}) collective-permute-start(s32[1,128]{1,0:T(1,128)S(1)} %get-tuple-element.41.ido_ref), channel_id=1, source_target_pairs={{0,16},{16,0},{1,17},{17,1},{2,18},{18,2},{3,19},{19,3},{4,20},{20... | collective-permute-start | bytes 1544 | tf_op jit(solution)/shard_map/ppermute | solution.py:262
  13.1 14.1 %collective-permute-done.2.idx_ref = s32[1,128]{1,0:T(1,128)S(1)} collective-permute-done((s32[1,128]{1,0:T(1,128)S(1)}, s32[1,128]{1,0:T(1,128)S(1)}, u32[]{:S(2)}, u32[]{:S(2)}) %collective-permute-start.2) | collective-permute-done | bytes 544 | tf_op jit(solution)/shard_map/ppermute | solution.py:262
  27.2 0.7 copy-done.7
  27.8 4.7 %shard_map.128 = (f32[128,1024]{1,0:T(8,128)S(1)}, bf16[16,128,256]{2,1,0:T(8,128)(2,1)S(1)}) custom-call(f32[2,16]{1,0:T(2,128)S(1)} %copy-done.7, s32[1,128]{1,0:T(1,128)S(1)} %get-tuple-element.41.ido_ref, s32[1,128]{1,0:T(1,128)S(1)} %collective-permute-done.2.idx_ref, bf16[128,1024]{1,0:T(8,128)(2,1)S(1)} %get-tuple-element.39.q_ref.qo_ref, ...), custom_call_target="tpu_custom_call" | custom-call | flops 536870912 | bytes 4194304 | tf_op jit(solution)/shard_map/pallas_call | solution.py:243
  32.6 4.7 %shard_map.129 = (f32[128,1024]{1,0:T(8,128)S(1)}, bf16[16,128,128]{2,1,0:T(8,128)(2,1)S(1)}) custom-call(f32[2,16]{1,0:T(2,128)S(1)} %copy-done.7, s32[1,128]{1,0:T(1,128)S(1)} %get-tuple-element.41.ido_ref, s32[1,128]{1,0:T(1,128)S(1)} %collective-permute-done.2.idx_ref, bf16[128,1024]{1,0:T(8,128)(2,1)S(1)} %collective-permute-done.q_ref.qx_ref, ...), custom_call_target="tpu_custom_call" | custom-call | flops 536870912 | bytes 4194304 | tf_op jit(solution)/shard_map/pallas_call | solution.py:243
  37.4 0.5 shard_map.132
  37.9 0.1 collective-permute-start.20
  38.0 2.9 %collective-permute-start.5 = (bf16[64,1024]{1,0:T(8,128)(2,1)S(1)}, bf16[64,1024]{1,0:T(8,128)(2,1)S(1)}, u32[]{:S(2)}, u32[]{:S(2)}) collective-permute-start(bf16[64,1024]{1,0:T(8,128)(2,1)S(1)} %copy-done.4), channel_id=1, source_target_pairs={{0,8},{1,9},{2,10},{3,11},{4,12},{5,13},{6,14},{7,15},{8,0},{9,1},... | collective-permute-start | bytes 393224 | tf_op jit(solution)/shard_map/ppermute | solution.py:259
  40.8 1.6 %collective-permute-start.6 = (bf16[64,1024]{1,0:T(8,128)(2,1)S(1)}, bf16[64,1024]{1,0:T(8,128)(2,1)S(1)}, u32[]{:S(2)}, u32[]{:S(2)}) collective-permute-start(bf16[64,1024]{1,0:T(8,128)(2,1)S(1)} %copy-done.4), channel_id=1, source_target_pairs={{0,4},{1,5},{2,6},{3,7},{4,0},{5,1},{6,2},{7,3},{8,12},{9,13},{10,... | collective-permute-start | bytes 393224 | tf_op jit(solution)/shard_map/ppermute | solution.py:259
  42.4 1.5 %collective-permute-start.8 = (bf16[64,1024]{1,0:T(8,128)(2,1)S(1)}, bf16[64,1024]{1,0:T(8,128)(2,1)S(1)}, u32[]{:S(2)}, u32[]{:S(2)}) collective-permute-start(bf16[64,1024]{1,0:T(8,128)(2,1)S(1)} %copy-done.4), channel_id=1, source_target_pairs={{0,2},{1,3},{2,0},{3,1},{4,6},{5,7},{6,4},{7,5},{8,10},{9,11},{10,... | collective-permute-start | bytes 393224 | tf_op jit(solution)/shard_map/ppermute | solution.py:259
  43.9 3.9 %collective-permute-done.5.rest_1_ = bf16[64,1024]{1,0:T(8,128)(2,1)S(1)} collective-permute-done((bf16[64,1024]{1,0:T(8,128)(2,1)S(1)}, bf16[64,1024]{1,0:T(8,128)(2,1)S(1)}, u32[]{:S(2)}, u32[]{:S(2)}) %collective-permute-start.5) | collective-permute-done | bytes 131104 | tf_op jit(solution)/shard_map/ppermute | solution.py:259
  47.8 0.6 collective-permute-start.7
  48.5 1.5 %collective-permute-start.9 = (bf16[64,1024]{1,0:T(8,128)(2,1)S(1)}, bf16[64,1024]{1,0:T(8,128)(2,1)S(1)}, u32[]{:S(2)}, u32[]{:S(2)}) collective-permute-start(bf16[64,1024]{1,0:T(8,128)(2,1)S(1)} %collective-permute-done.5.rest_1_), channel_id=1, source_target_pairs={{0,2},{1,3},{2,0},{3,1},{4,6},{5,7},{6,4},{7,5},{8,10},{9,11},{10,... | collective-permute-start | bytes 393224 | tf_op jit(solution)/shard_map/ppermute | solution.py:259
  50.0 0.5 collective-permute-start.10
  50.5 2.4 %collective-permute-done.7.rest_3_ = bf16[64,1024]{1,0:T(8,128)(2,1)S(1)} collective-permute-done((bf16[64,1024]{1,0:T(8,128)(2,1)S(1)}, bf16[64,1024]{1,0:T(8,128)(2,1)S(1)}, u32[]{:S(2)}, u32[]{:S(2)}) %collective-permute-start.7) | collective-permute-done | bytes 131104 | tf_op jit(solution)/shard_map/ppermute | solution.py:259
  52.9 2.0 %collective-permute-done.9.rest_5_ = bf16[64,1024]{1,0:T(8,128)(2,1)S(1)} collective-permute-done((bf16[64,1024]{1,0:T(8,128)(2,1)S(1)}, bf16[64,1024]{1,0:T(8,128)(2,1)S(1)}, u32[]{:S(2)}, u32[]{:S(2)}) %collective-permute-start.9) | collective-permute-done | bytes 131104 | tf_op jit(solution)/shard_map/ppermute | solution.py:259
  54.8 1.5 %collective-permute-start.11 = (bf16[64,1024]{1,0:T(8,128)(2,1)S(1)}, bf16[64,1024]{1,0:T(8,128)(2,1)S(1)}, u32[]{:S(2)}, u32[]{:S(2)}) collective-permute-start(bf16[64,1024]{1,0:T(8,128)(2,1)S(1)} %collective-permute-done.7.rest_3_), channel_id=1, source_target_pairs={{0,2},{1,3},{2,0},{3,1},{4,6},{5,7},{6,4},{7,5},{8,10},{9,11},{10,... | collective-permute-start | bytes 393224 | tf_op jit(solution)/shard_map/ppermute | solution.py:259
  56.3 0.1 shard_map.133
  56.5 1.4 %collective-permute-start.21 = (bf16[256,512]{1,0:T(8,128)(2,1)S(1)}, bf16[256,512]{1,0:T(8,128)(2,1)S(1)}, u32[]{:S(2)}, u32[]{:S(2)}) collective-permute-start(bf16[256,512]{1,0:T(8,128)(2,1)S(1)} %get-tuple-element.59), channel_id=1, source_target_pairs={{0,2},{1,3},{2,0},{3,1},{4,6},{5,7},{6,4},{7,5},{8,10},{9,11},{10,... | collective-permute-start | bytes 786440 | tf_op jit(solution)/shard_map/ppermute | solution.py:259
  58.0 0.5 collective-permute-start.17
  58.5 0.1 collective-permute-start.18
  58.5 2.7 %collective-permute-done.11.rest_7_ = bf16[64,1024]{1,0:T(8,128)(2,1)S(1)} collective-permute-done((bf16[64,1024]{1,0:T(8,128)(2,1)S(1)}, bf16[64,1024]{1,0:T(8,128)(2,1)S(1)}, u32[]{:S(2)}, u32[]{:S(2)}) %collective-permute-start.11) | collective-permute-done | bytes 131104 | tf_op jit(solution)/shard_map/ppermute | solution.py:259
  61.2 1.3 %collective-permute-done.19.rest_15_ = bf16[64,1024]{1,0:T(8,128)(2,1)S(1)} collective-permute-done((bf16[64,1024]{1,0:T(8,128)(2,1)S(1)}, bf16[64,1024]{1,0:T(8,128)(2,1)S(1)}, u32[]{:S(2)}, u32[]{:S(2)}) %collective-permute-start.19) | collective-permute-done | bytes 131104 | tf_op jit(solution)/shard_map/ppermute | solution.py:259
  62.6 4.6 %shard_map.130 = (bf16[8,2,64,1024]{3,2,1,0:T(8,128)(2,1)S(1)}, bf16[256,1024]{1,0:T(8,128)(2,1)S(1)}, bf16[16,128,256]{2,1,0:T(8,128)(2,1)S(1)}, bf16[16,128,128]{2,1,0:T(8,128)(2,1)S(1)}, f32[1,128]{1,0:T(1,128)S(1)}) custom-call(s32[1,128]{1,0:T(1,128)S(1)} %get-tuple-element.41.ido_ref, s32[1,128]{1,0:T(1,128)S(1)} %collective-permute-done.2.idx_ref, ...), custom_call_target="tpu_custom_call" | custom-call | flops 1073741824 | bytes 4194304 | tf_op jit(solution)/shard_map/pallas_call | solution.py:243
  67.2 0.2 collective-permute-start.22
  67.3 1.0 %collective-permute-done.22.b_ref = f32[1,128]{1,0:T(1,128)S(1)} collective-permute-done((f32[1,128]{1,0:T(1,128)S(1)}, f32[1,128]{1,0:T(1,128)S(1)}, u32[]{:S(2)}, u32[]{:S(2)}) %collective-permute-start.22) | collective-permute-done | bytes 544 | tf_op jit(solution)/shard_map/ppermute | solution.py:259
  68.4 1.5 %collective-permute-start.23 = (f32[1,128]{1,0:T(1,128)S(1)}, f32[1,128]{1,0:T(1,128)S(1)}, u32[]{:S(2)}, u32[]{:S(2)}) collective-permute-start(f32[1,128]{1,0:T(1,128)S(1)} %shard_map.134.refs_0_), channel_id=1, source_target_pairs={{0,2},{1,3},{2,0},{3,1},{4,6},{5,7},{6,4},{7,5},{8,10},{9,11},{10,... | collective-permute-start | bytes 1544 | tf_op jit(solution)/shard_map/ppermute | solution.py:259
  69.8 2.1 %collective-permute-done.23.refs_1_ = f32[1,128]{1,0:T(1,128)S(1)} collective-permute-done((f32[1,128]{1,0:T(1,128)S(1)}, f32[1,128]{1,0:T(1,128)S(1)}, u32[]{:S(2)}, u32[]{:S(2)}) %collective-permute-start.23) | collective-permute-done | bytes 544 | tf_op jit(solution)/shard_map/ppermute | solution.py:259
  71.9 0.1 shard_map.135
  72.0 1.2 %collective-permute-start.24 = (bf16[144,512]{1,0:T(8,128)(2,1)S(1)}, bf16[144,512]{1,0:T(8,128)(2,1)S(1)}, u32[]{:S(2)}, u32[]{:S(2)}) collective-permute-start(bf16[144,512]{1,0:T(8,128)(2,1)S(1)} %get-tuple-element.62), channel_id=1, source_target_pairs={{0,4},{1,5},{2,6},{3,7},{4,0},{5,1},{6,2},{7,3},{8,12},{9,13},{10,... | collective-permute-start | bytes 442376 | tf_op jit(solution)/shard_map/ppermute | solution.py:259
  73.3 4.0 %collective-permute-done.24.got_ref = bf16[144,512]{1,0:T(8,128)(2,1)S(1)} collective-permute-done((bf16[144,512]{1,0:T(8,128)(2,1)S(1)}, bf16[144,512]{1,0:T(8,128)(2,1)S(1)}, u32[]{:S(2)}, u32[]{:S(2)}) %collective-permute-start.24) | collective-permute-done | bytes 147488 | tf_op jit(solution)/shard_map/ppermute | solution.py:259
  77.2 0.1 shard_map.136
  77.3 4.1 %collective-permute-start.25 = (bf16[80,512]{1,0:T(8,128)(2,1)S(1)}, bf16[80,512]{1,0:T(8,128)(2,1)S(1)}, u32[]{:S(2)}, u32[]{:S(2)}) collective-permute-start(bf16[80,512]{1,0:T(8,128)(2,1)S(1)} %get-tuple-element.65), channel_id=1, source_target_pairs={{0,8},{1,9},{2,10},{3,11},{4,12},{5,13},{6,14},{7,15},{8,0},{9,1},... | collective-permute-start | bytes 245768 | tf_op jit(solution)/shard_map/ppermute | solution.py:259
  81.4 2.8 %collective-permute-done.25.got_ref = bf16[80,512]{1,0:T(8,128)(2,1)S(1)} collective-permute-done((bf16[80,512]{1,0:T(8,128)(2,1)S(1)}, bf16[80,512]{1,0:T(8,128)(2,1)S(1)}, u32[]{:S(2)}, u32[]{:S(2)}) %collective-permute-start.25) | collective-permute-done | bytes 81952 | tf_op jit(solution)/shard_map/ppermute | solution.py:259
  84.2 1.5 %collective-permute-start.26 = (bf16[80,512]{1,0:T(8,128)(2,1)S(1)}, bf16[80,512]{1,0:T(8,128)(2,1)S(1)}, u32[]{:S(2)}, u32[]{:S(2)}) collective-permute-start(bf16[80,512]{1,0:T(8,128)(2,1)S(1)} %get-tuple-element.69), channel_id=1, source_target_pairs={{0,16},{16,0},{1,17},{17,1},{2,18},{18,2},{3,19},{19,3},{4,20},{20... | collective-permute-start | bytes 245768 | tf_op jit(solution)/shard_map/ppermute | solution.py:262
  85.7 3.3 %shard_map.131 = (bf16[128,1024]{1,0:T(8,128)(2,1)}, bf16[128,1024]{1,0:T(8,128)(2,1)}, bf16[128,1024]{1,0:T(8,128)(2,1)}, bf16[128,1024]{1,0:T(8,128)(2,1)}) custom-call(bf16[128,1024]{1,0:T(8,128)(2,1)S(1)} %get-tuple-element.39.q_ref.qo_ref, bf16[128,1024]{1,0:T(8,128)(2,1)S(1)} %collective-permute-done.q_ref.qx_ref, ...), custom_call_target="tpu_custom_call" | custom-call | flops 1073741824 | bytes 4194304 | tf_op jit(solution)/shard_map/pallas_call | solution.py:243
  89.0 0.8 shard_map.138
  (34 shorter events, 0.1 us)
Async XLA Ops:
  0.6 26.5 %collective-permute-start.1 = (bf16[128,1024]{1,0:T(8,128)(2,1)}, bf16[128,1024]{1,0:T(8,128)(2,1)S(1)}, u32[]{:S(2)}, u32[]{:S(2)}) collective-permute-start(bf16[128,1024]{1,0:T(8,128)(2,1)} %bitcast.8), channel_id=1, source_target_pairs={{0,16},{16,0},{1,17},{17,1},{2,18},{18,2},{3,19},{19,3},{4,20},{20... | collective-permute-start | bytes 786440 | tf_op jit(solution)/shard_map/ppermute | solution.py:262
  3.7 23.5 %collective-permute-start.3 = (bf16[128,1024]{1,0:T(8,128)(2,1)}, bf16[128,1024]{1,0:T(8,128)(2,1)S(1)}, u32[]{:S(2)}, u32[]{:S(2)}) collective-permute-start(bf16[128,1024]{1,0:T(8,128)(2,1)} %bitcast.10), channel_id=1, source_target_pairs={{0,16},{16,0},{1,17},{17,1},{2,18},{18,2},{3,19},{19,3},{4,20},{20... | collective-permute-start | bytes 786440 | tf_op jit(solution)/shard_map/ppermute | solution.py:262
  3.8 28.8 %collective-permute-start = (bf16[128,1024]{1,0:T(8,128)(2,1)}, bf16[128,1024]{1,0:T(8,128)(2,1)S(1)}, u32[]{:S(2)}, u32[]{:S(2)}) collective-permute-start(bf16[128,1024]{1,0:T(8,128)(2,1)} %bitcast.12), channel_id=1, source_target_pairs={{0,16},{16,0},{1,17},{17,1},{2,18},{18,2},{3,19},{19,3},{4,20},{20... | collective-permute-start | bytes 786440 | tf_op jit(solution)/shard_map/ppermute | solution.py:262
  5.7 31.6 %collective-permute-start.4 = (bf16[128,1024]{1,0:T(8,128)(2,1)}, bf16[128,1024]{1,0:T(8,128)(2,1)S(1)}, u32[]{:S(2)}, u32[]{:S(2)}) collective-permute-start(bf16[128,1024]{1,0:T(8,128)(2,1)} %bitcast.14), channel_id=1, source_target_pairs={{0,16},{16,0},{1,17},{17,1},{2,18},{18,2},{3,19},{19,3},{4,20},{20... | collective-permute-start | bytes 786440 | tf_op jit(solution)/shard_map/ppermute | solution.py:262
  5.8 0.9 %copy-start = (bf16[1,128,1024]{2,1,0:T(8,128)(2,1)S(1)}, bf16[1,128,1024]{2,1,0:T(8,128)(2,1)}, u32[]{:S(2)}) copy-start(bf16[1,128,1024]{2,1,0:T(8,128)(2,1)} %param.9) | copy-start | bytes 786436
  6.8 0.9 %copy-start.1 = (bf16[1,128,1024]{2,1,0:T(8,128)(2,1)S(1)}, bf16[1,128,1024]{2,1,0:T(8,128)(2,1)}, u32[]{:S(2)}) copy-start(bf16[1,128,1024]{2,1,0:T(8,128)(2,1)} %param.10) | copy-start | bytes 786436
  7.7 0.9 %copy-start.2 = (bf16[1,128,1024]{2,1,0:T(8,128)(2,1)S(1)}, bf16[1,128,1024]{2,1,0:T(8,128)(2,1)}, u32[]{:S(2)}) copy-start(bf16[1,128,1024]{2,1,0:T(8,128)(2,1)} %param.8) | copy-start | bytes 786436
  8.7 0.9 %copy-start.3 = (bf16[1,128,1024]{2,1,0:T(8,128)(2,1)S(1)}, bf16[1,128,1024]{2,1,0:T(8,128)(2,1)}, u32[]{:S(2)}) copy-start(bf16[1,128,1024]{2,1,0:T(8,128)(2,1)} %param.11) | copy-start | bytes 786436
  9.6 0.7 copy-start.5
  10.3 0.7 copy-start.6
  11.0 16.1 %collective-permute-start.2 = (s32[1,128]{1,0:T(1,128)S(1)}, s32[1,128]{1,0:T(1,128)S(1)}, u32[]{:S(2)}, u32[]{:S(2)}) collective-permute-start(s32[1,128]{1,0:T(1,128)S(1)} %get-tuple-element.41.ido_ref), channel_id=1, source_target_pairs={{0,16},{16,0},{1,17},{17,1},{2,18},{18,2},{3,19},{19,3},{4,20},{20... | collective-permute-start | bytes 1544 | tf_op jit(solution)/shard_map/ppermute | solution.py:262
  27.2 0.7 copy-start.7
  32.6 5.4 %copy-start.4 = (bf16[64,1024]{1,0:T(8,128)(2,1)S(1)}, bf16[64,1024]{1,0:T(8,128)(2,1)}, u32[]{:S(2)}) copy-start(bf16[64,1024]{1,0:T(8,128)(2,1)} %rest_0_.1) | copy-start | bytes 393220
  37.9 17.0 %collective-permute-start.20 = (bf16[512,512]{1,0:T(8,128)(2,1)S(1)}, bf16[512,512]{1,0:T(8,128)(2,1)S(1)}, u32[]{:S(2)}, u32[]{:S(2)}) collective-permute-start(bf16[512,512]{1,0:T(8,128)(2,1)S(1)} %get-tuple-element.57), channel_id=1, source_target_pairs={{0,1},{1,0},{2,3},{3,2},{4,5},{5,4},{6,7},{7,6},{8,9},{9,8},{10,11... | collective-permute-start | bytes 1572872 | tf_op jit(solution)/shard_map/ppermute | solution.py:259
  38.0 9.9 %collective-permute-start.5 = (bf16[64,1024]{1,0:T(8,128)(2,1)S(1)}, bf16[64,1024]{1,0:T(8,128)(2,1)S(1)}, u32[]{:S(2)}, u32[]{:S(2)}) collective-permute-start(bf16[64,1024]{1,0:T(8,128)(2,1)S(1)} %copy-done.4), channel_id=1, source_target_pairs={{0,8},{1,9},{2,10},{3,11},{4,12},{5,13},{6,14},{7,15},{8,0},{9,1},... | collective-permute-start | bytes 393224 | tf_op jit(solution)/shard_map/ppermute | solution.py:259
  40.8 7.6 %collective-permute-start.6 = (bf16[64,1024]{1,0:T(8,128)(2,1)S(1)}, bf16[64,1024]{1,0:T(8,128)(2,1)S(1)}, u32[]{:S(2)}, u32[]{:S(2)}) collective-permute-start(bf16[64,1024]{1,0:T(8,128)(2,1)S(1)} %copy-done.4), channel_id=1, source_target_pairs={{0,4},{1,5},{2,6},{3,7},{4,0},{5,1},{6,2},{7,3},{8,12},{9,13},{10,... | collective-permute-start | bytes 393224 | tf_op jit(solution)/shard_map/ppermute | solution.py:259
  42.4 7.6 %collective-permute-start.8 = (bf16[64,1024]{1,0:T(8,128)(2,1)S(1)}, bf16[64,1024]{1,0:T(8,128)(2,1)S(1)}, u32[]{:S(2)}, u32[]{:S(2)}) collective-permute-start(bf16[64,1024]{1,0:T(8,128)(2,1)S(1)} %copy-done.4), channel_id=1, source_target_pairs={{0,2},{1,3},{2,0},{3,1},{4,6},{5,7},{6,4},{7,5},{8,10},{9,11},{10,... | collective-permute-start | bytes 393224 | tf_op jit(solution)/shard_map/ppermute | solution.py:259
  43.9 6.6 %collective-permute-start.12 = (bf16[64,1024]{1,0:T(8,128)(2,1)S(1)}, bf16[64,1024]{1,0:T(8,128)(2,1)S(1)}, u32[]{:S(2)}, u32[]{:S(2)}) collective-permute-start(bf16[64,1024]{1,0:T(8,128)(2,1)S(1)} %copy-done.4), channel_id=1, source_target_pairs={{0,1},{1,0},{2,3},{3,2},{4,5},{5,4},{6,7},{7,6},{8,9},{9,8},{10,11... | collective-permute-start | bytes 393224 | tf_op jit(solution)/shard_map/ppermute | solution.py:259
  47.8 5.0 %collective-permute-start.7 = (bf16[64,1024]{1,0:T(8,128)(2,1)S(1)}, bf16[64,1024]{1,0:T(8,128)(2,1)S(1)}, u32[]{:S(2)}, u32[]{:S(2)}) collective-permute-start(bf16[64,1024]{1,0:T(8,128)(2,1)S(1)} %collective-permute-done.5.rest_1_), channel_id=1, source_target_pairs={{0,4},{1,5},{2,6},{3,7},{4,0},{5,1},{6,2},{7,3},{8,12},{9,13},{10,... | collective-permute-start | bytes 393224 | tf_op jit(solution)/shard_map/ppermute | solution.py:259
  48.5 6.4 %collective-permute-start.9 = (bf16[64,1024]{1,0:T(8,128)(2,1)S(1)}, bf16[64,1024]{1,0:T(8,128)(2,1)S(1)}, u32[]{:S(2)}, u32[]{:S(2)}) collective-permute-start(bf16[64,1024]{1,0:T(8,128)(2,1)S(1)} %collective-permute-done.5.rest_1_), channel_id=1, source_target_pairs={{0,2},{1,3},{2,0},{3,1},{4,6},{5,7},{6,4},{7,5},{8,10},{9,11},{10,... | collective-permute-start | bytes 393224 | tf_op jit(solution)/shard_map/ppermute | solution.py:259
  50.0 6.5 %collective-permute-start.10 = (bf16[64,1024]{1,0:T(8,128)(2,1)S(1)}, bf16[64,1024]{1,0:T(8,128)(2,1)S(1)}, u32[]{:S(2)}, u32[]{:S(2)}) collective-permute-start(bf16[64,1024]{1,0:T(8,128)(2,1)S(1)} %collective-permute-done.6.rest_2_), channel_id=1, source_target_pairs={{0,2},{1,3},{2,0},{3,1},{4,6},{5,7},{6,4},{7,5},{8,10},{9,11},{10,... | collective-permute-start | bytes 393224 | tf_op jit(solution)/shard_map/ppermute | solution.py:259
  50.5 7.4 %collective-permute-start.13 = (bf16[64,1024]{1,0:T(8,128)(2,1)S(1)}, bf16[64,1024]{1,0:T(8,128)(2,1)S(1)}, u32[]{:S(2)}, u32[]{:S(2)}) collective-permute-start(bf16[64,1024]{1,0:T(8,128)(2,1)S(1)} %collective-permute-done.5.rest_1_), channel_id=1, source_target_pairs={{0,1},{1,0},{2,3},{3,2},{4,5},{5,4},{6,7},{7,6},{8,9},{9,8},{10,11... | collective-permute-start | bytes 393224 | tf_op jit(solution)/shard_map/ppermute | solution.py:259
  52.9 5.1 %collective-permute-start.14 = (bf16[64,1024]{1,0:T(8,128)(2,1)S(1)}, bf16[64,1024]{1,0:T(8,128)(2,1)S(1)}, u32[]{:S(2)}, u32[]{:S(2)}) collective-permute-start(bf16[64,1024]{1,0:T(8,128)(2,1)S(1)} %collective-permute-done.6.rest_2_), channel_id=1, source_target_pairs={{0,1},{1,0},{2,3},{3,2},{4,5},{5,4},{6,7},{7,6},{8,9},{9,8},{10,11... | collective-permute-start | bytes 393224 | tf_op jit(solution)/shard_map/ppermute | solution.py:259
  54.8 3.6 %collective-permute-start.16 = (bf16[64,1024]{1,0:T(8,128)(2,1)S(1)}, bf16[64,1024]{1,0:T(8,128)(2,1)S(1)}, u32[]{:S(2)}, u32[]{:S(2)}) collective-permute-start(bf16[64,1024]{1,0:T(8,128)(2,1)S(1)} %collective-permute-done.8.rest_4_), channel_id=1, source_target_pairs={{0,1},{1,0},{2,3},{3,2},{4,5},{5,4},{6,7},{7,6},{8,9},{9,8},{10,11... | collective-permute-start | bytes 393224 | tf_op jit(solution)/shard_map/ppermute | solution.py:259
  54.8 6.4 %collective-permute-start.11 = (bf16[64,1024]{1,0:T(8,128)(2,1)S(1)}, bf16[64,1024]{1,0:T(8,128)(2,1)S(1)}, u32[]{:S(2)}, u32[]{:S(2)}) collective-permute-start(bf16[64,1024]{1,0:T(8,128)(2,1)S(1)} %collective-permute-done.7.rest_3_), channel_id=1, source_target_pairs={{0,2},{1,3},{2,0},{3,1},{4,6},{5,7},{6,4},{7,5},{8,10},{9,11},{10,... | collective-permute-start | bytes 393224 | tf_op jit(solution)/shard_map/ppermute | solution.py:259
  56.5 15.4 %collective-permute-start.21 = (bf16[256,512]{1,0:T(8,128)(2,1)S(1)}, bf16[256,512]{1,0:T(8,128)(2,1)S(1)}, u32[]{:S(2)}, u32[]{:S(2)}) collective-permute-start(bf16[256,512]{1,0:T(8,128)(2,1)S(1)} %get-tuple-element.59), channel_id=1, source_target_pairs={{0,2},{1,3},{2,0},{3,1},{4,6},{5,7},{6,4},{7,5},{8,10},{9,11},{10,... | collective-permute-start | bytes 786440 | tf_op jit(solution)/shard_map/ppermute | solution.py:259
  57.9 3.3 %collective-permute-start.15 = (bf16[64,1024]{1,0:T(8,128)(2,1)S(1)}, bf16[64,1024]{1,0:T(8,128)(2,1)S(1)}, u32[]{:S(2)}, u32[]{:S(2)}) collective-permute-start(bf16[64,1024]{1,0:T(8,128)(2,1)S(1)} %collective-permute-done.7.rest_3_), channel_id=1, source_target_pairs={{0,1},{1,0},{2,3},{3,2},{4,5},{5,4},{6,7},{7,6},{8,9},{9,8},{10,11... | collective-permute-start | bytes 393224 | tf_op jit(solution)/shard_map/ppermute | solution.py:259
  58.0 3.3 %collective-permute-start.17 = (bf16[64,1024]{1,0:T(8,128)(2,1)S(1)}, bf16[64,1024]{1,0:T(8,128)(2,1)S(1)}, u32[]{:S(2)}, u32[]{:S(2)}) collective-permute-start(bf16[64,1024]{1,0:T(8,128)(2,1)S(1)} %collective-permute-done.9.rest_5_), channel_id=1, source_target_pairs={{0,1},{1,0},{2,3},{3,2},{4,5},{5,4},{6,7},{7,6},{8,9},{9,8},{10,11... | collective-permute-start | bytes 393224 | tf_op jit(solution)/shard_map/ppermute | solution.py:259
  58.5 2.8 %collective-permute-start.18 = (bf16[64,1024]{1,0:T(8,128)(2,1)S(1)}, bf16[64,1024]{1,0:T(8,128)(2,1)S(1)}, u32[]{:S(2)}, u32[]{:S(2)}) collective-permute-start(bf16[64,1024]{1,0:T(8,128)(2,1)S(1)} %collective-permute-done.10.rest_6_), channel_id=1, source_target_pairs={{0,1},{1,0},{2,3},{3,2},{4,5},{5,4},{6,7},{7,6},{8,9},{9,8},{10,11... | collective-permute-start | bytes 393224 | tf_op jit(solution)/shard_map/ppermute | solution.py:259
  61.2 1.3 %collective-permute-start.19 = (bf16[64,1024]{1,0:T(8,128)(2,1)S(1)}, bf16[64,1024]{1,0:T(8,128)(2,1)S(1)}, u32[]{:S(2)}, u32[]{:S(2)}) collective-permute-start(bf16[64,1024]{1,0:T(8,128)(2,1)S(1)} %collective-permute-done.11.rest_7_), channel_id=1, source_target_pairs={{0,1},{1,0},{2,3},{3,2},{4,5},{5,4},{6,7},{7,6},{8,9},{9,8},{10,11... | collective-permute-start | bytes 393224 | tf_op jit(solution)/shard_map/ppermute | solution.py:259
  67.2 1.2 %collective-permute-start.22 = (f32[1,128]{1,0:T(1,128)S(1)}, f32[1,128]{1,0:T(1,128)S(1)}, u32[]{:S(2)}, u32[]{:S(2)}) collective-permute-start(f32[1,128]{1,0:T(1,128)S(1)} %get-tuple-element.60.a_ref), channel_id=1, source_target_pairs={{0,1},{1,0},{2,3},{3,2},{4,5},{5,4},{6,7},{7,6},{8,9},{9,8},{10,11... | collective-permute-start | bytes 1544 | tf_op jit(solution)/shard_map/ppermute | solution.py:259
  68.4 3.6 %collective-permute-start.23 = (f32[1,128]{1,0:T(1,128)S(1)}, f32[1,128]{1,0:T(1,128)S(1)}, u32[]{:S(2)}, u32[]{:S(2)}) collective-permute-start(f32[1,128]{1,0:T(1,128)S(1)} %shard_map.134.refs_0_), channel_id=1, source_target_pairs={{0,2},{1,3},{2,0},{3,1},{4,6},{5,7},{6,4},{7,5},{8,10},{9,11},{10,... | collective-permute-start | bytes 1544 | tf_op jit(solution)/shard_map/ppermute | solution.py:259
  72.0 5.2 %collective-permute-start.24 = (bf16[144,512]{1,0:T(8,128)(2,1)S(1)}, bf16[144,512]{1,0:T(8,128)(2,1)S(1)}, u32[]{:S(2)}, u32[]{:S(2)}) collective-permute-start(bf16[144,512]{1,0:T(8,128)(2,1)S(1)} %get-tuple-element.62), channel_id=1, source_target_pairs={{0,4},{1,5},{2,6},{3,7},{4,0},{5,1},{6,2},{7,3},{8,12},{9,13},{10,... | collective-permute-start | bytes 442376 | tf_op jit(solution)/shard_map/ppermute | solution.py:259
  77.3 6.9 %collective-permute-start.25 = (bf16[80,512]{1,0:T(8,128)(2,1)S(1)}, bf16[80,512]{1,0:T(8,128)(2,1)S(1)}, u32[]{:S(2)}, u32[]{:S(2)}) collective-permute-start(bf16[80,512]{1,0:T(8,128)(2,1)S(1)} %get-tuple-element.65), channel_id=1, source_target_pairs={{0,8},{1,9},{2,10},{3,11},{4,12},{5,13},{6,14},{7,15},{8,0},{9,1},... | collective-permute-start | bytes 245768 | tf_op jit(solution)/shard_map/ppermute | solution.py:259
  84.2 4.8 %collective-permute-start.26 = (bf16[80,512]{1,0:T(8,128)(2,1)S(1)}, bf16[80,512]{1,0:T(8,128)(2,1)S(1)}, u32[]{:S(2)}, u32[]{:S(2)}) collective-permute-start(bf16[80,512]{1,0:T(8,128)(2,1)S(1)} %get-tuple-element.69), channel_id=1, source_target_pairs={{0,16},{16,0},{1,17},{17,1},{2,18},{18,2},{3,19},{19,3},{4,20},{20... | collective-permute-start | bytes 245768 | tf_op jit(solution)/shard_map/ppermute | solution.py:262

commit v3 on v2

v3 whole, which is shorter than its diff:
```python
import functools

import jax
import jax.numpy as jnp
from jax import lax
from jax.experimental import pallas as pl
from jax.experimental.pallas import tpu as pltpu
from jax.sharding import PartitionSpec as P


HEADS = 16
HEAD_DIM = 64
PAIR = 2 * HEAD_DIM
SCALE = HEAD_DIM ** -0.5
NEG = -1e30
TAIL = 16
BF = jnp.bfloat16
F32 = jnp.float32


def dot_nt(a, b):
    return lax.dot_general(a, b, (((1,), (1,)), ((), ())), preferred_element_type=F32)


def dot_tn(a, b):
    return lax.dot_general(a, b, (((0,), (0,)), ((), ())), preferred_element_type=F32)


def dot_nn(a, b):
    return lax.dot_general(a, b, (((1,), (0,)), ((), ())), preferred_element_type=F32)


def columns(row):
    return jnp.transpose(jnp.broadcast_to(row, (128, row.shape[1])))[:, :1]


def low_bit(bit):
    return (lax.axis_index("dp") // bit) % 2 == 0


def prepare_kernel(bias_ref, series_ref, variate_ref, d_ref, q_ref, k_ref, v_ref, code_ref, gap_ref, d_out,
                   qv_out, k_out, *refs):
    cuts, (bias_buf, ids_ref, sem) = refs[:-3], refs[-3:]
    tok = d_ref.shape[0]
    moves = [(bias_ref, bias_buf), (series_ref, ids_ref.at[0]), (variate_ref, ids_ref.at[1]), (d_ref, d_out),
             (q_ref, qv_out.at[:tok]), (v_ref, qv_out.at[tok:]), (k_ref, k_out)]
    copies = [pltpu.make_async_copy(source, target, sem.at[i]) for i, (source, target) in enumerate(moves)]
    for copy in copies:
        copy.start()
    for copy in copies:
        copy.wait()
    code_ref[...] = ids_ref[0] * 256 + ids_ref[1]
    gap = jnp.broadcast_to(bias_buf[0:1, :] - bias_buf[1:2, :], (128, HEADS))
    gap = jnp.concatenate([gap, jnp.zeros((128, 128 - HEADS), F32)], axis=1)
    gap_ref[...] = jnp.transpose(gap)[:HEADS]
    n, me, cols = lax.axis_size("ctx"), lax.axis_index("ctx"), cuts[0].shape[1]
    for by, ref in enumerate(cuts, 1):
        ref[...] = d_out[:, pl.ds(pl.multiple_of(((me + by) % n) * cols, 128), cols)]


def heads_at_once(tokens):
    return HEADS if tokens <= 512 else 4


def each_group(tokens, body):
    group = heads_at_once(tokens)
    lanes = group * HEAD_DIM
    if group == HEADS:
        body(0, slice(0, lanes))
        return

    def step(index, carry):
        body(index, pl.ds(pl.multiple_of(index * lanes, lanes), lanes))
        return carry

    lax.fori_loop(0, HEADS // group, step, 0)


def low_lanes(rows):
    return lax.broadcasted_iota(jnp.int32, (rows, PAIR), 1) < HEAD_DIM


def stacked(pair):
    low, zero = low_lanes(pair.shape[0]), jnp.zeros_like(pair)
    return jnp.concatenate([jnp.where(low, pair, zero), jnp.where(low, zero, pair)], axis=0)


def unstacked(rows):
    half = rows.shape[0] // 2
    return jnp.where(low_lanes(half), rows[:half], rows[half:])


def equal_ids(own_ref, oth_ref, count, shift):
    row = (jnp.concatenate([own_ref[...], oth_ref[...]], axis=1) >> shift) & 255
    return row == columns(row)[:count]


def forward_kernel(gap_ref, ido_ref, idx_ref, qvo_ref, qvx_ref, ko_ref, kx_ref,
                   co_ref, cx_ref, wo_ref, wx_ref, neg_ref, same_ref):
    tok, rest = co_ref.shape[0], cx_ref.shape[0]
    heads = heads_at_once(tok + rest)
    neg_ref[...] = jnp.where(equal_ids(ido_ref, idx_ref, tok + rest, 8), 0.0, NEG)
    same_ref[...] = jnp.where(equal_ids(ido_ref, idx_ref, tok + rest, 0), 1.0, 0.0)

    def body(group, at):
        k = jnp.concatenate([ko_ref[:, at], kx_ref[:, at]], axis=0)
        v = jnp.concatenate([qvo_ref[tok:, at], qvx_ref[rest:, at]], axis=0)
        for chunk in range((tok + rest) // tok):
            rows = slice(chunk * tok, (chunk + 1) * tok)
            place = slice((chunk - 1) * tok, chunk * tok)
            q = (qvx_ref[place, at] if chunk else qvo_ref[:tok, at]) * jnp.asarray(SCALE, BF)
            found = []
            for pair in range(heads // 2):
                lanes = slice(pair * PAIR, (pair + 1) * PAIR)
                s = dot_nt(stacked(q[:, lanes]), k[:, lanes])
                both_w = []
                for half in range(2):
                    head = heads * group + 2 * pair + half
                    gap = gap_ref[pl.ds(head, 1), :1]
                    sh = s[half * tok:(half + 1) * tok] + (same_ref[rows, :] * gap + neg_ref[rows, :])
                    e = jnp.exp(sh - jnp.max(sh, axis=1, keepdims=True))
                    w = (e * (1.0 / jnp.sum(e, axis=1, keepdims=True))).astype(BF)
                    if chunk:
                        wx_ref[head, place, :] = w[:, :tok]
                    else:
                        wo_ref[head] = w
                    both_w.append(w)
                found.append(unstacked(dot_nn(jnp.concatenate(both_w, axis=0), v[:, lanes])))
            if chunk:
                cx_ref[place, at] = jnp.concatenate(found, axis=1)
            else:
                co_ref[:, at] = jnp.concatenate(found, axis=1)

    each_group(tok + rest, body)


def split(summed, bit, keep_ref, send_ref, low=1):
    n, block, cols = keep_ref.shape
    mine = low_bit(bit)
    summed = summed.reshape(n // low, 2, low, block, cols)
    keep = jnp.where(mine, summed[:, 0], summed[:, 1])
    send = jnp.where(mine, summed[:, 1], summed[:, 0])
    keep_ref[...] = keep.reshape(n, block, cols)
    write_blocks(send.reshape(n * block, cols), send_ref)


def write_blocks(rows, send_ref):
    count, lanes = rows.shape[0], send_ref.shape[1]
    for part in range(rows.shape[1] // lanes):
        send_ref[part * count:(part + 1) * count, :] = rows[:, part * lanes:(part + 1) * lanes].astype(BF)


def read_blocks(got_ref, count, cols):
    lanes = got_ref.shape[1]
    parts = [got_ref[part * count:(part + 1) * count, :].astype(F32) for part in range(cols // lanes)]
    return jnp.concatenate(parts, axis=1)


def weight_kernel(co_ref, cx_ref, do_ref, dx_ref, keep_ref, send_ref):
    n, _, cols = keep_ref.shape
    cut = pl.ds(pl.multiple_of(lax.axis_index("ctx") * cols, 128), cols)
    d = jnp.concatenate([do_ref[:, cut], dx_ref[...]], axis=0)
    half = co_ref.shape[1] // 2
    for part in range(2):
        at = slice(part * half, (part + 1) * half)
        c = jnp.concatenate([co_ref[:, at], cx_ref[:, at]], axis=0).astype(BF)
        split(dot_tn(c, d), 1, keep_ref.at[part * n // 2:(part + 1) * n // 2],
              send_ref.at[part * half // 2:(part + 1) * half // 2])


def pack_tail(sums, send_ref):
    high = sums.astype(BF)
    low = (sums - high.astype(F32)).astype(BF)
    place = lax.broadcasted_iota(jnp.int32, (TAIL, 128), 0)
    tail = jnp.where(place == 0, high.astype(F32), jnp.where(place == 1, low.astype(F32), 0.0))
    send_ref[send_ref.shape[0] - TAIL:, :] = tail.astype(BF)


def unpack_tail(got_ref):
    tail = got_ref[got_ref.shape[0] - TAIL:, :].astype(F32)
    return tail[0:1] + tail[1:2]


def halve_kernel(bit, low, keep_ref, got_ref, *refs):
    n, block, cols = keep_ref.shape
    summed = keep_ref[...] + got_ref[...].astype(F32).reshape(n, block, cols)
    if len(refs) == 2:
        split(summed, bit, *refs, low=low)
        return
    sums_ref, extra_ref, keep_out, send_ref, keep_send_ref, sums_out = refs
    split(summed, bit, keep_out, send_ref)
    write_blocks(keep_out[0], keep_send_ref)
    sums = sums_ref[...] + extra_ref[...]
    sums_out[...] = sums
    pack_tail(sums, send_ref)
    pack_tail(sums, keep_send_ref)


def add_kernel(a_ref, b_ref, out_ref):
    out_ref[...] = a_ref[...] + b_ref[...]


def final_kernel(keep_ref, sums_ref, got_ref, *refs):
    got, (w_ref, bias_ref) = refs[:-2], refs[-2:]
    _, block, cols = keep_ref.shape
    n, me = lax.axis_size("ctx"), lax.axis_index("ctx")
    sums = sums_ref[...] + unpack_tail(got_ref)
    w_ref[:, pl.ds(pl.multiple_of(me * cols, 128), cols)] = keep_ref[0] + read_blocks(got_ref, block, cols)
    for by, (ref, more_ref) in enumerate(zip(got[::2], got[1::2]), 1):
        sums = sums + (unpack_tail(ref) + unpack_tail(more_ref))
        at = pl.multiple_of(((me + n - by) % n) * cols, 128)
        w_ref[:, pl.ds(at, cols)] = read_blocks(ref, block, cols) + read_blocks(more_ref, block, cols)
    same, total = sums[:, :HEADS], sums[:, HEADS:2 * HEADS]
    bias_ref[0:1, :] = same
    bias_ref[1:2, :] = total - same


def score_grad_kernel(pieces, parts, ido_ref, idx_ref, qvo_ref, qvx_ref, co_ref, cx_ref, wo_ref, wx_ref,
                      do_ref, *rest):
    dx_refs, piece_refs = rest[:parts], rest[parts:parts + len(pieces)]
    wfull_ref, dc_ref, so_ref, sx_ref, sums_ref, same_ref, dall_ref, rows_ref = rest[parts + len(pieces):]
    tok, rest_rows = qvo_ref.shape[0] // 2, qvx_ref.shape[0] // 2
    heads = heads_at_once(tok + rest_rows)
    nb = heads * HEAD_DIM // (2 * wfull_ref.shape[2])
    same_ref[...] = jnp.where(equal_ids(ido_ref, idx_ref, tok, 0), 1.0, 0.0)
    dall_ref[:tok, :] = do_ref[...]
    if parts == 1:
        dall_ref[tok:, :] = dx_refs[0][...]
    else:
        me, cols = lax.axis_index("ctx"), dx_refs[0].shape[1]
        for ref, at in zip(dx_refs, (me, 1 - me)):
            dall_ref[tok:, pl.ds(pl.multiple_of(at * cols, 128), cols)] = ref[...]
    for piece, ref in zip(pieces, piece_refs):
        index = jnp.bitwise_xor(lax.axis_index("dp"), piece)
        wfull_ref[index // 2, index % 2] = ref[...]

    def body(group, at):
        w = wfull_ref[pl.ds(group * nb, nb)].reshape(heads * HEAD_DIM, wfull_ref.shape[3])
        d = dot_nt(dall_ref[...], w).astype(BF)
        dc_ref[:, at] = d
        prod = d.astype(F32) * jnp.concatenate([co_ref[:, at], cx_ref[:, at]], axis=0)
        v = jnp.concatenate([qvo_ref[tok:, at], qvx_ref[rest_rows:, at]], axis=0)
        same = same_ref[...]
        for pair in range(heads // 2):
            lanes = slice(pair * PAIR, (pair + 1) * PAIR)
            dp, vp = d[:, lanes], v[:, lanes]
            delta = jnp.sum(stacked(prod[:, lanes]), axis=1, keepdims=True)
            total = dp.shape[0]
            own = dot_nt(stacked(dp[:tok]), vp)
            oth = dot_nt(stacked(dp[tok:]), vp[:tok])
            for half in range(2):
                head = heads * group + 2 * pair + half
                dh = delta[half * total:(half + 1) * total]
                ds = wo_ref[head].astype(F32) * (own[half * tok:(half + 1) * tok] - dh[:tok])
                rows_ref[pl.ds(head, 1), :] = jnp.sum(ds * same, axis=0, keepdims=True)
                rows_ref[pl.ds(HEADS + head, 1), :] = jnp.sum(ds, axis=0, keepdims=True)
                so_ref[head] = ds.astype(BF)
                down = oth[half * rest_rows:(half + 1) * rest_rows]
                sx_ref[head] = (wx_ref[head].astype(F32) * (down - dh[tok:])).astype(BF)

    each_group(tok + rest_rows, body)
    col = jnp.sum(rows_ref[...], axis=1, keepdims=True)
    col = jnp.concatenate([col, jnp.zeros((128 - 2 * HEADS, 1), F32)], axis=0)
    sums_ref[...] = jnp.transpose(jnp.broadcast_to(col, (128, 128)))[:1]


def input_grad_kernel(qvo_ref, qvx_ref, ko_ref, kx_ref, co_ref, dc_ref, wo_ref, wx_ref, so_ref, sx_ref,
                      wfull_ref, mixed_ref, qg_ref, kg_ref, vg_ref, acc_ref):
    tok, rest_rows = qvo_ref.shape[0] // 2, qvx_ref.shape[0] // 2
    heads = heads_at_once(tok + rest_rows)
    nb = heads * HEAD_DIM // (2 * wfull_ref.shape[2])
    acc_ref[...] = jnp.zeros_like(acc_ref)

    def side_by_side(own_ref, oth_ref, head):
        return jnp.concatenate(
            [jnp.concatenate([own_ref[h, :, :tok], oth_ref[h]], axis=0) for h in (head, head + 1)], axis=1)

    def body(group, at):
        w = wfull_ref[pl.ds(group * nb, nb)].reshape(heads * HEAD_DIM, wfull_ref.shape[3])
        acc_ref[...] += dot_nn(co_ref[:, at].astype(BF), w)
        q = jnp.concatenate([qvo_ref[:tok, at], qvx_ref[:rest_rows, at]], axis=0) * jnp.asarray(SCALE, BF)
        k = jnp.concatenate([ko_ref[:, at], kx_ref[:, at]], axis=0)
        d = dc_ref[:, at]
        found = []
        for pair in range(heads // 2):
            lanes = slice(pair * PAIR, (pair + 1) * PAIR)
            head = heads * group + 2 * pair
            so = jnp.concatenate([so_ref[head], so_ref[head + 1]], axis=0)
            found.append((unstacked(dot_nn(so, k[:, lanes])) * SCALE,
                          unstacked(dot_tn(side_by_side(so_ref, sx_ref, head), q[:, lanes])),
                          unstacked(dot_tn(side_by_side(wo_ref, wx_ref, head), d[:, lanes]))))
        for ref, parts in zip((qg_ref, kg_ref, vg_ref), zip(*found)):
            ref[:, at] = jnp.concatenate(parts, axis=1).astype(BF)

    each_group(tok + rest_rows, body)
    mixed_ref[...] = acc_ref[...].astype(BF)


def shape(dims, dtype):
    return jax.ShapeDtypeStruct(dims, dtype)


def cost(flops):
    return pl.CostEstimate(flops=flops, bytes_accessed=4 << 20, transcendentals=0)


def plain(kernel, args, outs, flops=1 << 22, scratch=(), in_specs=None, limit=8 << 20):
    spec = pl.BlockSpec(memory_space=pltpu.VMEM)
    return pl.pallas_call(
        kernel, in_specs=in_specs or [spec] * len(args), out_specs=[spec] * len(outs), out_shape=outs,
        scratch_shapes=scratch, compiler_params=pltpu.CompilerParams(vmem_limit_bytes=limit),
        cost_estimate=cost(flops))(*args)


def on_device(queries, keys, values, d_mixed, series_ids, variate_ids, variate_bias, w_out):
    query, key_rows, value_rows, upstream = queries[0], keys[0], values[0], d_mixed[0]
    tok, width = query.shape
    n_ctx, n_dp = lax.axis_size("ctx"), lax.axis_size("dp")
    total, cols, block = tok * n_ctx, width // n_ctx, width // n_dp
    rest = total - tok
    bits = [1 << i for i in range(n_dp.bit_length() - 1)]
    assert 1 << len(bits) == n_dp and len(bits) > 3 and n_ctx > 1

    def swap(array, bit):
        return lax.ppermute(array, "dp", [(i, i ^ bit) for i in range(n_dp)])

    def turns(array):
        return [lax.ppermute(array, "ctx", [(i, (i + by) % n_ctx) for i in range(n_ctx)])
                for by in range(1, n_ctx)]

    def others(array, axis):
        parts = turns(array)
        return parts[0] if len(parts) == 1 else jnp.concatenate(parts, axis=axis)

    hbm = pl.BlockSpec(memory_space=pltpu.HBM)
    limit = (12 << 20) + 40 * total * width
    kx = others(key_rows, 0)
    local = [variate_bias, series_ids, variate_ids, upstream, query, key_rows, value_rows]
    cut = shape((tok, cols), BF)
    code, gaps, upstream, qv, key_rows, *cuts = plain(
        prepare_kernel, [pltpu.with_memory_space_constraint(a, pltpu.HBM) for a in local],
        [shape(series_ids.shape, jnp.int32), shape((HEADS, 128), F32), shape((tok, width), BF),
         shape((2 * tok, width), BF), shape((tok, width), BF)] + [cut] * n_ctx,
        scratch=[pltpu.VMEM((2, HEADS), F32), pltpu.VMEM((2, 1, tok), jnp.int32), pltpu.SemaphoreType.DMA((len(local),))],
        in_specs=[hbm] * len(local))
    code_x = others(code, 1)
    parts = turns(qv)
    qvx = parts[0] if n_ctx == 2 else jnp.concatenate([p[:tok] for p in parts] + [p[tok:] for p in parts])
    near = [lax.ppermute(part, "ctx", [(i, (i + by) % n_ctx) for i in range(n_ctx)])
            for by, part in enumerate(cuts[:-1], 1)]
    near = near[0] if len(near) == 1 else jnp.concatenate(near, axis=0)
    dx = [near, *turns(cuts[-1])] if n_ctx == 2 else [others(upstream, 0)]

    pieces = {0: w_out}
    for bit in reversed(bits):
        for piece in list(pieces):
            pieces[piece ^ bit] = swap(pieces[piece], bit)
    order = list(pieces)

    o_shape, x_shape = shape((HEADS, tok, total), BF), shape((HEADS, rest, tok), BF)

    ctx_o, ctx_x, w_o, w_x = plain(
        forward_kernel, [gaps, code, code_x, qv, qvx, key_rows, kx],
        [shape((tok, width), F32), shape((rest, width), F32), o_shape, x_shape],
        16 * HEADS * total * total * HEAD_DIM, [pltpu.VMEM((total, total), F32)] * 2, limit=limit)
    keep, send = plain(weight_kernel, [ctx_o, ctx_x, upstream, near],
                       [shape((n_dp // 2, block, cols), F32), shape((width // 2, cols), BF)],
                       2 * total * width * cols, limit=limit)
    w_full, d_ctx, s_o, s_x, sums = plain(
        functools.partial(score_grad_kernel, order, len(dx)),
        [code, code_x, qv, qvx, ctx_o, ctx_x, w_o, w_x, upstream, *dx, *[pieces[p] for p in order]],
        [shape((n_dp // 2, 2, block, width), BF), shape((total, width), BF), o_shape, x_shape,
         shape((1, 128), F32)], 16 * HEADS * total * total * HEAD_DIM,
        [pltpu.VMEM((tok, total), F32), pltpu.VMEM((total, width), BF), pltpu.VMEM((2 * HEADS, total), F32)],
        limit=limit)

    bits = bits[:2] + bits[:1:-1]
    for bit in bits[:-1]:
        got = swap(sums, bit)
        if bit != bits[-2]:
            sums, = plain(add_kernel, [sums, got], [shape((1, 128), F32)])
    for bit, after in zip(bits, bits[1:]):
        n = keep.shape[0] // 2
        args, outs = [keep, swap(send, bit)], [shape((n, block, cols), F32)]
        if n > 1:
            outs.append(shape((n * block, cols), BF))
        else:
            args += [sums, got]
            outs += [shape((block * cols // 128 + TAIL, 128), BF)] * 2 + [shape((1, 128), F32)]
        keep, send, *last = plain(functools.partial(halve_kernel, after, n if after in bits[2:] else 1), args, outs)
    keep_send, sums = last
    args = [keep, sums, swap(send, bits[-1])]
    for by, part in enumerate(turns(keep_send), 1):
        route = [(c * n_dp + d, (c + by) % n_ctx * n_dp + (d ^ bits[-1])) for c in range(n_ctx) for d in range(n_dp)]
        args += [part, lax.ppermute(send, ("ctx", "dp"), route)]
    w_grad, bias_grad = plain(final_kernel, args, [shape((block, width), F32), shape((2, HEADS), F32)])
    mixed, q_grad, k_grad, v_grad = plain(
        input_grad_kernel, [qv, qvx, key_rows, kx, ctx_o, d_ctx, w_o, w_x, s_o, s_x, w_full],
        [shape((tok, width), BF)] * 4, 16 * HEADS * total * total * HEAD_DIM,
        [pltpu.VMEM((tok, width), F32)], limit=limit)
    return mixed[None], q_grad[None], k_grad[None], v_grad[None], w_grad, bias_grad


def solution(mesh):
    data = P("dp", "ctx", None)

    return jax.shard_map(
        on_device,
        mesh=mesh,
        in_specs=(data, data, data, data, P("dp", "ctx"), P("dp", "ctx"), P(), P("dp", None)),
        out_specs=(data, data, data, data, P("dp", None), P()),
        check_vma=False,
    )
```

time: 90 us -> 79.3 us (0.88)
  Pallas kernels: 19.1 us -> 9.59 us
  local copies, waits for them, and re-layouts: 5.79 us -> 0.01 us
  waiting for transfers between devices: 36.2 us -> 40 us
  starting transfers between devices: 27.9 us -> 28.8 us
    pallas_call x12 -> x11, Pallas kernels: 19.1 us -> 9.59 us  [plain(): pl.pallas_call(kernel, in_specs=in_specs or [spec] * len(args), out_specs...]
    unnamed x16 -> x2, local copies, waits for them, and re-layouts: 5.79 us -> 0.01 us
    ppermute x6 -> x5, waiting for transfers between devices: 14.1 us -> 18.9 us  [turns(): lax.ppermute(array, 'ctx', [(i, (i + by) % n_ctx) for i in range(n_ctx)])]
    ppermute x0 -> x2, starting transfers between devices: none -> 3.63 us  [the longest x1 1.95 us: on_device(): lax.ppermute(part, 'ctx', [(i, (i + by) % n_ctx) for i in range(n_ctx)])]
    ppermute x6 -> x5, starting transfers between devices: 8.64 us -> 6.54 us  [turns(): lax.ppermute(array, 'ctx', [(i, (i + by) % n_ctx) for i in range(n_ctx)])]
    ppermute x21 -> x22, waiting for transfers between devices: 22.1 us -> 21.1 us  [swap(): return lax.ppermute(array, 'dp', [(i, i ^ bit) for i in range(n_dp)])]
    ppermute x21 -> x22, starting transfers between devices: 19.2 us -> 18.6 us  [swap(): return lax.ppermute(array, 'dp', [(i, i ^ bit) for i in range(n_dp)])]
  transfers between devices with their start and end apart: 27 -> 29, of which waited for: 10 -> 10; matrix products, arithmetic and copies ran while one was open for 0% -> 0% of each run, Pallas kernels for 20% -> 9%
where the time goes in v3:
time: 79.3 us; the launch traced here: 79.2 us
  waiting for transfers between devices  40 us (50%)
  starting transfers between devices  28.8 us (36%)
  Pallas kernels  9.59 us (12%)
    ppermute x22, waiting for transfers between devices, swap(): return lax.ppermute(array, 'dp', [(i, i ^ bit) for i in range(n_dp)])  21.1 us
    ppermute x5, waiting for transfers between devices, turns(): lax.ppermute(array, 'ctx', [(i, (i + by) % n_ctx) for i in range(n_ctx)])  18.9 us
    ppermute x22, starting transfers between devices, swap(): return lax.ppermute(array, 'dp', [(i, i ^ bit) for i in range(n_dp)])  18.6 us
    pallas_call x11, Pallas kernels, plain(): pl.pallas_call(kernel, in_specs=in_specs or [spec] * len(args), out_specs...  9.59 us
    ppermute x5, starting transfers between devices, turns(): lax.ppermute(array, 'ctx', [(i, (i + by) % n_ctx) for i in range(n_ctx)])  6.54 us
    ppermute x1, starting transfers between devices, on_device(): lax.ppermute(part, 'ctx', [(i, (i + by) % n_ctx) for i in range(n_ctx)])  1.95 us
    ppermute x1, starting transfers between devices, on_device(): args += [part, lax.ppermute(send, ('ctx', 'dp'), route)]  1.68 us
  transfers between devices with their start and end apart: 29, of which 10 were waited for; matrix products, arithmetic and copies ran while one was open for 0% of the time, Pallas kernels for 9%

profile of v3, /device:TPU:0, one launch (start us, length us, event | category | flops | bytes accessed | tf_op | source)
XLA Modules:
  0.0 79.2 jit_solution(15271276302042613097)
XLA Ops:
  0.6 1.4 %shard_map.127 = (s32[1,128]{1,0:T(1,128)S(1)}, f32[16,128]{1,0:T(8,128)S(1)}, bf16[128,1024]{1,0:T(8,128)(2,1)S(1)}, bf16[256,1024]{1,0:T(8,128)(2,1)S(1)}, bf1...) custom-call(f32[2,16]{1,0:T(2,128)} %bias_ref.1, s32[1,128]{1,0:T(1,128)} %series_ref.1, ...), custom_call_target="tpu_custom_call" | custom-call | flops 4194304 | bytes 4194304 | tf_op jit(solution)/shard_map/pallas_call | solution.py:309
  2.0 3.1 %collective-permute-start = (bf16[256,1024]{1,0:T(8,128)(2,1)S(1)}, bf16[256,1024]{1,0:T(8,128)(2,1)S(1)}, u32[]{:S(2)}, u32[]{:S(2)}) collective-permute-start(bf16[256,1024]{1,0:T(8,128)(2,1)S(1)} %get-tuple-element.38.qvo_ref), channel_id=1, source_target_pairs={{0,16},{16,0},{1,17},{17,1},{2,18},{18,2},{3,19},{19,3},{4,20},{20... | collective-permute-start | bytes 1572872 | tf_op jit(solution)/shard_map/ppermute | solution.py:328
  5.1 0.1 collective-permute-start.1
  5.2 1.9 %collective-permute-start.3 = (bf16[128,512]{1,0:T(8,128)(2,1)S(1)}, bf16[128,512]{1,0:T(8,128)(2,1)S(1)}, u32[]{:S(2)}, u32[]{:S(2)}) collective-permute-start(bf16[128,512]{1,0:T(8,128)(2,1)S(1)} %get-tuple-element.47), channel_id=1, source_target_pairs={{0,16},{16,0},{1,17},{17,1},{2,18},{18,2},{3,19},{19,3},{4,20},{20... | collective-permute-start | bytes 393224 | tf_op jit(solution)/shard_map/ppermute | solution.py:349
  7.1 0.1 collective-permute-start.2
  7.2 18.3 %collective-permute-done.2.idx_ref = s32[1,128]{1,0:T(1,128)S(1)} collective-permute-done((s32[1,128]{1,0:T(1,128)S(1)}, s32[1,128]{1,0:T(1,128)S(1)}, u32[]{:S(2)}, u32[]{:S(2)}) %collective-permute-start.2) | collective-permute-done | bytes 544 | tf_op jit(solution)/shard_map/ppermute | solution.py:328
  25.5 0.0 collective-permute-done.1.kx_ref
  25.5 0.0 collective-permute-done.qvx_ref
  25.5 2.4 %shard_map.128 = (f32[128,1024]{1,0:T(8,128)S(1)}, f32[128,1024]{1,0:T(8,128)S(1)}, bf16[16,128,256]{2,1,0:T(8,128)(2,1)S(1)}, bf16[16,128,128]{2,1,0:T(8,128)(2,1)S(1)}) custom-call(f32[16,128]{1,0:T(8,128)S(1)} %get-tuple-element.40.gap_ref, s32[1,128]{1,0:T(1,128)S(1)} %get-tuple-element.41.ido_ref, s32[1,128]{1,0:T(1,128)S(1)} %collective-permute-done.2.idx_ref, ...), custom_call_target="tpu_custom_call" | custom-call | flops 1073741824 | bytes 4194304 | tf_op jit(solution)/shard_map/pallas_call | solution.py:309
  27.9 0.5 shard_map.131
  28.4 0.1 collective-permute-start.20
  28.5 1.8 %collective-permute-start.4 = (bf16[128,512]{1,0:T(8,128)(2,1)S(1)}, bf16[128,512]{1,0:T(8,128)(2,1)S(1)}, u32[]{:S(2)}, u32[]{:S(2)}) collective-permute-start(bf16[128,512]{1,0:T(8,128)(2,1)S(1)} %get-tuple-element.48), channel_id=1, source_target_pairs={{0,16},{16,0},{1,17},{17,1},{2,18},{18,2},{3,19},{19,3},{4,20},{20... | collective-permute-start | bytes 393224 | tf_op jit(solution)/shard_map/ppermute | solution.py:328
  30.3 2.6 %collective-permute-start.5 = (bf16[64,1024]{1,0:T(8,128)(2,1)S(1)}, bf16[64,1024]{1,0:T(8,128)(2,1)S(1)}, u32[]{:S(2)}, u32[]{:S(2)}) collective-permute-start(bf16[64,1024]{1,0:T(8,128)(2,1)S(1)} %copy-done), channel_id=1, source_target_pairs={{0,8},{1,9},{2,10},{3,11},{4,12},{5,13},{6,14},{7,15},{8,0},{9,1},... | collective-permute-start | bytes 393224 | tf_op jit(solution)/shard_map/ppermute | solution.py:325
  32.9 1.6 %collective-permute-start.6 = (bf16[64,1024]{1,0:T(8,128)(2,1)S(1)}, bf16[64,1024]{1,0:T(8,128)(2,1)S(1)}, u32[]{:S(2)}, u32[]{:S(2)}) collective-permute-start(bf16[64,1024]{1,0:T(8,128)(2,1)S(1)} %copy-done), channel_id=1, source_target_pairs={{0,4},{1,5},{2,6},{3,7},{4,0},{5,1},{6,2},{7,3},{8,12},{9,13},{10,... | collective-permute-start | bytes 393224 | tf_op jit(solution)/shard_map/ppermute | solution.py:325
  34.5 1.5 %collective-permute-start.8 = (bf16[64,1024]{1,0:T(8,128)(2,1)S(1)}, bf16[64,1024]{1,0:T(8,128)(2,1)S(1)}, u32[]{:S(2)}, u32[]{:S(2)}) collective-permute-start(bf16[64,1024]{1,0:T(8,128)(2,1)S(1)} %copy-done), channel_id=1, source_target_pairs={{0,2},{1,3},{2,0},{3,1},{4,6},{5,7},{6,4},{7,5},{8,10},{9,11},{10,... | collective-permute-start | bytes 393224 | tf_op jit(solution)/shard_map/ppermute | solution.py:325
  36.0 0.0 collective-permute-start.12
  36.0 3.7 %collective-permute-done.5.rest_3_ = bf16[64,1024]{1,0:T(8,128)(2,1)S(1)} collective-permute-done((bf16[64,1024]{1,0:T(8,128)(2,1)S(1)}, bf16[64,1024]{1,0:T(8,128)(2,1)S(1)}, u32[]{:S(2)}, u32[]{:S(2)}) %collective-permute-start.5) | collective-permute-done | bytes 131104 | tf_op jit(solution)/shard_map/ppermute | solution.py:325
  39.7 0.6 collective-permute-start.7
  40.3 0.0 collective-permute-done.20.got_ref
  40.3 1.5 %collective-permute-start.9 = (bf16[64,1024]{1,0:T(8,128)(2,1)S(1)}, bf16[64,1024]{1,0:T(8,128)(2,1)S(1)}, u32[]{:S(2)}, u32[]{:S(2)}) collective-permute-start(bf16[64,1024]{1,0:T(8,128)(2,1)S(1)} %collective-permute-done.5.rest_3_), channel_id=1, source_target_pairs={{0,2},{1,3},{2,0},{3,1},{4,6},{5,7},{6,4},{7,5},{8,10},{9,11},{10,... | collective-permute-start | bytes 393224 | tf_op jit(solution)/shard_map/ppermute | solution.py:325
  41.8 0.2 shard_map.132
  41.9 0.0 collective-permute-done.6.rest_4_
  42.0 0.6 collective-permute-start.21
  42.6 1.5 %collective-permute-start.10 = (bf16[64,1024]{1,0:T(8,128)(2,1)S(1)}, bf16[64,1024]{1,0:T(8,128)(2,1)S(1)}, u32[]{:S(2)}, u32[]{:S(2)}) collective-permute-start(bf16[64,1024]{1,0:T(8,128)(2,1)S(1)} %collective-permute-done.6.rest_4_), channel_id=1, source_target_pairs={{0,2},{1,3},{2,0},{3,1},{4,6},{5,7},{6,4},{7,5},{8,10},{9,11},{10,... | collective-permute-start | bytes 393224 | tf_op jit(solution)/shard_map/ppermute | solution.py:325
  44.1 0.6 collective-permute-done.7.rest_5_
  44.7 2.0 %collective-permute-done.9.rest_7_ = bf16[64,1024]{1,0:T(8,128)(2,1)S(1)} collective-permute-done((bf16[64,1024]{1,0:T(8,128)(2,1)S(1)}, bf16[64,1024]{1,0:T(8,128)(2,1)S(1)}, u32[]{:S(2)}, u32[]{:S(2)}) %collective-permute-start.9) | collective-permute-done | bytes 131104 | tf_op jit(solution)/shard_map/ppermute | solution.py:325
  46.7 1.5 %collective-permute-start.11 = (bf16[64,1024]{1,0:T(8,128)(2,1)S(1)}, bf16[64,1024]{1,0:T(8,128)(2,1)S(1)}, u32[]{:S(2)}, u32[]{:S(2)}) collective-permute-start(bf16[64,1024]{1,0:T(8,128)(2,1)S(1)} %collective-permute-done.7.rest_5_), channel_id=1, source_target_pairs={{0,2},{1,3},{2,0},{3,1},{4,6},{5,7},{6,4},{7,5},{8,10},{9,11},{10,... | collective-permute-start | bytes 393224 | tf_op jit(solution)/shard_map/ppermute | solution.py:325
  48.1 6.9 %collective-permute-done.10.rest_8_ = bf16[64,1024]{1,0:T(8,128)(2,1)S(1)} collective-permute-done((bf16[64,1024]{1,0:T(8,128)(2,1)S(1)}, bf16[64,1024]{1,0:T(8,128)(2,1)S(1)}, u32[]{:S(2)}, u32[]{:S(2)}) %collective-permute-start.10) | collective-permute-done | bytes 131104 | tf_op jit(solution)/shard_map/ppermute | solution.py:325
  55.1 0.5 collective-permute-start.15
  55.6 0.1 collective-permute-start.17
  55.7 1.0 %collective-permute-done.11.rest_9_ = bf16[64,1024]{1,0:T(8,128)(2,1)S(1)} collective-permute-done((bf16[64,1024]{1,0:T(8,128)(2,1)S(1)}, bf16[64,1024]{1,0:T(8,128)(2,1)S(1)}, u32[]{:S(2)}, u32[]{:S(2)}) %collective-permute-start.11) | collective-permute-done | bytes 131104 | tf_op jit(solution)/shard_map/ppermute | solution.py:325
  56.7 0.5 collective-permute-start.19
  57.2 0.1 shard_map.133
  57.3 3.4 %collective-permute-start.22 = (bf16[128,512]{1,0:T(8,128)(2,1)S(1)}, bf16[128,512]{1,0:T(8,128)(2,1)S(1)}, u32[]{:S(2)}, u32[]{:S(2)}) collective-permute-start(bf16[128,512]{1,0:T(8,128)(2,1)S(1)} %get-tuple-element.62), channel_id=1, source_target_pairs={{0,8},{1,9},{2,10},{3,11},{4,12},{5,13},{6,14},{7,15},{8,0},{9,1},... | collective-permute-start | bytes 393224 | tf_op jit(solution)/shard_map/ppermute | solution.py:325
  60.7 1.9 %shard_map.129 = (bf16[8,2,64,1024]{3,2,1,0:T(8,128)(2,1)S(1)}, bf16[256,1024]{1,0:T(8,128)(2,1)S(1)}, bf16[16,128,256]{2,1,0:T(8,128)(2,1)S(1)}, bf16[16,128,128]{2,1,0:T(8,128)(2,1)S(1)}, f32[1,128]{1,0:T(1,128)S(1)}) custom-call(s32[1,128]{1,0:T(1,128)S(1)} %get-tuple-element.41.ido_ref, s32[1,128]{1,0:T(1,128)S(1)} %collective-permute-done.2.idx_ref, ...), custom_call_target="tpu_custom_call" | custom-call | flops 1073741824 | bytes 4194304 | tf_op jit(solution)/shard_map/pallas_call | solution.py:309
  62.7 0.0 collective-permute-start.23
  62.7 1.1 %collective-permute-done.23.b_ref = f32[1,128]{1,0:T(1,128)S(1)} collective-permute-done((f32[1,128]{1,0:T(1,128)S(1)}, f32[1,128]{1,0:T(1,128)S(1)}, u32[]{:S(2)}, u32[]{:S(2)}) %collective-permute-start.23) | collective-permute-done | bytes 544 | tf_op jit(solution)/shard_map/ppermute | solution.py:325
  63.9 1.5 %collective-permute-start.24 = (f32[1,128]{1,0:T(1,128)S(1)}, f32[1,128]{1,0:T(1,128)S(1)}, u32[]{:S(2)}, u32[]{:S(2)}) collective-permute-start(f32[1,128]{1,0:T(1,128)S(1)} %shard_map.134.a_ref), channel_id=1, source_target_pairs={{0,2},{1,3},{2,0},{3,1},{4,6},{5,7},{6,4},{7,5},{8,10},{9,11},{10,... | collective-permute-start | bytes 1544 | tf_op jit(solution)/shard_map/ppermute | solution.py:325
  65.4 2.1 %collective-permute-done.24.b_ref = f32[1,128]{1,0:T(1,128)S(1)} collective-permute-done((f32[1,128]{1,0:T(1,128)S(1)}, f32[1,128]{1,0:T(1,128)S(1)}, u32[]{:S(2)}, u32[]{:S(2)}) %collective-permute-start.24) | collective-permute-done | bytes 544 | tf_op jit(solution)/shard_map/ppermute | solution.py:325
  67.5 0.8 %collective-permute-start.25 = (f32[1,128]{1,0:T(1,128)S(1)}, f32[1,128]{1,0:T(1,128)S(1)}, u32[]{:S(2)}, u32[]{:S(2)}) collective-permute-start(f32[1,128]{1,0:T(1,128)S(1)} %shard_map.135.refs_0_), channel_id=1, source_target_pairs={{0,8},{1,9},{2,10},{3,11},{4,12},{5,13},{6,14},{7,15},{8,0},{9,1},... | collective-permute-start | bytes 1544 | tf_op jit(solution)/shard_map/ppermute | solution.py:325
  68.3 3.7 %collective-permute-done.25.refs_1_ = f32[1,128]{1,0:T(1,128)S(1)} collective-permute-done((f32[1,128]{1,0:T(1,128)S(1)}, f32[1,128]{1,0:T(1,128)S(1)}, u32[]{:S(2)}, u32[]{:S(2)}) %collective-permute-start.25) | collective-permute-done | bytes 544 | tf_op jit(solution)/shard_map/ppermute | solution.py:325
  71.9 0.1 shard_map.136
  72.0 0.4 collective-permute-start.26
  72.4 1.7 %collective-permute-start.28 = (bf16[272,128]{1,0:T(8,128)(2,1)S(1)}, bf16[272,128]{1,0:T(8,128)(2,1)S(1)}, u32[]{:S(2)}, u32[]{:S(2)}) collective-permute-start(bf16[272,128]{1,0:T(8,128)(2,1)S(1)} %get-tuple-element.66), channel_id=1, source_target_pairs={{0,20},{1,21},{2,22},{3,23},{4,16},{5,17},{6,18},{7,19},{8,28},{9,... | collective-permute-start | bytes 208904 | tf_op jit(solution)/shard_map/ppermute | solution.py:395
  74.0 1.5 %collective-permute-start.27 = (bf16[272,128]{1,0:T(8,128)(2,1)S(1)}, bf16[272,128]{1,0:T(8,128)(2,1)S(1)}, u32[]{:S(2)}, u32[]{:S(2)}) collective-permute-start(bf16[272,128]{1,0:T(8,128)(2,1)S(1)} %get-tuple-element.67), channel_id=1, source_target_pairs={{0,16},{16,0},{1,17},{17,1},{2,18},{18,2},{3,19},{19,3},{4,20},{20... | collective-permute-start | bytes 208904 | tf_op jit(solution)/shard_map/ppermute | solution.py:328
  75.6 2.3 %shard_map.130 = (bf16[128,1024]{1,0:T(8,128)(2,1)}, bf16[128,1024]{1,0:T(8,128)(2,1)}, bf16[128,1024]{1,0:T(8,128)(2,1)}, bf16[128,1024]{1,0:T(8,128)(2,1)}) custom-call(bf16[256,1024]{1,0:T(8,128)(2,1)S(1)} %get-tuple-element.38.qvo_ref, bf16[256,1024]{1,0:T(8,128)(2,1)S(1)} %collective-permute-done.qvx_ref, ...), custom_call_target="tpu_custom_call" | custom-call | flops 1073741824 | bytes 4194304 | tf_op jit(solution)/shard_map/pallas_call | solution.py:309
  77.8 0.5 collective-permute-done.27.refs_0_
  78.4 0.8 %shard_map.137 = (f32[64,1024]{1,0:T(8,128)}, f32[2,16]{1,0:T(2,128)}) custom-call(f32[1,64,512]{2,1,0:T(8,128)S(1)} %get-tuple-element.64.keep_ref, f32[1,128]{1,0:T(1,128)S(1)} %get-tuple-element.65.sums_ref, bf16[272,128]{1,0:T(8,128)(2,1)S(1)} %collective-permute-done.26.got_ref, bf16[272,128]{1,0:T(8,128)(2,1)S(1)} %collective-permute-done.27.refs_0_, ...), custom_call_target="tpu_custom_call" | custom-call | flops 4194304 | bytes 4194304 | tf_op jit(solution)/shard_map/pallas_call | solution.py:309
  (23 shorter events, 0.1 us)
Async XLA Ops:
  2.0 23.5 %collective-permute-start = (bf16[256,1024]{1,0:T(8,128)(2,1)S(1)}, bf16[256,1024]{1,0:T(8,128)(2,1)S(1)}, u32[]{:S(2)}, u32[]{:S(2)}) collective-permute-start(bf16[256,1024]{1,0:T(8,128)(2,1)S(1)} %get-tuple-element.38.qvo_ref), channel_id=1, source_target_pairs={{0,16},{16,0},{1,17},{17,1},{2,18},{18,2},{3,19},{19,3},{4,20},{20... | collective-permute-start | bytes 1572872 | tf_op jit(solution)/shard_map/ppermute | solution.py:328
  5.1 20.4 %collective-permute-start.1 = (bf16[128,1024]{1,0:T(8,128)(2,1)}, bf16[128,1024]{1,0:T(8,128)(2,1)S(1)}, u32[]{:S(2)}, u32[]{:S(2)}) collective-permute-start(bf16[128,1024]{1,0:T(8,128)(2,1)} %bitcast.12), channel_id=1, source_target_pairs={{0,16},{16,0},{1,17},{17,1},{2,18},{18,2},{3,19},{19,3},{4,20},{20... | collective-permute-start | bytes 786440 | tf_op jit(solution)/shard_map/ppermute | solution.py:328
  5.2 22.8 %collective-permute-start.3 = (bf16[128,512]{1,0:T(8,128)(2,1)S(1)}, bf16[128,512]{1,0:T(8,128)(2,1)S(1)}, u32[]{:S(2)}, u32[]{:S(2)}) collective-permute-start(bf16[128,512]{1,0:T(8,128)(2,1)S(1)} %get-tuple-element.47), channel_id=1, source_target_pairs={{0,16},{16,0},{1,17},{17,1},{2,18},{18,2},{3,19},{19,3},{4,20},{20... | collective-permute-start | bytes 393224 | tf_op jit(solution)/shard_map/ppermute | solution.py:349
  7.1 18.4 %collective-permute-start.2 = (s32[1,128]{1,0:T(1,128)S(1)}, s32[1,128]{1,0:T(1,128)S(1)}, u32[]{:S(2)}, u32[]{:S(2)}) collective-permute-start(s32[1,128]{1,0:T(1,128)S(1)} %get-tuple-element.41.ido_ref), channel_id=1, source_target_pairs={{0,16},{16,0},{1,17},{17,1},{2,18},{18,2},{3,19},{19,3},{4,20},{20... | collective-permute-start | bytes 1544 | tf_op jit(solution)/shard_map/ppermute | solution.py:328
  25.5 4.8 %copy-start = (bf16[64,1024]{1,0:T(8,128)(2,1)S(1)}, bf16[64,1024]{1,0:T(8,128)(2,1)}, u32[]{:S(2)}) copy-start(bf16[64,1024]{1,0:T(8,128)(2,1)} %rest_2_.1) | copy-start | bytes 393220
  28.4 11.8 %collective-permute-start.20 = (bf16[512,512]{1,0:T(8,128)(2,1)S(1)}, bf16[512,512]{1,0:T(8,128)(2,1)S(1)}, u32[]{:S(2)}, u32[]{:S(2)}) collective-permute-start(bf16[512,512]{1,0:T(8,128)(2,1)S(1)} %get-tuple-element.58), channel_id=1, source_target_pairs={{0,1},{1,0},{2,3},{3,2},{4,5},{5,4},{6,7},{7,6},{8,9},{9,8},{10,11... | collective-permute-start | bytes 1572872 | tf_op jit(solution)/shard_map/ppermute | solution.py:325
  28.5 7.5 %collective-permute-start.4 = (bf16[128,512]{1,0:T(8,128)(2,1)S(1)}, bf16[128,512]{1,0:T(8,128)(2,1)S(1)}, u32[]{:S(2)}, u32[]{:S(2)}) collective-permute-start(bf16[128,512]{1,0:T(8,128)(2,1)S(1)} %get-tuple-element.48), channel_id=1, source_target_pairs={{0,16},{16,0},{1,17},{17,1},{2,18},{18,2},{3,19},{19,3},{4,20},{20... | collective-permute-start | bytes 393224 | tf_op jit(solution)/shard_map/ppermute | solution.py:328
  30.3 9.4 %collective-permute-start.5 = (bf16[64,1024]{1,0:T(8,128)(2,1)S(1)}, bf16[64,1024]{1,0:T(8,128)(2,1)S(1)}, u32[]{:S(2)}, u32[]{:S(2)}) collective-permute-start(bf16[64,1024]{1,0:T(8,128)(2,1)S(1)} %copy-done), channel_id=1, source_target_pairs={{0,8},{1,9},{2,10},{3,11},{4,12},{5,13},{6,14},{7,15},{8,0},{9,1},... | collective-permute-start | bytes 393224 | tf_op jit(solution)/shard_map/ppermute | solution.py:325
  32.9 9.0 %collective-permute-start.6 = (bf16[64,1024]{1,0:T(8,128)(2,1)S(1)}, bf16[64,1024]{1,0:T(8,128)(2,1)S(1)}, u32[]{:S(2)}, u32[]{:S(2)}) collective-permute-start(bf16[64,1024]{1,0:T(8,128)(2,1)S(1)} %copy-done), channel_id=1, source_target_pairs={{0,4},{1,5},{2,6},{3,7},{4,0},{5,1},{6,2},{7,3},{8,12},{9,13},{10,... | collective-permute-start | bytes 393224 | tf_op jit(solution)/shard_map/ppermute | solution.py:325
  34.5 8.1 %collective-permute-start.8 = (bf16[64,1024]{1,0:T(8,128)(2,1)S(1)}, bf16[64,1024]{1,0:T(8,128)(2,1)S(1)}, u32[]{:S(2)}, u32[]{:S(2)}) collective-permute-start(bf16[64,1024]{1,0:T(8,128)(2,1)S(1)} %copy-done), channel_id=1, source_target_pairs={{0,2},{1,3},{2,0},{3,1},{4,6},{5,7},{6,4},{7,5},{8,10},{9,11},{10,... | collective-permute-start | bytes 393224 | tf_op jit(solution)/shard_map/ppermute | solution.py:325
  36.0 8.1 %collective-permute-start.12 = (bf16[64,1024]{1,0:T(8,128)(2,1)S(1)}, bf16[64,1024]{1,0:T(8,128)(2,1)S(1)}, u32[]{:S(2)}, u32[]{:S(2)}) collective-permute-start(bf16[64,1024]{1,0:T(8,128)(2,1)S(1)} %copy-done), channel_id=1, source_target_pairs={{0,1},{1,0},{2,3},{3,2},{4,5},{5,4},{6,7},{7,6},{8,9},{9,8},{10,11... | collective-permute-start | bytes 393224 | tf_op jit(solution)/shard_map/ppermute | solution.py:325
  39.7 5.0 %collective-permute-start.7 = (bf16[64,1024]{1,0:T(8,128)(2,1)S(1)}, bf16[64,1024]{1,0:T(8,128)(2,1)S(1)}, u32[]{:S(2)}, u32[]{:S(2)}) collective-permute-start(bf16[64,1024]{1,0:T(8,128)(2,1)S(1)} %collective-permute-done.5.rest_3_), channel_id=1, source_target_pairs={{0,4},{1,5},{2,6},{3,7},{4,0},{5,1},{6,2},{7,3},{8,12},{9,13},{10,... | collective-permute-start | bytes 393224 | tf_op jit(solution)/shard_map/ppermute | solution.py:325
  40.3 6.4 %collective-permute-start.9 = (bf16[64,1024]{1,0:T(8,128)(2,1)S(1)}, bf16[64,1024]{1,0:T(8,128)(2,1)S(1)}, u32[]{:S(2)}, u32[]{:S(2)}) collective-permute-start(bf16[64,1024]{1,0:T(8,128)(2,1)S(1)} %collective-permute-done.5.rest_3_), channel_id=1, source_target_pairs={{0,2},{1,3},{2,0},{3,1},{4,6},{5,7},{6,4},{7,5},{8,10},{9,11},{10,... | collective-permute-start | bytes 393224 | tf_op jit(solution)/shard_map/ppermute | solution.py:325
  42.0 14.7 %collective-permute-start.21 = (bf16[256,512]{1,0:T(8,128)(2,1)S(1)}, bf16[256,512]{1,0:T(8,128)(2,1)S(1)}, u32[]{:S(2)}, u32[]{:S(2)}) collective-permute-start(bf16[256,512]{1,0:T(8,128)(2,1)S(1)} %get-tuple-element.60), channel_id=1, source_target_pairs={{0,2},{1,3},{2,0},{3,1},{4,6},{5,7},{6,4},{7,5},{8,10},{9,11},{10,... | collective-permute-start | bytes 786440 | tf_op jit(solution)/shard_map/ppermute | solution.py:325
  42.6 12.5 %collective-permute-start.10 = (bf16[64,1024]{1,0:T(8,128)(2,1)S(1)}, bf16[64,1024]{1,0:T(8,128)(2,1)S(1)}, u32[]{:S(2)}, u32[]{:S(2)}) collective-permute-start(bf16[64,1024]{1,0:T(8,128)(2,1)S(1)} %collective-permute-done.6.rest_4_), channel_id=1, source_target_pairs={{0,2},{1,3},{2,0},{3,1},{4,6},{5,7},{6,4},{7,5},{8,10},{9,11},{10,... | collective-permute-start | bytes 393224 | tf_op jit(solution)/shard_map/ppermute | solution.py:325
  44.1 11.0 %collective-permute-start.13 = (bf16[64,1024]{1,0:T(8,128)(2,1)S(1)}, bf16[64,1024]{1,0:T(8,128)(2,1)S(1)}, u32[]{:S(2)}, u32[]{:S(2)}) collective-permute-start(bf16[64,1024]{1,0:T(8,128)(2,1)S(1)} %collective-permute-done.5.rest_3_), channel_id=1, source_target_pairs={{0,1},{1,0},{2,3},{3,2},{4,5},{5,4},{6,7},{7,6},{8,9},{9,8},{10,11... | collective-permute-start | bytes 393224 | tf_op jit(solution)/shard_map/ppermute | solution.py:325
  44.7 10.9 %collective-permute-start.14 = (bf16[64,1024]{1,0:T(8,128)(2,1)S(1)}, bf16[64,1024]{1,0:T(8,128)(2,1)S(1)}, u32[]{:S(2)}, u32[]{:S(2)}) collective-permute-start(bf16[64,1024]{1,0:T(8,128)(2,1)S(1)} %collective-permute-done.6.rest_4_), channel_id=1, source_target_pairs={{0,1},{1,0},{2,3},{3,2},{4,5},{5,4},{6,7},{7,6},{8,9},{9,8},{10,11... | collective-permute-start | bytes 393224 | tf_op jit(solution)/shard_map/ppermute | solution.py:325
  46.7 10.0 %collective-permute-start.11 = (bf16[64,1024]{1,0:T(8,128)(2,1)S(1)}, bf16[64,1024]{1,0:T(8,128)(2,1)S(1)}, u32[]{:S(2)}, u32[]{:S(2)}) collective-permute-start(bf16[64,1024]{1,0:T(8,128)(2,1)S(1)} %collective-permute-done.7.rest_5_), channel_id=1, source_target_pairs={{0,2},{1,3},{2,0},{3,1},{4,6},{5,7},{6,4},{7,5},{8,10},{9,11},{10,... | collective-permute-start | bytes 393224 | tf_op jit(solution)/shard_map/ppermute | solution.py:325
  55.1 2.2 %collective-permute-start.16 = (bf16[64,1024]{1,0:T(8,128)(2,1)S(1)}, bf16[64,1024]{1,0:T(8,128)(2,1)S(1)}, u32[]{:S(2)}, u32[]{:S(2)}) collective-permute-start(bf16[64,1024]{1,0:T(8,128)(2,1)S(1)} %collective-permute-done.8.rest_6_), channel_id=1, source_target_pairs={{0,1},{1,0},{2,3},{3,2},{4,5},{5,4},{6,7},{7,6},{8,9},{9,8},{10,11... | collective-permute-start | bytes 393224 | tf_op jit(solution)/shard_map/ppermute | solution.py:325
  55.1 5.6 %collective-permute-start.15 = (bf16[64,1024]{1,0:T(8,128)(2,1)S(1)}, bf16[64,1024]{1,0:T(8,128)(2,1)S(1)}, u32[]{:S(2)}, u32[]{:S(2)}) collective-permute-start(bf16[64,1024]{1,0:T(8,128)(2,1)S(1)} %collective-permute-done.7.rest_5_), channel_id=1, source_target_pairs={{0,1},{1,0},{2,3},{3,2},{4,5},{5,4},{6,7},{7,6},{8,9},{9,8},{10,11... | collective-permute-start | bytes 393224 | tf_op jit(solution)/shard_map/ppermute | solution.py:325
  55.6 5.1 %collective-permute-start.17 = (bf16[64,1024]{1,0:T(8,128)(2,1)S(1)}, bf16[64,1024]{1,0:T(8,128)(2,1)S(1)}, u32[]{:S(2)}, u32[]{:S(2)}) collective-permute-start(bf16[64,1024]{1,0:T(8,128)(2,1)S(1)} %collective-permute-done.9.rest_7_), channel_id=1, source_target_pairs={{0,1},{1,0},{2,3},{3,2},{4,5},{5,4},{6,7},{7,6},{8,9},{9,8},{10,11... | collective-permute-start | bytes 393224 | tf_op jit(solution)/shard_map/ppermute | solution.py:325
  56.7 4.1 %collective-permute-start.18 = (bf16[64,1024]{1,0:T(8,128)(2,1)S(1)}, bf16[64,1024]{1,0:T(8,128)(2,1)S(1)}, u32[]{:S(2)}, u32[]{:S(2)}) collective-permute-start(bf16[64,1024]{1,0:T(8,128)(2,1)S(1)} %collective-permute-done.10.rest_8_), channel_id=1, source_target_pairs={{0,1},{1,0},{2,3},{3,2},{4,5},{5,4},{6,7},{7,6},{8,9},{9,8},{10,11... | collective-permute-start | bytes 393224 | tf_op jit(solution)/shard_map/ppermute | solution.py:325
  56.7 4.1 %collective-permute-start.19 = (bf16[64,1024]{1,0:T(8,128)(2,1)S(1)}, bf16[64,1024]{1,0:T(8,128)(2,1)S(1)}, u32[]{:S(2)}, u32[]{:S(2)}) collective-permute-start(bf16[64,1024]{1,0:T(8,128)(2,1)S(1)} %collective-permute-done.11.rest_9_), channel_id=1, source_target_pairs={{0,1},{1,0},{2,3},{3,2},{4,5},{5,4},{6,7},{7,6},{8,9},{9,8},{10,11... | collective-permute-start | bytes 393224 | tf_op jit(solution)/shard_map/ppermute | solution.py:325
  57.3 14.7 %collective-permute-start.22 = (bf16[128,512]{1,0:T(8,128)(2,1)S(1)}, bf16[128,512]{1,0:T(8,128)(2,1)S(1)}, u32[]{:S(2)}, u32[]{:S(2)}) collective-permute-start(bf16[128,512]{1,0:T(8,128)(2,1)S(1)} %get-tuple-element.62), channel_id=1, source_target_pairs={{0,8},{1,9},{2,10},{3,11},{4,12},{5,13},{6,14},{7,15},{8,0},{9,1},... | collective-permute-start | bytes 393224 | tf_op jit(solution)/shard_map/ppermute | solution.py:325
  62.7 1.2 %collective-permute-start.23 = (f32[1,128]{1,0:T(1,128)S(1)}, f32[1,128]{1,0:T(1,128)S(1)}, u32[]{:S(2)}, u32[]{:S(2)}) collective-permute-start(f32[1,128]{1,0:T(1,128)S(1)} %get-tuple-element.63.a_ref), channel_id=1, source_target_pairs={{0,1},{1,0},{2,3},{3,2},{4,5},{5,4},{6,7},{7,6},{8,9},{9,8},{10,11... | collective-permute-start | bytes 1544 | tf_op jit(solution)/shard_map/ppermute | solution.py:325
  63.9 3.6 %collective-permute-start.24 = (f32[1,128]{1,0:T(1,128)S(1)}, f32[1,128]{1,0:T(1,128)S(1)}, u32[]{:S(2)}, u32[]{:S(2)}) collective-permute-start(f32[1,128]{1,0:T(1,128)S(1)} %shard_map.134.a_ref), channel_id=1, source_target_pairs={{0,2},{1,3},{2,0},{3,1},{4,6},{5,7},{6,4},{7,5},{8,10},{9,11},{10,... | collective-permute-start | bytes 1544 | tf_op jit(solution)/shard_map/ppermute | solution.py:325
  67.5 4.5 %collective-permute-start.25 = (f32[1,128]{1,0:T(1,128)S(1)}, f32[1,128]{1,0:T(1,128)S(1)}, u32[]{:S(2)}, u32[]{:S(2)}) collective-permute-start(f32[1,128]{1,0:T(1,128)S(1)} %shard_map.135.refs_0_), channel_id=1, source_target_pairs={{0,8},{1,9},{2,10},{3,11},{4,12},{5,13},{6,14},{7,15},{8,0},{9,1},... | collective-permute-start | bytes 1544 | tf_op jit(solution)/shard_map/ppermute | solution.py:325
  72.0 5.8 %collective-permute-start.26 = (bf16[272,128]{1,0:T(8,128)(2,1)S(1)}, bf16[272,128]{1,0:T(8,128)(2,1)S(1)}, u32[]{:S(2)}, u32[]{:S(2)}) collective-permute-start(bf16[272,128]{1,0:T(8,128)(2,1)S(1)} %get-tuple-element.66), channel_id=1, source_target_pairs={{0,4},{1,5},{2,6},{3,7},{4,0},{5,1},{6,2},{7,3},{8,12},{9,13},{10,... | collective-permute-start | bytes 208904 | tf_op jit(solution)/shard_map/ppermute | solution.py:325
  72.4 6.0 %collective-permute-start.28 = (bf16[272,128]{1,0:T(8,128)(2,1)S(1)}, bf16[272,128]{1,0:T(8,128)(2,1)S(1)}, u32[]{:S(2)}, u32[]{:S(2)}) collective-permute-start(bf16[272,128]{1,0:T(8,128)(2,1)S(1)} %get-tuple-element.66), channel_id=1, source_target_pairs={{0,20},{1,21},{2,22},{3,23},{4,16},{5,17},{6,18},{7,19},{8,28},{9,... | collective-permute-start | bytes 208904 | tf_op jit(solution)/shard_map/ppermute | solution.py:395
  74.0 4.3 %collective-permute-start.27 = (bf16[272,128]{1,0:T(8,128)(2,1)S(1)}, bf16[272,128]{1,0:T(8,128)(2,1)S(1)}, u32[]{:S(2)}, u32[]{:S(2)}) collective-permute-start(bf16[272,128]{1,0:T(8,128)(2,1)S(1)} %get-tuple-element.67), channel_id=1, source_target_pairs={{0,16},{16,0},{1,17},{17,1},{2,18},{18,2},{3,19},{19,3},{4,20},{20... | collective-permute-start | bytes 208904 | tf_op jit(solution)/shard_map/ppermute | solution.py:328

commit v4 on v3

--- a/solution.py
+++ b/solution.py
@@ -156,16 +156,30 @@
     return jnp.concatenate(parts, axis=1)
 
 
-def weight_kernel(co_ref, cx_ref, do_ref, dx_ref, keep_ref, send_ref):
-    n, _, cols = keep_ref.shape
+def weight_kernel(co_ref, cx_ref, do_ref, dx_ref, go_ref, stay_ref, send_go_ref, send_stay_ref):
+    n, block, cols = go_ref.shape
     cut = pl.ds(pl.multiple_of(lax.axis_index("ctx") * cols, 128), cols)
     d = jnp.concatenate([do_ref[:, cut], dx_ref[...]], axis=0)
-    half = co_ref.shape[1] // 2
+    half, some = co_ref.shape[1] // 2, n // 2
+    first, second = low_bit(1), low_bit(2)
     for part in range(2):
         at = slice(part * half, (part + 1) * half)
         c = jnp.concatenate([co_ref[:, at], cx_ref[:, at]], axis=0).astype(BF)
-        split(dot_tn(c, d), 1, keep_ref.at[part * n // 2:(part + 1) * n // 2],
-              send_ref.at[part * half // 2:(part + 1) * half // 2])
+        grads = dot_tn(c, d).reshape(some, 2, 2, block, cols)
+        kept = jnp.where(first, grads[:, :, 0], grads[:, :, 1])
+        sent = jnp.where(first, grads[:, :, 1], grads[:, :, 0])
+        rows, place = slice(part * some * block, (part + 1) * some * block), slice(part * some, (part + 1) * some)
+        go_ref[place] = jnp.where(second, kept[:, 1], kept[:, 0])
+        stay_ref[place] = jnp.where(second, kept[:, 0], kept[:, 1])
+        for ref, value in ((send_go_ref, jnp.where(second, sent[:, 1], sent[:, 0])),
+                           (send_stay_ref, jnp.where(second, sent[:, 0], sent[:, 1]))):
+            ref[rows, :] = value.astype(BF).reshape(some * block, cols)
+
+
+def sum_kernel(keep_ref, got_ref, out_ref):
+    n, block, cols = keep_ref.shape
+    summed = keep_ref[...] + got_ref[...].astype(F32).reshape(n, block, cols)
+    out_ref[...] = summed.reshape(out_ref.shape).astype(out_ref.dtype)
 
 
 def pack_tail(sums, send_ref):
@@ -363,9 +377,11 @@
         forward_kernel, [gaps, code, code_x, qv, qvx, key_rows, kx],
         [shape((tok, width), F32), shape((rest, width), F32), o_shape, x_shape],
         16 * HEADS * total * total * HEAD_DIM, [pltpu.VMEM((total, total), F32)] * 2, limit=limit)
-    keep, send = plain(weight_kernel, [ctx_o, ctx_x, upstream, near],
-                       [shape((n_dp // 2, block, cols), F32), shape((width // 2, cols), BF)],
-                       2 * total * width * cols, limit=limit)
+    blocks, rows = shape((n_dp // 4, block, cols), F32), shape((width // 4, cols), BF)
+    go, stay, send_go, send_stay = plain(weight_kernel, [ctx_o, ctx_x, upstream, near], [blocks] * 2 + [rows] * 2,
+                                         2 * total * width * cols, limit=limit)
+    send, = plain(sum_kernel, [go, swap(send_go, 1)], [rows])
+    keep, = plain(sum_kernel, [stay, swap(send_stay, 1)], [blocks])
     w_full, d_ctx, s_o, s_x, sums = plain(
         functools.partial(score_grad_kernel, order, len(dx)),
         [code, code_x, qv, qvx, ctx_o, ctx_x, w_o, w_x, upstream, *dx, *[pieces[p] for p in order]],
@@ -379,7 +395,7 @@
         got = swap(sums, bit)
         if bit != bits[-2]:
             sums, = plain(add_kernel, [sums, got], [shape((1, 128), F32)])
-    for bit, after in zip(bits, bits[1:]):
+    for bit, after in zip(bits[1:], bits[2:]):
         n = keep.shape[0] // 2
         args, outs = [keep, swap(send, bit)], [shape((n, block, cols), F32)]
         if n > 1:

time: 79.3 us -> 79.4 us (level)
    ppermute x22 -> x23, starting transfers between devices: 18.6 us -> 19 us  [swap(): return lax.ppermute(array, 'dp', [(i, i ^ bit) for i in range(n_dp)])]
    ppermute x22 -> x23, waiting for transfers between devices: 21.1 us -> 20.9 us  [swap(): return lax.ppermute(array, 'dp', [(i, i ^ bit) for i in range(n_dp)])]
    pallas_call x11 -> x12, Pallas kernels: 9.59 us -> 9.51 us  [plain(): pl.pallas_call(kernel, in_specs=in_specs or [spec] * len(args), out_specs...]
  transfers between devices with their start and end apart: 29 -> 30, of which waited for: 10 -> 10; matrix products, arithmetic and copies ran while one was open for 0% -> 0% of each run, Pallas kernels for 9% -> 9%
where the time goes in v4:
time: 79.4 us; the launch traced here: 79.3 us
  waiting for transfers between devices  39.8 us (50%)
  starting transfers between devices  29.2 us (37%)
  Pallas kernels  9.51 us (12%)
    ppermute x23, waiting for transfers between devices, swap(): return lax.ppermute(array, 'dp', [(i, i ^ bit) for i in range(n_dp)])  20.9 us
    ppermute x23, starting transfers between devices, swap(): return lax.ppermute(array, 'dp', [(i, i ^ bit) for i in range(n_dp)])  19 us
    ppermute x5, waiting for transfers between devices, turns(): lax.ppermute(array, 'ctx', [(i, (i + by) % n_ctx) for i in range(n_ctx)])  18.9 us
    pallas_call x12, Pallas kernels, plain(): pl.pallas_call(kernel, in_specs=in_specs or [spec] * len(args), out_specs...  9.51 us
    ppermute x5, starting transfers between devices, turns(): lax.ppermute(array, 'ctx', [(i, (i + by) % n_ctx) for i in range(n_ctx)])  6.55 us
    ppermute x1, starting transfers between devices, on_device(): lax.ppermute(part, 'ctx', [(i, (i + by) % n_ctx) for i in range(n_ctx)])  1.95 us
    ppermute x1, starting transfers between devices, on_device(): args += [part, lax.ppermute(send, ('ctx', 'dp'), route)]  1.68 us
  transfers between devices with their start and end apart: 30, of which 10 were waited for; matrix products, arithmetic and copies ran while one was open for 0% of the time, Pallas kernels for 9%

profile of v4, /device:TPU:0, one launch (start us, length us, event | category | flops | bytes accessed | tf_op | source)
XLA Modules:
  0.0 79.3 jit_solution(14507039328951311427)
XLA Ops:
  0.6 1.4 %shard_map.127 = (s32[1,128]{1,0:T(1,128)S(1)}, f32[16,128]{1,0:T(8,128)S(1)}, bf16[128,1024]{1,0:T(8,128)(2,1)S(1)}, bf16[256,1024]{1,0:T(8,128)(2,1)S(1)}, bf1...) custom-call(f32[2,16]{1,0:T(2,128)} %bias_ref.1, s32[1,128]{1,0:T(1,128)} %series_ref.1, ...), custom_call_target="tpu_custom_call" | custom-call | flops 4194304 | bytes 4194304 | tf_op jit(solution)/shard_map/pallas_call | solution.py:323
  2.0 3.1 %collective-permute-start = (bf16[256,1024]{1,0:T(8,128)(2,1)S(1)}, bf16[256,1024]{1,0:T(8,128)(2,1)S(1)}, u32[]{:S(2)}, u32[]{:S(2)}) collective-permute-start(bf16[256,1024]{1,0:T(8,128)(2,1)S(1)} %get-tuple-element.38.qvo_ref), channel_id=1, source_target_pairs={{0,16},{16,0},{1,17},{17,1},{2,18},{18,2},{3,19},{19,3},{4,20},{20... | collective-permute-start | bytes 1572872 | tf_op jit(solution)/shard_map/ppermute | solution.py:342
  5.1 0.1 collective-permute-start.1
  5.2 1.9 %collective-permute-start.3 = (bf16[128,512]{1,0:T(8,128)(2,1)S(1)}, bf16[128,512]{1,0:T(8,128)(2,1)S(1)}, u32[]{:S(2)}, u32[]{:S(2)}) collective-permute-start(bf16[128,512]{1,0:T(8,128)(2,1)S(1)} %get-tuple-element.47), channel_id=1, source_target_pairs={{0,16},{16,0},{1,17},{17,1},{2,18},{18,2},{3,19},{19,3},{4,20},{20... | collective-permute-start | bytes 393224 | tf_op jit(solution)/shard_map/ppermute | solution.py:363
  7.1 0.1 collective-permute-start.2
  7.2 18.3 %collective-permute-done.2.idx_ref = s32[1,128]{1,0:T(1,128)S(1)} collective-permute-done((s32[1,128]{1,0:T(1,128)S(1)}, s32[1,128]{1,0:T(1,128)S(1)}, u32[]{:S(2)}, u32[]{:S(2)}) %collective-permute-start.2) | collective-permute-done | bytes 544 | tf_op jit(solution)/shard_map/ppermute | solution.py:342
  25.5 0.0 collective-permute-done.1.kx_ref
  25.5 0.0 collective-permute-done.qvx_ref
  25.5 2.4 %shard_map.128 = (f32[128,1024]{1,0:T(8,128)S(1)}, f32[128,1024]{1,0:T(8,128)S(1)}, bf16[16,128,256]{2,1,0:T(8,128)(2,1)S(1)}, bf16[16,128,128]{2,1,0:T(8,128)(2,1)S(1)}) custom-call(f32[16,128]{1,0:T(8,128)S(1)} %get-tuple-element.40.gap_ref, s32[1,128]{1,0:T(1,128)S(1)} %get-tuple-element.41.ido_ref, s32[1,128]{1,0:T(1,128)S(1)} %collective-permute-done.2.idx_ref, ...), custom_call_target="tpu_custom_call" | custom-call | flops 1073741824 | bytes 4194304 | tf_op jit(solution)/shard_map/pallas_call | solution.py:323
  27.9 0.5 shard_map.131
  28.5 0.1 collective-permute-start.21
  28.5 1.8 %collective-permute-start.4 = (bf16[128,512]{1,0:T(8,128)(2,1)S(1)}, bf16[128,512]{1,0:T(8,128)(2,1)S(1)}, u32[]{:S(2)}, u32[]{:S(2)}) collective-permute-start(bf16[128,512]{1,0:T(8,128)(2,1)S(1)} %get-tuple-element.48), channel_id=1, source_target_pairs={{0,16},{16,0},{1,17},{17,1},{2,18},{18,2},{3,19},{19,3},{4,20},{20... | collective-permute-start | bytes 393224 | tf_op jit(solution)/shard_map/ppermute | solution.py:342
  30.3 2.6 %collective-permute-start.5 = (bf16[64,1024]{1,0:T(8,128)(2,1)S(1)}, bf16[64,1024]{1,0:T(8,128)(2,1)S(1)}, u32[]{:S(2)}, u32[]{:S(2)}) collective-permute-start(bf16[64,1024]{1,0:T(8,128)(2,1)S(1)} %copy-done), channel_id=1, source_target_pairs={{0,8},{1,9},{2,10},{3,11},{4,12},{5,13},{6,14},{7,15},{8,0},{9,1},... | collective-permute-start | bytes 393224 | tf_op jit(solution)/shard_map/ppermute | solution.py:339
  32.9 1.6 %collective-permute-start.6 = (bf16[64,1024]{1,0:T(8,128)(2,1)S(1)}, bf16[64,1024]{1,0:T(8,128)(2,1)S(1)}, u32[]{:S(2)}, u32[]{:S(2)}) collective-permute-start(bf16[64,1024]{1,0:T(8,128)(2,1)S(1)} %copy-done), channel_id=1, source_target_pairs={{0,4},{1,5},{2,6},{3,7},{4,0},{5,1},{6,2},{7,3},{8,12},{9,13},{10,... | collective-permute-start | bytes 393224 | tf_op jit(solution)/shard_map/ppermute | solution.py:339
  34.5 1.5 %collective-permute-start.8 = (bf16[64,1024]{1,0:T(8,128)(2,1)S(1)}, bf16[64,1024]{1,0:T(8,128)(2,1)S(1)}, u32[]{:S(2)}, u32[]{:S(2)}) collective-permute-start(bf16[64,1024]{1,0:T(8,128)(2,1)S(1)} %copy-done), channel_id=1, source_target_pairs={{0,2},{1,3},{2,0},{3,1},{4,6},{5,7},{6,4},{7,5},{8,10},{9,11},{10,... | collective-permute-start | bytes 393224 | tf_op jit(solution)/shard_map/ppermute | solution.py:339
  36.0 0.0 collective-permute-start.12
  36.0 3.7 %collective-permute-done.5.rest_3_ = bf16[64,1024]{1,0:T(8,128)(2,1)S(1)} collective-permute-done((bf16[64,1024]{1,0:T(8,128)(2,1)S(1)}, bf16[64,1024]{1,0:T(8,128)(2,1)S(1)}, u32[]{:S(2)}, u32[]{:S(2)}) %collective-permute-start.5) | collective-permute-done | bytes 131104 | tf_op jit(solution)/shard_map/ppermute | solution.py:339
  39.7 0.6 collective-permute-start.7
  40.3 1.5 %collective-permute-start.9 = (bf16[64,1024]{1,0:T(8,128)(2,1)S(1)}, bf16[64,1024]{1,0:T(8,128)(2,1)S(1)}, u32[]{:S(2)}, u32[]{:S(2)}) collective-permute-start(bf16[64,1024]{1,0:T(8,128)(2,1)S(1)} %collective-permute-done.5.rest_3_), channel_id=1, source_target_pairs={{0,2},{1,3},{2,0},{3,1},{4,6},{5,7},{6,4},{7,5},{8,10},{9,11},{10,... | collective-permute-start | bytes 393224 | tf_op jit(solution)/shard_map/ppermute | solution.py:339
  41.8 0.5 collective-permute-start.10
  42.4 0.1 collective-permute-start.20
  42.5 0.0 collective-permute-done.12.rest_10_
  42.5 1.6 %collective-permute-start.22 = (bf16[256,512]{1,0:T(8,128)(2,1)S(1)}, bf16[256,512]{1,0:T(8,128)(2,1)S(1)}, u32[]{:S(2)}, u32[]{:S(2)}) collective-permute-start(bf16[256,512]{1,0:T(8,128)(2,1)S(1)} %shard_map.133), channel_id=1, source_target_pairs={{0,2},{1,3},{2,0},{3,1},{4,6},{5,7},{6,4},{7,5},{8,10},{9,11},{10,... | collective-permute-start | bytes 786440 | tf_op jit(solution)/shard_map/ppermute | solution.py:339
  44.0 0.6 collective-permute-done.7.rest_5_
  44.7 2.0 %collective-permute-done.9.rest_7_ = bf16[64,1024]{1,0:T(8,128)(2,1)S(1)} collective-permute-done((bf16[64,1024]{1,0:T(8,128)(2,1)S(1)}, bf16[64,1024]{1,0:T(8,128)(2,1)S(1)}, u32[]{:S(2)}, u32[]{:S(2)}) %collective-permute-start.9) | collective-permute-done | bytes 131104 | tf_op jit(solution)/shard_map/ppermute | solution.py:339
  46.7 0.0 collective-permute-start.14
  46.7 2.8 %collective-permute-done.10.rest_8_ = bf16[64,1024]{1,0:T(8,128)(2,1)S(1)} collective-permute-done((bf16[64,1024]{1,0:T(8,128)(2,1)S(1)}, bf16[64,1024]{1,0:T(8,128)(2,1)S(1)}, u32[]{:S(2)}, u32[]{:S(2)}) %collective-permute-start.10) | collective-permute-done | bytes 131104 | tf_op jit(solution)/shard_map/ppermute | solution.py:339
  49.5 1.5 %collective-permute-start.11 = (bf16[64,1024]{1,0:T(8,128)(2,1)S(1)}, bf16[64,1024]{1,0:T(8,128)(2,1)S(1)}, u32[]{:S(2)}, u32[]{:S(2)}) collective-permute-start(bf16[64,1024]{1,0:T(8,128)(2,1)S(1)} %collective-permute-done.7.rest_5_), channel_id=1, source_target_pairs={{0,2},{1,3},{2,0},{3,1},{4,6},{5,7},{6,4},{7,5},{8,10},{9,11},{10,... | collective-permute-start | bytes 393224 | tf_op jit(solution)/shard_map/ppermute | solution.py:339
  51.0 0.5 collective-permute-start.15
  51.5 5.2 %collective-permute-done.11.rest_9_ = bf16[64,1024]{1,0:T(8,128)(2,1)S(1)} collective-permute-done((bf16[64,1024]{1,0:T(8,128)(2,1)S(1)}, bf16[64,1024]{1,0:T(8,128)(2,1)S(1)}, u32[]{:S(2)}, u32[]{:S(2)}) %collective-permute-start.11) | collective-permute-done | bytes 131104 | tf_op jit(solution)/shard_map/ppermute | solution.py:339
  56.7 0.5 collective-permute-start.18
  57.2 0.1 collective-permute-start.19
  57.3 0.1 shard_map.134
  57.4 3.4 %collective-permute-start.23 = (bf16[128,512]{1,0:T(8,128)(2,1)S(1)}, bf16[128,512]{1,0:T(8,128)(2,1)S(1)}, u32[]{:S(2)}, u32[]{:S(2)}) collective-permute-start(bf16[128,512]{1,0:T(8,128)(2,1)S(1)} %get-tuple-element.62), channel_id=1, source_target_pairs={{0,8},{1,9},{2,10},{3,11},{4,12},{5,13},{6,14},{7,15},{8,0},{9,1},... | collective-permute-start | bytes 393224 | tf_op jit(solution)/shard_map/ppermute | solution.py:339
  60.9 2.0 %shard_map.129 = (bf16[8,2,64,1024]{3,2,1,0:T(8,128)(2,1)S(1)}, bf16[256,1024]{1,0:T(8,128)(2,1)S(1)}, bf16[16,128,256]{2,1,0:T(8,128)(2,1)S(1)}, bf16[16,128,128]{2,1,0:T(8,128)(2,1)S(1)}, f32[1,128]{1,0:T(1,128)S(1)}) custom-call(s32[1,128]{1,0:T(1,128)S(1)} %get-tuple-element.41.ido_ref, s32[1,128]{1,0:T(1,128)S(1)} %collective-permute-done.2.idx_ref, ...), custom_call_target="tpu_custom_call" | custom-call | flops 1073741824 | bytes 4194304 | tf_op jit(solution)/shard_map/pallas_call | solution.py:323
  62.8 0.2 collective-permute-start.24
  63.0 1.0 %collective-permute-done.24.b_ref = f32[1,128]{1,0:T(1,128)S(1)} collective-permute-done((f32[1,128]{1,0:T(1,128)S(1)}, f32[1,128]{1,0:T(1,128)S(1)}, u32[]{:S(2)}, u32[]{:S(2)}) %collective-permute-start.24) | collective-permute-done | bytes 544 | tf_op jit(solution)/shard_map/ppermute | solution.py:339
  64.0 1.5 %collective-permute-start.25 = (f32[1,128]{1,0:T(1,128)S(1)}, f32[1,128]{1,0:T(1,128)S(1)}, u32[]{:S(2)}, u32[]{:S(2)}) collective-permute-start(f32[1,128]{1,0:T(1,128)S(1)} %shard_map.135.a_ref), channel_id=1, source_target_pairs={{0,2},{1,3},{2,0},{3,1},{4,6},{5,7},{6,4},{7,5},{8,10},{9,11},{10,... | collective-permute-start | bytes 1544 | tf_op jit(solution)/shard_map/ppermute | solution.py:339
  65.5 2.1 %collective-permute-done.25.b_ref = f32[1,128]{1,0:T(1,128)S(1)} collective-permute-done((f32[1,128]{1,0:T(1,128)S(1)}, f32[1,128]{1,0:T(1,128)S(1)}, u32[]{:S(2)}, u32[]{:S(2)}) %collective-permute-start.25) | collective-permute-done | bytes 544 | tf_op jit(solution)/shard_map/ppermute | solution.py:339
  67.6 1.0 %collective-permute-start.26 = (f32[1,128]{1,0:T(1,128)S(1)}, f32[1,128]{1,0:T(1,128)S(1)}, u32[]{:S(2)}, u32[]{:S(2)}) collective-permute-start(f32[1,128]{1,0:T(1,128)S(1)} %shard_map.136.refs_0_), channel_id=1, source_target_pairs={{0,8},{1,9},{2,10},{3,11},{4,12},{5,13},{6,14},{7,15},{8,0},{9,1},... | collective-permute-start | bytes 1544 | tf_op jit(solution)/shard_map/ppermute | solution.py:339
  68.6 3.4 %collective-permute-done.26.refs_1_ = f32[1,128]{1,0:T(1,128)S(1)} collective-permute-done((f32[1,128]{1,0:T(1,128)S(1)}, f32[1,128]{1,0:T(1,128)S(1)}, u32[]{:S(2)}, u32[]{:S(2)}) %collective-permute-start.26) | collective-permute-done | bytes 544 | tf_op jit(solution)/shard_map/ppermute | solution.py:339
  72.1 0.1 shard_map.137
  72.1 0.3 collective-permute-start.27
  72.5 1.7 %collective-permute-start.29 = (bf16[272,128]{1,0:T(8,128)(2,1)S(1)}, bf16[272,128]{1,0:T(8,128)(2,1)S(1)}, u32[]{:S(2)}, u32[]{:S(2)}) collective-permute-start(bf16[272,128]{1,0:T(8,128)(2,1)S(1)} %get-tuple-element.66), channel_id=1, source_target_pairs={{0,20},{1,21},{2,22},{3,23},{4,16},{5,17},{6,18},{7,19},{8,28},{9,... | collective-permute-start | bytes 208904 | tf_op jit(solution)/shard_map/ppermute | solution.py:411
  74.2 1.5 %collective-permute-start.28 = (bf16[272,128]{1,0:T(8,128)(2,1)S(1)}, bf16[272,128]{1,0:T(8,128)(2,1)S(1)}, u32[]{:S(2)}, u32[]{:S(2)}) collective-permute-start(bf16[272,128]{1,0:T(8,128)(2,1)S(1)} %get-tuple-element.67), channel_id=1, source_target_pairs={{0,16},{16,0},{1,17},{17,1},{2,18},{18,2},{3,19},{19,3},{4,20},{20... | collective-permute-start | bytes 208904 | tf_op jit(solution)/shard_map/ppermute | solution.py:342
  75.7 2.3 %shard_map.130 = (bf16[128,1024]{1,0:T(8,128)(2,1)}, bf16[128,1024]{1,0:T(8,128)(2,1)}, bf16[128,1024]{1,0:T(8,128)(2,1)}, bf16[128,1024]{1,0:T(8,128)(2,1)}) custom-call(bf16[256,1024]{1,0:T(8,128)(2,1)S(1)} %get-tuple-element.38.qvo_ref, bf16[256,1024]{1,0:T(8,128)(2,1)S(1)} %collective-permute-done.qvx_ref, ...), custom_call_target="tpu_custom_call" | custom-call | flops 1073741824 | bytes 4194304 | tf_op jit(solution)/shard_map/pallas_call | solution.py:323
  78.0 0.5 collective-permute-done.28.refs_0_
  78.5 0.8 shard_map.138
  (26 shorter events, 0.2 us)
Async XLA Ops:
  2.0 23.5 %collective-permute-start = (bf16[256,1024]{1,0:T(8,128)(2,1)S(1)}, bf16[256,1024]{1,0:T(8,128)(2,1)S(1)}, u32[]{:S(2)}, u32[]{:S(2)}) collective-permute-start(bf16[256,1024]{1,0:T(8,128)(2,1)S(1)} %get-tuple-element.38.qvo_ref), channel_id=1, source_target_pairs={{0,16},{16,0},{1,17},{17,1},{2,18},{18,2},{3,19},{19,3},{4,20},{20... | collective-permute-start | bytes 1572872 | tf_op jit(solution)/shard_map/ppermute | solution.py:342
  5.1 20.4 %collective-permute-start.1 = (bf16[128,1024]{1,0:T(8,128)(2,1)}, bf16[128,1024]{1,0:T(8,128)(2,1)S(1)}, u32[]{:S(2)}, u32[]{:S(2)}) collective-permute-start(bf16[128,1024]{1,0:T(8,128)(2,1)} %bitcast.12), channel_id=1, source_target_pairs={{0,16},{16,0},{1,17},{17,1},{2,18},{18,2},{3,19},{19,3},{4,20},{20... | collective-permute-start | bytes 786440 | tf_op jit(solution)/shard_map/ppermute | solution.py:342
  5.2 22.8 %collective-permute-start.3 = (bf16[128,512]{1,0:T(8,128)(2,1)S(1)}, bf16[128,512]{1,0:T(8,128)(2,1)S(1)}, u32[]{:S(2)}, u32[]{:S(2)}) collective-permute-start(bf16[128,512]{1,0:T(8,128)(2,1)S(1)} %get-tuple-element.47), channel_id=1, source_target_pairs={{0,16},{16,0},{1,17},{17,1},{2,18},{18,2},{3,19},{19,3},{4,20},{20... | collective-permute-start | bytes 393224 | tf_op jit(solution)/shard_map/ppermute | solution.py:363
  7.1 18.4 %collective-permute-start.2 = (s32[1,128]{1,0:T(1,128)S(1)}, s32[1,128]{1,0:T(1,128)S(1)}, u32[]{:S(2)}, u32[]{:S(2)}) collective-permute-start(s32[1,128]{1,0:T(1,128)S(1)} %get-tuple-element.41.ido_ref), channel_id=1, source_target_pairs={{0,16},{16,0},{1,17},{17,1},{2,18},{18,2},{3,19},{19,3},{4,20},{20... | collective-permute-start | bytes 1544 | tf_op jit(solution)/shard_map/ppermute | solution.py:342
  25.5 4.8 %copy-start = (bf16[64,1024]{1,0:T(8,128)(2,1)S(1)}, bf16[64,1024]{1,0:T(8,128)(2,1)}, u32[]{:S(2)}) copy-start(bf16[64,1024]{1,0:T(8,128)(2,1)} %rest_2_.1) | copy-start | bytes 393220
  28.5 13.3 %collective-permute-start.21 = (bf16[256,512]{1,0:T(8,128)(2,1)S(1)}, bf16[256,512]{1,0:T(8,128)(2,1)S(1)}, u32[]{:S(2)}, u32[]{:S(2)}) collective-permute-start(bf16[256,512]{1,0:T(8,128)(2,1)S(1)} %get-tuple-element.60), channel_id=1, source_target_pairs={{0,1},{1,0},{2,3},{3,2},{4,5},{5,4},{6,7},{7,6},{8,9},{9,8},{10,11... | collective-permute-start | bytes 786440 | tf_op jit(solution)/shard_map/ppermute | solution.py:339
  28.5 7.5 %collective-permute-start.4 = (bf16[128,512]{1,0:T(8,128)(2,1)S(1)}, bf16[128,512]{1,0:T(8,128)(2,1)S(1)}, u32[]{:S(2)}, u32[]{:S(2)}) collective-permute-start(bf16[128,512]{1,0:T(8,128)(2,1)S(1)} %get-tuple-element.48), channel_id=1, source_target_pairs={{0,16},{16,0},{1,17},{17,1},{2,18},{18,2},{3,19},{19,3},{4,20},{20... | collective-permute-start | bytes 393224 | tf_op jit(solution)/shard_map/ppermute | solution.py:342
  30.3 9.4 %collective-permute-start.5 = (bf16[64,1024]{1,0:T(8,128)(2,1)S(1)}, bf16[64,1024]{1,0:T(8,128)(2,1)S(1)}, u32[]{:S(2)}, u32[]{:S(2)}) collective-permute-start(bf16[64,1024]{1,0:T(8,128)(2,1)S(1)} %copy-done), channel_id=1, source_target_pairs={{0,8},{1,9},{2,10},{3,11},{4,12},{5,13},{6,14},{7,15},{8,0},{9,1},... | collective-permute-start | bytes 393224 | tf_op jit(solution)/shard_map/ppermute | solution.py:339
  32.9 7.4 %collective-permute-start.6 = (bf16[64,1024]{1,0:T(8,128)(2,1)S(1)}, bf16[64,1024]{1,0:T(8,128)(2,1)S(1)}, u32[]{:S(2)}, u32[]{:S(2)}) collective-permute-start(bf16[64,1024]{1,0:T(8,128)(2,1)S(1)} %copy-done), channel_id=1, source_target_pairs={{0,4},{1,5},{2,6},{3,7},{4,0},{5,1},{6,2},{7,3},{8,12},{9,13},{10,... | collective-permute-start | bytes 393224 | tf_op jit(solution)/shard_map/ppermute | solution.py:339
  34.5 7.9 %collective-permute-start.8 = (bf16[64,1024]{1,0:T(8,128)(2,1)S(1)}, bf16[64,1024]{1,0:T(8,128)(2,1)S(1)}, u32[]{:S(2)}, u32[]{:S(2)}) collective-permute-start(bf16[64,1024]{1,0:T(8,128)(2,1)S(1)} %copy-done), channel_id=1, source_target_pairs={{0,2},{1,3},{2,0},{3,1},{4,6},{5,7},{6,4},{7,5},{8,10},{9,11},{10,... | collective-permute-start | bytes 393224 | tf_op jit(solution)/shard_map/ppermute | solution.py:339
  36.0 6.5 %collective-permute-start.12 = (bf16[64,1024]{1,0:T(8,128)(2,1)S(1)}, bf16[64,1024]{1,0:T(8,128)(2,1)S(1)}, u32[]{:S(2)}, u32[]{:S(2)}) collective-permute-start(bf16[64,1024]{1,0:T(8,128)(2,1)S(1)} %copy-done), channel_id=1, source_target_pairs={{0,1},{1,0},{2,3},{3,2},{4,5},{5,4},{6,7},{7,6},{8,9},{9,8},{10,11... | collective-permute-start | bytes 393224 | tf_op jit(solution)/shard_map/ppermute | solution.py:339
  39.7 5.0 %collective-permute-start.7 = (bf16[64,1024]{1,0:T(8,128)(2,1)S(1)}, bf16[64,1024]{1,0:T(8,128)(2,1)S(1)}, u32[]{:S(2)}, u32[]{:S(2)}) collective-permute-start(bf16[64,1024]{1,0:T(8,128)(2,1)S(1)} %collective-permute-done.5.rest_3_), channel_id=1, source_target_pairs={{0,4},{1,5},{2,6},{3,7},{4,0},{5,1},{6,2},{7,3},{8,12},{9,13},{10,... | collective-permute-start | bytes 393224 | tf_op jit(solution)/shard_map/ppermute | solution.py:339
  40.3 6.4 %collective-permute-start.9 = (bf16[64,1024]{1,0:T(8,128)(2,1)S(1)}, bf16[64,1024]{1,0:T(8,128)(2,1)S(1)}, u32[]{:S(2)}, u32[]{:S(2)}) collective-permute-start(bf16[64,1024]{1,0:T(8,128)(2,1)S(1)} %collective-permute-done.5.rest_3_), channel_id=1, source_target_pairs={{0,2},{1,3},{2,0},{3,1},{4,6},{5,7},{6,4},{7,5},{8,10},{9,11},{10,... | collective-permute-start | bytes 393224 | tf_op jit(solution)/shard_map/ppermute | solution.py:339
  41.8 7.7 %collective-permute-start.10 = (bf16[64,1024]{1,0:T(8,128)(2,1)S(1)}, bf16[64,1024]{1,0:T(8,128)(2,1)S(1)}, u32[]{:S(2)}, u32[]{:S(2)}) collective-permute-start(bf16[64,1024]{1,0:T(8,128)(2,1)S(1)} %collective-permute-done.6.rest_4_), channel_id=1, source_target_pairs={{0,2},{1,3},{2,0},{3,1},{4,6},{5,7},{6,4},{7,5},{8,10},{9,11},{10,... | collective-permute-start | bytes 393224 | tf_op jit(solution)/shard_map/ppermute | solution.py:339
  42.4 14.3 %collective-permute-start.20 = (bf16[256,512]{1,0:T(8,128)(2,1)S(1)}, bf16[256,512]{1,0:T(8,128)(2,1)S(1)}, u32[]{:S(2)}, u32[]{:S(2)}) collective-permute-start(bf16[256,512]{1,0:T(8,128)(2,1)S(1)} %get-tuple-element.58), channel_id=1, source_target_pairs={{0,1},{1,0},{2,3},{3,2},{4,5},{5,4},{6,7},{7,6},{8,9},{9,8},{10,11... | collective-permute-start | bytes 786440 | tf_op jit(solution)/shard_map/ppermute | solution.py:339
  42.5 14.7 %collective-permute-start.22 = (bf16[256,512]{1,0:T(8,128)(2,1)S(1)}, bf16[256,512]{1,0:T(8,128)(2,1)S(1)}, u32[]{:S(2)}, u32[]{:S(2)}) collective-permute-start(bf16[256,512]{1,0:T(8,128)(2,1)S(1)} %shard_map.133), channel_id=1, source_target_pairs={{0,2},{1,3},{2,0},{3,1},{4,6},{5,7},{6,4},{7,5},{8,10},{9,11},{10,... | collective-permute-start | bytes 786440 | tf_op jit(solution)/shard_map/ppermute | solution.py:339
  44.7 6.3 %collective-permute-start.13 = (bf16[64,1024]{1,0:T(8,128)(2,1)S(1)}, bf16[64,1024]{1,0:T(8,128)(2,1)S(1)}, u32[]{:S(2)}, u32[]{:S(2)}) collective-permute-start(bf16[64,1024]{1,0:T(8,128)(2,1)S(1)} %collective-permute-done.5.rest_3_), channel_id=1, source_target_pairs={{0,1},{1,0},{2,3},{3,2},{4,5},{5,4},{6,7},{7,6},{8,9},{9,8},{10,11... | collective-permute-start | bytes 393224 | tf_op jit(solution)/shard_map/ppermute | solution.py:339
  46.7 4.3 %collective-permute-start.14 = (bf16[64,1024]{1,0:T(8,128)(2,1)S(1)}, bf16[64,1024]{1,0:T(8,128)(2,1)S(1)}, u32[]{:S(2)}, u32[]{:S(2)}) collective-permute-start(bf16[64,1024]{1,0:T(8,128)(2,1)S(1)} %collective-permute-done.6.rest_4_), channel_id=1, source_target_pairs={{0,1},{1,0},{2,3},{3,2},{4,5},{5,4},{6,7},{7,6},{8,9},{9,8},{10,11... | collective-permute-start | bytes 393224 | tf_op jit(solution)/shard_map/ppermute | solution.py:339
  49.5 7.2 %collective-permute-start.11 = (bf16[64,1024]{1,0:T(8,128)(2,1)S(1)}, bf16[64,1024]{1,0:T(8,128)(2,1)S(1)}, u32[]{:S(2)}, u32[]{:S(2)}) collective-permute-start(bf16[64,1024]{1,0:T(8,128)(2,1)S(1)} %collective-permute-done.7.rest_5_), channel_id=1, source_target_pairs={{0,2},{1,3},{2,0},{3,1},{4,6},{5,7},{6,4},{7,5},{8,10},{9,11},{10,... | collective-permute-start | bytes 393224 | tf_op jit(solution)/shard_map/ppermute | solution.py:339
  51.0 6.4 %collective-permute-start.16 = (bf16[64,1024]{1,0:T(8,128)(2,1)S(1)}, bf16[64,1024]{1,0:T(8,128)(2,1)S(1)}, u32[]{:S(2)}, u32[]{:S(2)}) collective-permute-start(bf16[64,1024]{1,0:T(8,128)(2,1)S(1)} %collective-permute-done.8.rest_6_), channel_id=1, source_target_pairs={{0,1},{1,0},{2,3},{3,2},{4,5},{5,4},{6,7},{7,6},{8,9},{9,8},{10,11... | collective-permute-start | bytes 393224 | tf_op jit(solution)/shard_map/ppermute | solution.py:339
  51.0 9.9 %collective-permute-start.15 = (bf16[64,1024]{1,0:T(8,128)(2,1)S(1)}, bf16[64,1024]{1,0:T(8,128)(2,1)S(1)}, u32[]{:S(2)}, u32[]{:S(2)}) collective-permute-start(bf16[64,1024]{1,0:T(8,128)(2,1)S(1)} %collective-permute-done.7.rest_5_), channel_id=1, source_target_pairs={{0,1},{1,0},{2,3},{3,2},{4,5},{5,4},{6,7},{7,6},{8,9},{9,8},{10,11... | collective-permute-start | bytes 393224 | tf_op jit(solution)/shard_map/ppermute | solution.py:339
  56.7 4.2 %collective-permute-start.17 = (bf16[64,1024]{1,0:T(8,128)(2,1)S(1)}, bf16[64,1024]{1,0:T(8,128)(2,1)S(1)}, u32[]{:S(2)}, u32[]{:S(2)}) collective-permute-start(bf16[64,1024]{1,0:T(8,128)(2,1)S(1)} %collective-permute-done.9.rest_7_), channel_id=1, source_target_pairs={{0,1},{1,0},{2,3},{3,2},{4,5},{5,4},{6,7},{7,6},{8,9},{9,8},{10,11... | collective-permute-start | bytes 393224 | tf_op jit(solution)/shard_map/ppermute | solution.py:339
  56.7 4.2 %collective-permute-start.18 = (bf16[64,1024]{1,0:T(8,128)(2,1)S(1)}, bf16[64,1024]{1,0:T(8,128)(2,1)S(1)}, u32[]{:S(2)}, u32[]{:S(2)}) collective-permute-start(bf16[64,1024]{1,0:T(8,128)(2,1)S(1)} %collective-permute-done.10.rest_8_), channel_id=1, source_target_pairs={{0,1},{1,0},{2,3},{3,2},{4,5},{5,4},{6,7},{7,6},{8,9},{9,8},{10,11... | collective-permute-start | bytes 393224 | tf_op jit(solution)/shard_map/ppermute | solution.py:339
  57.2 3.7 %collective-permute-start.19 = (bf16[64,1024]{1,0:T(8,128)(2,1)S(1)}, bf16[64,1024]{1,0:T(8,128)(2,1)S(1)}, u32[]{:S(2)}, u32[]{:S(2)}) collective-permute-start(bf16[64,1024]{1,0:T(8,128)(2,1)S(1)} %collective-permute-done.11.rest_9_), channel_id=1, source_target_pairs={{0,1},{1,0},{2,3},{3,2},{4,5},{5,4},{6,7},{7,6},{8,9},{9,8},{10,11... | collective-permute-start | bytes 393224 | tf_op jit(solution)/shard_map/ppermute | solution.py:339
  57.4 14.7 %collective-permute-start.23 = (bf16[128,512]{1,0:T(8,128)(2,1)S(1)}, bf16[128,512]{1,0:T(8,128)(2,1)S(1)}, u32[]{:S(2)}, u32[]{:S(2)}) collective-permute-start(bf16[128,512]{1,0:T(8,128)(2,1)S(1)} %get-tuple-element.62), channel_id=1, source_target_pairs={{0,8},{1,9},{2,10},{3,11},{4,12},{5,13},{6,14},{7,15},{8,0},{9,1},... | collective-permute-start | bytes 393224 | tf_op jit(solution)/shard_map/ppermute | solution.py:339
  62.8 1.2 %collective-permute-start.24 = (f32[1,128]{1,0:T(1,128)S(1)}, f32[1,128]{1,0:T(1,128)S(1)}, u32[]{:S(2)}, u32[]{:S(2)}) collective-permute-start(f32[1,128]{1,0:T(1,128)S(1)} %get-tuple-element.63.a_ref), channel_id=1, source_target_pairs={{0,1},{1,0},{2,3},{3,2},{4,5},{5,4},{6,7},{7,6},{8,9},{9,8},{10,11... | collective-permute-start | bytes 1544 | tf_op jit(solution)/shard_map/ppermute | solution.py:339
  64.0 3.6 %collective-permute-start.25 = (f32[1,128]{1,0:T(1,128)S(1)}, f32[1,128]{1,0:T(1,128)S(1)}, u32[]{:S(2)}, u32[]{:S(2)}) collective-permute-start(f32[1,128]{1,0:T(1,128)S(1)} %shard_map.135.a_ref), channel_id=1, source_target_pairs={{0,2},{1,3},{2,0},{3,1},{4,6},{5,7},{6,4},{7,5},{8,10},{9,11},{10,... | collective-permute-start | bytes 1544 | tf_op jit(solution)/shard_map/ppermute | solution.py:339
  67.6 4.5 %collective-permute-start.26 = (f32[1,128]{1,0:T(1,128)S(1)}, f32[1,128]{1,0:T(1,128)S(1)}, u32[]{:S(2)}, u32[]{:S(2)}) collective-permute-start(f32[1,128]{1,0:T(1,128)S(1)} %shard_map.136.refs_0_), channel_id=1, source_target_pairs={{0,8},{1,9},{2,10},{3,11},{4,12},{5,13},{6,14},{7,15},{8,0},{9,1},... | collective-permute-start | bytes 1544 | tf_op jit(solution)/shard_map/ppermute | solution.py:339
  72.1 5.8 %collective-permute-start.27 = (bf16[272,128]{1,0:T(8,128)(2,1)S(1)}, bf16[272,128]{1,0:T(8,128)(2,1)S(1)}, u32[]{:S(2)}, u32[]{:S(2)}) collective-permute-start(bf16[272,128]{1,0:T(8,128)(2,1)S(1)} %get-tuple-element.66), channel_id=1, source_target_pairs={{0,4},{1,5},{2,6},{3,7},{4,0},{5,1},{6,2},{7,3},{8,12},{9,13},{10,... | collective-permute-start | bytes 208904 | tf_op jit(solution)/shard_map/ppermute | solution.py:339
  72.5 6.0 %collective-permute-start.29 = (bf16[272,128]{1,0:T(8,128)(2,1)S(1)}, bf16[272,128]{1,0:T(8,128)(2,1)S(1)}, u32[]{:S(2)}, u32[]{:S(2)}) collective-permute-start(bf16[272,128]{1,0:T(8,128)(2,1)S(1)} %get-tuple-element.66), channel_id=1, source_target_pairs={{0,20},{1,21},{2,22},{3,23},{4,16},{5,17},{6,18},{7,19},{8,28},{9,... | collective-permute-start | bytes 208904 | tf_op jit(solution)/shard_map/ppermute | solution.py:411
  74.2 4.3 %collective-permute-start.28 = (bf16[272,128]{1,0:T(8,128)(2,1)S(1)}, bf16[272,128]{1,0:T(8,128)(2,1)S(1)}, u32[]{:S(2)}, u32[]{:S(2)}) collective-permute-start(bf16[272,128]{1,0:T(8,128)(2,1)S(1)} %get-tuple-element.67), channel_id=1, source_target_pairs={{0,16},{16,0},{1,17},{17,1},{2,18},{18,2},{3,19},{19,3},{4,20},{20... | collective-permute-start | bytes 208904 | tf_op jit(solution)/shard_map/ppermute | solution.py:342
